TPU v7x, 256 devices: a whole 4x4x8 slice. The times are simulated.
256 devices in a mesh: span: 64 (over y, x, z_lo, core), head: 4 (over z_hi).
Axes of the slice: x: 4, y: 4, z: 8 (z_hi: 4, z_lo: 2; z = z_hi * 2 + z_lo), core: 2. Of those that a mesh axis runs over, the one named last changes fastest.
Arguments:
- decoder_states: bfloat16 [131072, 1024], P('span'), may hold values from -21 to 21
- encodings: bfloat16 [4096, 128, 1024], P('span', 'head'), may hold values from -21 to 21
- neighbor_table: int32 [2048, 2, 2], P('span'), may hold values from 0 to 63, as said below
- query_weight: bfloat16 [1024, 1024], P(None, 'head'), may hold values from -0.1875 to 0.1875
- key_weight: bfloat16 [1024, 1024], P(None, 'head'), may hold values from -0.1875 to 0.1875
- value_weight: bfloat16 [1024, 1024], P(None, 'head'), may hold values from -0.1875 to 0.1875
- out_weight: bfloat16 [1024, 1024], P('head'), may hold values from -0.1875 to 0.1875
Outputs:
- attended: bfloat16 [131072, 1024], P('span', 'head')
Inputs may be any that keep to these rules, and one draw needn't show every extreme that they name: neighbor_table[c, k, 0] is the database shard and neighbor_table[c, k, 1] the slot in that shard of neighbor k of span c; in each aligned block of 32 spans (the spans of one device along `span`) every shard is named by exactly one neighbor, and every slot of every shard is named exactly once in the whole table.
All inputs are finite; a program needn't handle non-finite values.
Results may differ from a plain program's by a relative error of at most 0.012.
The roundings to bfloat16 on the way count: a program that leaves them out, or rounds other values in their place, can miss the bound.
Values may be sent and summed in bfloat16 or wider, within the bound.
No kernel may reach another device: no remote copies, remote signals or barrier semaphores. Data moves between devices by JAX's collectives and lax.ppermute only.
A program may use at most 128 MiB of HBM per device.

v0:
```python
import jax
import jax.numpy as jnp
from jax import lax
from jax.sharding import PartitionSpec as P

HEAD_DIM = 64
SPAN_LEN = 64
SEQ_LEN = 2048


def body(
    decoder_states, encodings, neighbor_table, query_weight, key_weight, value_weight, out_weight
):
    peer_count = lax.axis_size("span")
    column_rows = lax.all_to_all(out_weight, "head", split_axis=1, concat_axis=0, tiled=True)
    shard_ids = neighbor_table[:, :, 0].reshape(-1)
    slot_ids = neighbor_table[:, :, 1].reshape(-1)
    entries = shard_ids.shape[0]
    per_peer = entries // peer_count
    numbering = jnp.arange(entries, dtype=jnp.int32)
    same_before = (shard_ids[:, None] == shard_ids[None, :]) & (
        numbering[None, :] < numbering[:, None]
    )
    ranking = jnp.sum(same_before.astype(jnp.int32), axis=1)
    position = shard_ids * per_peer + ranking
    placed = position[None, :] == numbering[:, None]
    request = jnp.sum(jnp.where(placed, slot_ids[None, :], 0), axis=1)
    wanted = lax.all_to_all(request, "span", split_axis=0, concat_axis=0, tiled=True)
    selected = encodings[wanted]
    model_width = decoder_states.shape[1]
    group_cols = query_weight.shape[1]
    both_weights = jnp.concatenate([key_weight, value_weight], axis=1)
    arrived = lax.all_to_all(selected, "span", split_axis=0, concat_axis=0, tiled=True)
    block_in = lax.all_gather(arrived, "head", axis=1, tiled=True)
    flattened = block_in.reshape(-1, model_width)
    result = jnp.dot(flattened, both_weights, preferred_element_type=jnp.float32).astype(
        jnp.bfloat16
    )
    projected = result.reshape(block_in.shape[0], block_in.shape[1], 2 * group_cols)
    ordered = projected[position]
    span_count = neighbor_table.shape[0]
    neighbors = neighbor_table.shape[1]
    heads_here = group_cols // HEAD_DIM
    ordered = ordered.reshape(span_count, neighbors * projected.shape[1], 2 * group_cols)
    key_rows = ordered[:, :, :group_cols].reshape(span_count, -1, heads_here, HEAD_DIM)
    value_rows = ordered[:, :, group_cols:].reshape(span_count, -1, heads_here, HEAD_DIM)
    queries = jnp.dot(decoder_states, query_weight, preferred_element_type=jnp.float32).astype(
        jnp.bfloat16
    )
    sequences = decoder_states.shape[0] // SEQ_LEN
    offset = SPAN_LEN - 1
    queries = queries.reshape(sequences, SEQ_LEN, group_cols)
    shifted = jnp.concatenate(
        [queries[:, offset:], jnp.zeros((sequences, offset, group_cols), jnp.bfloat16)], axis=1
    )
    shifted = shifted.reshape(span_count, SPAN_LEN, heads_here, HEAD_DIM)
    inv_root = HEAD_DIM ** (-0.5)
    scores = (
        jnp.einsum("cqhd,ckhd->chqk", shifted, key_rows, preferred_element_type=jnp.float32)
        * inv_root
    )
    weights = jax.nn.softmax(scores, axis=-1).astype(jnp.bfloat16)
    context = jnp.einsum(
        "chqk,ckhd->cqhd", weights, value_rows, preferred_element_type=jnp.float32
    ).astype(jnp.bfloat16)
    context = context.reshape(sequences, SEQ_LEN, group_cols)
    context = jnp.concatenate(
        [jnp.zeros((sequences, offset, group_cols), jnp.bfloat16), context[:, : SEQ_LEN - offset]],
        axis=1,
    )
    context = context.reshape(-1, group_cols)
    summed = jnp.dot(
        lax.all_gather(context, "head", axis=1, tiled=True),
        column_rows,
        preferred_element_type=jnp.float32,
    )
    return summed.astype(jnp.bfloat16)


def solution(mesh):
    return jax.shard_map(
        body,
        mesh=mesh,
        in_specs=(
            P("span", None),
            P("span", "head", None),
            P("span", None, None),
            P(None, "head"),
            P(None, "head"),
            P(None, "head"),
            P("head", None),
        ),
        out_specs=P("span", "head"),
        check_vma=False,
    )
```

profile of v0, /device:TPU:34, one launch (start us, length us, event | category | flops | bytes accessed | tf_op | source)
XLA Modules:
  0.0 559.6 jit_solution(16839109739039627777)
XLA Ops:
  6.5 0.0 copy-start
  6.5 0.0 all-gather.4.cloned.1.call-start
  6.5 0.8 fusion.30
  7.3 0.1 copy.50
  7.4 0.1 reshape_squeeze.5
  7.5 0.2 convert_reduce_fusion
  7.7 0.1 copy.51
  7.8 0.1 broadcast_in_dim.14
  7.9 0.1 select_reduce_fusion
  8.0 0.1 copy.52
  8.1 14.9 %all_to_all.36 = s32[64,1,1]{2,1,0:T(1,128)S(1)} all-to-all(s32[64,1,1]{2,1,0:T(1,128)S(1)} %copy.52), channel_id=1, replica_groups=mesh['span'=64,'head'=4] {'span'}, dimensions={0} | all-to-all | bytes 512 | tf_op jit(solution)/shard_map/all_to_all | solution.py:28
  23.0 1.2 reduce
  24.2 4.9 gather_fusion
  29.2 56.4 %all_to_all.37 = bf16[64,32,1024]{2,1,0:T(8,128)(2,1)} all-to-all(bf16[64,32,1024]{2,1,0:T(8,128)(2,1)} %gather_fusion), channel_id=1, replica_groups=mesh['span'=64,'head'=4] {'span'}, dimensions={0} | all-to-all | bytes 8388608 | tf_op jit(solution)/shard_map/all_to_all | solution.py:33
  85.5 0.0 all-gather.4.cloned.1.call-update
  85.5 0.2 all-gather.6.cloned.1.call-start
  85.8 0.1 reshape_squeeze.6
  85.9 0.0 copy-done
  85.9 3.4 fusion.11
  89.3 0.0 copy-start.4
  89.3 0.2 slice.29
  89.6 1.0 concatenate.10
  90.6 3.3 reshape.100
  94.0 282.5 %all-gather.4.cloned.1.call-done = bf16[64,128,1024]{2,1,0:T(8,128)(2,1)} async-done(((bf16[64,32,1024]{2,1,0:T(8,128)(2,1)}), bf16[64,128,1024]{2,1,0:T(8,128)(2,1)}) %all-gather.4.cloned.1.call-update) | async-done | bytes 16777232 | tf_op jit(solution)/shard_map/all_gather | solution.py:34
  376.5 0.0 copy-done.4
  376.5 14.5 %convolution_convert_fusion = bf16[8192,512]{1,0:T(8,128)(2,1)} fusion(bf16[8192,1024]{1,0:T(8,128)(2,1)} %bitcast.54, bf16[1024,256]{1,0:T(8,128)(2,1)S(1)} %copy-done.4, bf16[1024,256]{1,0:T(8,128)(2,1)} %param.11), kind=kOutput, calls=%fused_computation.3 | convolution fusion | flops 8596226048 | bytes 26214400 | tf_op jit(solution)/shard_map/dot_general | solution.py:36
  391.0 8.9 %gather_fusion.1 = bf16[64,128,512]{2,1,0:T(8,128)(2,1)} fusion(bf16[64,128,512]{2,1,0:T(8,128)(2,1)} %bitcast.47, s32[1024]{0:T(1024)S(1)} %pad_clamp_fusion), kind=kCustom, calls=%fused_computation.1 | custom fusion | bytes 16777472 | tf_op jit(solution)/shard_map/gather | solution.py:40
  399.9 5.9 %fusion.29 = (bf16[32,256,256]{2,1,0:T(8,128)(2,1)}, bf16[32,256,256]{2,1,0:T(8,128)(2,1)}) fusion(bf16[32,256,512]{2,1,0:T(8,128)(2,1)} %bitcast.45), kind=kLoop, calls=%fused_computation.37 | loop fusion | bytes 16777216 | tf_op jit(solution)/shard_map/slice | solution.py:45
  405.8 6.4 %copy.61 = bf16[32,256,256]{1,2,0:T(8,128)(2,1)} copy(bf16[32,256,256]{2,1,0:T(8,128)(2,1)} %get-tuple-element.5) | data formatting | bytes 8388608
  412.2 3.4 fusion.12
  415.6 0.0 copy-start.2
  415.6 3.1 fusion.31
  418.8 0.1 copy-done.2
  418.9 6.4 %copy.60 = bf16[32,256,256]{1,2,0:T(8,128)(2,1)} copy(bf16[32,256,256]{2,1,0:T(8,128)(2,1)} %get-tuple-element.6) | data formatting | bytes 8388608
  425.2 22.4 %convert_bitcast_fusion = bf16[32,64,4,64]{1,3,2,0:T(8,128)(2,1)} fusion(bf16[32,256,4,64]{1,3,2,0:T(8,128)(2,1)} %bitcast.49, f32[32,4,64]{2,1,0:T(4,128)S(1)} %fusion.31, f32[32,4,64,256]{3,2,1,0:T(8,128)} %copy-done.2), kind=kOutput, calls=%fused_computation.17 | convolution fusion | flops 279453952 | bytes 13664256 | tf_op jit(solution)/shard_map/chqk,ckhd->cqhd/dot_general | solution.py:63
  447.6 2.9 copy.57
  450.6 0.0 copy-start.3
  450.6 2.4 reshape.102
  453.0 2.6 concatenate.11
  455.7 0.0 all-gather.6.cloned.1.call-update
  455.7 0.0 copy-done.3
  455.7 0.2 copy.58
  455.9 22.9 %all_to_all.38 = bf16[256,4,256]{0,2,1:T(8,128)(2,1)S(1)} all-to-all(bf16[256,4,256]{0,2,1:T(8,128)(2,1)S(1)} %bitcast.51), channel_id=1, replica_groups=mesh['span'=64,'head'=4] {'head'}, dimensions={1} | all-to-all | bytes 1048576 | tf_op jit(solution)/shard_map/all_to_all | solution.py:15
  478.8 0.2 copy.59
  479.0 69.2 %all-gather.6.cloned.1.call-done = bf16[1,2048,1024]{1,2,0:T(8,128)(2,1)} async-done(((bf16[1,2048,256]{1,2,0:T(8,128)(2,1)}), bf16[1,2048,1024]{1,2,0:T(8,128)(2,1)}) %all-gather.6.cloned.1.call-update) | async-done | bytes 4194320 | tf_op jit(solution)/shard_map/all_gather | solution.py:73
  548.2 0.0 copy-start.1
  548.2 4.6 fusion.8
  552.7 0.0 copy-done.1
  (5 shorter events, 0.0 us)
Async XLA Ops:
  6.5 79.3 %copy-start = (bf16[1024,256]{1,0:T(8,128)(2,1)S(1)}, bf16[1024,256]{1,0:T(8,128)(2,1)}, u32[]{:S(2)}) copy-start(bf16[1024,256]{1,0:T(8,128)(2,1)} %param.10) | copy-start | bytes 1572868
  6.5 369.9 %all-gather.4.cloned.1.call-start = ((), (), s32[]{:S(2)}) async-start(), calls=%async_computation.3 | async-start | bytes 20971520 | tf_op jit(solution)/shard_map/all_gather | solution.py:34
  85.5 462.6 %all-gather.6.cloned.1.call-start = ((), (), s32[]{:S(2)}) async-start(), calls=%async_computation.4 | async-start | bytes 5242880 | tf_op jit(solution)/shard_map/all_gather | solution.py:73
  89.3 287.2 %copy-start.4 = (bf16[1024,256]{1,0:T(8,128)(2,1)S(1)}, bf16[1024,256]{1,0:T(8,128)(2,1)}, u32[]{:S(2)}) copy-start(bf16[1024,256]{1,0:T(8,128)(2,1)} %param.12) | copy-start | bytes 1572868
  415.6 3.2 copy-start.2
  450.6 5.1 copy-start.3
  548.2 4.6 copy-start.1
Sparse Core Ops, SparseCore 0:
  85.7 290.7 all-gather.3
  455.8 92.3 all-gather.5
where the time goes:
time: 561 us; the launch traced here: 560 us
  waiting for transfers between devices  352 us (63%)
  blocking collectives  94.1 us (17%)
  matrix products  48.3 us (9%)
  local copies, waits for them, and re-layouts  47 us (8%)
  between operations  13.5 us (2%)
    all_gather x1, waiting for transfers between devices, body(): block_in = lax.all_gather(arrived, 'head', axis=1, tiled=True)  282 us
    all_gather x1, waiting for transfers between devices, body(): lax.all_gather(context, 'head', axis=1, tiled=True)  69.2 us
    all_to_all x1, blocking collectives, body(): lax.all_to_all(selected, 'span', split_axis=0, concat_axis=0, tiled=True)  56.4 us
    all_to_all x1, blocking collectives, body(): lax.all_to_all(out_weight, 'head', split_axis=1, concat_axis=0, tiled=True)  22.9 us
    dot_general x1, matrix products, body(): jnp.einsum('chqk,ckhd->cqhd', weights, value_rows, preferred_element_type...  22.4 us
    all_to_all x1, blocking collectives, body(): lax.all_to_all(request, 'span', split_axis=0, concat_axis=0, tiled=True)  14.9 us
    dot_general x1, matrix products, body(): jnp.dot(flattened, both_weights, preferred_element_type=jnp.float32)  14.5 us
    unnamed x13, local copies, waits for them, and re-layouts  13.1 us
  transfers between devices with their start and end apart: 2, of which 2 were waited for; matrix products, arithmetic and copies ran while one was open for 2% of the time, Pallas kernels for 0%

commit v1 on v0

v1 whole, which is shorter than its diff:
```python
import functools

import jax
import jax.numpy as jnp
from jax import lax
from jax.experimental import pallas as pl
from jax.experimental.pallas import tpu as pltpu
from jax.sharding import PartitionSpec as P

HEAD_DIM = 64
SPAN_LEN = 64
SPANS_STEP = 2


def attention_kernel(head_ref, x_ref, now_ref, next_ref, w_ref, out_ref, k_ref, v_ref):
    f32, bf16 = jnp.float32, jnp.bfloat16
    parts, entries, piece, width = x_ref.shape
    spans = entries // 2
    keys = 2 * parts * piece
    groups = w_ref.shape[1]
    cols = width // groups
    rows = spans * SPAN_LEN

    x = jnp.concatenate(
        [x_ref[:, 2 * i : 2 * i + 2].reshape(keys, width) for i in range(spans)], axis=0
    )
    both = jnp.concatenate([now_ref[...], next_ref[...]], axis=0)
    row = lax.broadcasted_iota(jnp.int32, (rows, rows + SPAN_LEN), 0)
    col = lax.broadcasted_iota(jnp.int32, (rows, rows + SPAN_LEN), 1)
    shift = jnp.where(col == row + SPAN_LEN - 1, 1.0, 0.0).astype(bf16)
    states = jnp.dot(shift, both, preferred_element_type=f32).astype(bf16)

    def weight(which, g):
        return w_ref[:, g, :, which * cols : (which + 1) * cols].reshape(width, cols)

    total = jnp.zeros((rows, width), f32)
    lane = lax.broadcasted_iota(jnp.int32, (SPAN_LEN, 128), 1)
    low = lane < HEAD_DIM
    for g in range(groups):
        k_ref[...] = jnp.dot(x, weight(0, g), preferred_element_type=f32).astype(bf16)
        v_ref[...] = jnp.dot(x, weight(1, g), preferred_element_type=f32).astype(bf16)
        q = jnp.dot(states, weight(2, g), preferred_element_type=f32).astype(bf16)
        context_rows = []
        for i in range(spans):
            pieces = []
            for pair in range(cols // 128):
                here = slice(pair * 128, pair * 128 + 128)
                qp = q[i * SPAN_LEN : (i + 1) * SPAN_LEN, here]
                zero = jnp.zeros_like(qp)
                two = jnp.concatenate([jnp.where(low, qp, zero), jnp.where(low, zero, qp)], axis=0)
                kp = k_ref[i * keys : (i + 1) * keys, here]
                vp = v_ref[i * keys : (i + 1) * keys, here]
                scores = lax.dot_general(
                    two, kp, (((1,), (1,)), ((), ())), preferred_element_type=f32
                ) * (HEAD_DIM ** -0.5)
                top = jnp.max(scores, axis=1, keepdims=True)
                raised = jnp.exp(scores - top)
                weights = raised * (1.0 / jnp.sum(raised, axis=1, keepdims=True))
                mixed = jnp.dot(weights.astype(bf16), vp, preferred_element_type=f32)
                pieces.append(jnp.where(low, mixed[:SPAN_LEN], mixed[SPAN_LEN:]).astype(bf16))
            context_rows.append(jnp.concatenate(pieces, axis=1))
        context = jnp.concatenate(context_rows, axis=0)
        total = total + lax.dot_general(
            context, weight(3, g), (((1,), (1,)), ((), ())), preferred_element_type=f32
        )
    out_ref[...] = total.astype(bf16)


def attend(head, x, states, weights):
    parts, entries, piece, width = x.shape
    spans = entries // 2
    steps = spans // SPANS_STEP
    rows = SPANS_STEP * SPAN_LEN
    last = states.shape[0] // SPAN_LEN - 1
    keys = 2 * parts * piece
    cols = width // weights.shape[1]

    def after(i, head_ref):
        return jnp.minimum((head_ref[0] * steps + i + 1) * SPANS_STEP, last), 0

    flops = 2 * spans * (keys * width * 2 * width + SPAN_LEN * 2 * width * width)
    return pl.pallas_call(
        attention_kernel,
        out_shape=jax.ShapeDtypeStruct((spans * SPAN_LEN, width), jnp.bfloat16),
        grid_spec=pltpu.PrefetchScalarGridSpec(
            num_scalar_prefetch=1,
            grid=(steps,),
            in_specs=[
                pl.BlockSpec((parts, 2 * SPANS_STEP, piece, width), lambda i, h: (0, i, 0, 0)),
                pl.BlockSpec((rows, width), lambda i, h: (h[0] * steps + i, 0)),
                pl.BlockSpec((SPAN_LEN, width), after),
                pl.BlockSpec(memory_space=pltpu.VMEM),
            ],
            out_specs=pl.BlockSpec((rows, width), lambda i, h: (i, 0)),
            scratch_shapes=[
                pltpu.VMEM((SPANS_STEP * keys, cols), jnp.bfloat16),
                pltpu.VMEM((SPANS_STEP * keys, cols), jnp.bfloat16),
            ],
        ),
        compiler_params=pltpu.CompilerParams(
            dimension_semantics=("arbitrary",), vmem_limit_bytes=48 * 1024 * 1024
        ),
        cost_estimate=pl.CostEstimate(
            flops=flops, bytes_accessed=2 * (x.size + weights.size), transcendentals=0
        ),
        name="attend",
    )(head, x, states, states, weights)


def body(
    decoder_states, encodings, neighbor_table, query_weight, key_weight, value_weight, out_weight
):
    peers = lax.axis_size("span")
    groups = lax.axis_size("head")
    span = lax.axis_index("span")
    head = lax.axis_index("head")
    width = decoder_states.shape[1]

    depth = width // peers
    part = jnp.concatenate(
        [
            lax.dynamic_slice_in_dim(w, span * depth, depth, 0)
            for w in (key_weight, value_weight, query_weight)
        ]
        + [lax.dynamic_slice_in_dim(out_weight, span * depth, depth, 1).T],
        axis=1,
    )
    weights = lax.all_gather(part, ("span", "head"), axis=0, tiled=False)
    weights = weights.reshape(peers, groups, depth, width)

    shard_ids = neighbor_table[:, :, 0].reshape(-1)
    slot_ids = neighbor_table[:, :, 1].reshape(-1)
    entries = shard_ids.shape[0]
    numbering = jnp.arange(entries, dtype=jnp.int32)
    placed = shard_ids[None, :] == numbering[:, None]
    request = jnp.sum(jnp.where(placed, slot_ids[None, :], 0), axis=1)
    wanted = lax.all_to_all(request, "span", split_axis=0, concat_axis=0, tiled=True)
    arrived = lax.all_to_all(
        encodings[wanted], "span", split_axis=0, concat_axis=0, tiled=True
    )
    ordered = arrived[shard_ids]
    own = lax.all_to_all(
        ordered.reshape(groups, entries // groups, *arrived.shape[1:]),
        "head",
        split_axis=0,
        concat_axis=0,
        tiled=True,
    )
    result = attend(head.reshape(1), own, decoder_states, weights)
    columns = lax.all_to_all(result, "head", split_axis=1, concat_axis=0, tiled=True)
    offset = SPAN_LEN - 1
    return jnp.concatenate(
        [jnp.zeros((offset, columns.shape[1]), columns.dtype), columns[: columns.shape[0] - offset]],
        axis=0,
    )


def solution(mesh):
    return jax.shard_map(
        body,
        mesh=mesh,
        in_specs=(
            P("span", None),
            P("span", "head", None),
            P("span", None, None),
            P(None, "head"),
            P(None, "head"),
            P(None, "head"),
            P("head", None),
        ),
        out_specs=P("span", "head"),
        check_vma=False,
    )
```

time: 561 us -> 904 us (1.61)
  waiting for transfers between devices: 352 us -> 731 us
  matrix products: 48.3 us -> 0 us
  local copies, waits for them, and re-layouts: 47 us -> 15.2 us
  Pallas kernels: 0 us -> 31.3 us
  starting transfers between devices: 0.22 us -> 13.9 us
    all_gather x2 -> x1, waiting for transfers between devices: 352 us -> 582 us  [body(): weights = lax.all_gather(part, ('span', 'head'), axis=0, tiled=False)]
    all_to_all x0 -> x2, waiting for transfers between devices: none -> 149 us  [the longest x1 95.6 us: body(): lax.all_to_all(ordered.reshape(groups, entries // groups, *arrived.shape[...]
    dot_general x5 -> x0, matrix products: 48.3 us -> none  [the longest x1 22.4 us: body(): jnp.einsum('chqk,ckhd->cqhd', weights, value_rows, preferred_element_type...]
    pallas_call x0 -> x1, Pallas kernels: none -> 31.3 us  [attend(): pl.pallas_call(attention_kernel, out_shape=jax.ShapeDtypeStruct((spans *...]
    all_to_all x0 -> x2, starting transfers between devices: none -> 13.9 us  [the longest x1 7.43 us: body(): lax.all_to_all(encodings[wanted], 'span', split_axis=0, concat_axis=0, ti...]
    unnamed x13 -> x3, local copies, waits for them, and re-layouts: 13.1 us -> 1.1 us
    all_to_all x2 -> x1, blocking collectives: 79.2 us -> 81.9 us  [body(): lax.all_to_all(result, 'head', split_axis=1, concat_axis=0, tiled=True)]
  transfers between devices with their start and end apart: 2 -> 3, of which waited for: 2 -> 3; matrix products, arithmetic and copies ran while one was open for 2% -> 1% of each run, Pallas kernels for 0% -> 0%
where the time goes in v1:
time: 904 us; the launch traced here: 903 us
  waiting for transfers between devices  731 us (81%)
  blocking collectives  96.7 us (11%)
  Pallas kernels  31.3 us (3%)
  local copies, waits for them, and re-layouts  15.2 us (2%)
  starting transfers between devices  13.9 us (2%)
  between operations  13.5 us (1%)
    all_gather x1, waiting for transfers between devices, body(): weights = lax.all_gather(part, ('span', 'head'), axis=0, tiled=False)  582 us
    all_to_all x1, waiting for transfers between devices, body(): lax.all_to_all(ordered.reshape(groups, entries // groups, *arrived.shape[...  95.6 us
    all_to_all x1, blocking collectives, body(): lax.all_to_all(result, 'head', split_axis=1, concat_axis=0, tiled=True)  81.9 us
    all_to_all x1, waiting for transfers between devices, body(): lax.all_to_all(encodings[wanted], 'span', split_axis=0, concat_axis=0, ti...  53.1 us
    pallas_call x1, Pallas kernels, attend(): pl.pallas_call(attention_kernel, out_shape=jax.ShapeDtypeStruct((spans *...  31.3 us
  transfers between devices with their start and end apart: 3, of which 3 were waited for; matrix products, arithmetic and copies ran while one was open for 1% of the time, Pallas kernels for 0%

profile of v1, /device:TPU:34, one launch (start us, length us, event | category | flops | bytes accessed | tf_op | source)
XLA Modules:
  0.0 903.5 jit_solution(2322200967793047187)
XLA Ops:
  6.5 0.0 copy-start
  6.5 0.0 all-gather.3.cloned.1.call-start
  6.5 1.0 copy-done
  7.6 0.1 constant_dynamic-slice_fusion
  7.7 0.1 copy.42
  7.7 0.7 constant_dynamic-slice_fusion.3
  8.5 0.7 constant_dynamic-slice_fusion.1
  9.2 0.6 pad_maximum_fusion
  9.8 0.0 all-gather.3.cloned.1.call-update
  9.8 0.8 fusion.2
  10.6 0.1 copy.37
  10.7 0.1 broadcast_in_dim.18
  10.8 0.1 copy.36
  10.9 0.1 eq.15
  11.0 0.1 select_reduce_fusion
  11.1 0.1 copy.38
  11.2 14.9 %all_to_all.41 = s32[64,1,1]{2,1,0:T(1,128)S(1)} all-to-all(s32[64,1,1]{2,1,0:T(1,128)S(1)} %copy.38), channel_id=1, replica_groups=mesh['span'=64,'head'=4] {'span'}, dimensions={0} | all-to-all | bytes 512 | tf_op jit(solution)/shard_map/all_to_all | solution.py:137
  26.1 1.2 reduce
  27.3 4.9 gather_fusion
  32.3 7.4 all-to-all-start.1
  39.7 0.1 reshape_squeeze.3
  39.8 53.1 %all-to-all-done.1 = bf16[64,32,1024]{2,1,0:T(8,128)(2,1)} async-done(((bf16[64,32,1024]{2,1,0:T(8,128)(2,1)}), bf16[64,32,1024]{2,1,0:T(8,128)(2,1)}, u32[]{:S(2)}, u32[]{:S(2)}) %all-to-all-start.1) | async-done | bytes 4194336 | tf_op jit(solution)/shard_map/all_to_all | solution.py:138
  93.0 4.9 gather_fusion.1
  97.9 6.5 all-to-all-start.2
  104.4 95.6 %all-to-all-done.2.x_ref = bf16[4,16,32,1024]{3,2,1,0:T(8,128)(2,1)} async-done(((bf16[4,16,32,1024]{3,2,1,0:T(8,128)(2,1)}), bf16[4,16,32,1024]{3,2,1,0:T(8,128)(2,1)}, u32[]{:S(2)}, u32[]{:S(2)}) %all-to-all-start.2) | async-done | bytes 4194336 | tf_op jit(solution)/shard_map/all_to_all | solution.py:142
  200.0 582.1 %all-gather.3.cloned.1.call-done = bf16[4096,1024]{1,0:T(8,128)(2,1)} async-done(((bf16[16,1024]{1,0:T(8,128)(2,1)}), bf16[4096,1024]{1,0:T(8,128)(2,1)}) %all-gather.3.cloned.1.call-update) | async-done | bytes 8388624 | tf_op jit(solution)/shard_map/all_gather | solution.py:128
  782.1 31.3 %attend.1 = bf16[512,1024]{1,0:T(8,128)(2,1)S(1)} custom-call(s32[1]{0:T(128)} %bitcast.head_ref, bf16[4,16,32,1024]{3,2,1,0:T(8,128)(2,1)} %all-to-all-done.2.x_ref, bf16[2048,1024]{1,0:T(8,128)(2,1)} %next_ref.1, bf16[2048,1024]{1,0:T(8,128)(2,1)} %next_ref.1, bf16[64,4,16,1024]{3,2,1,0:T(8,128)(2,1)} %bitcast.30), custom_call_target="tpu_custom_call" | custom-call | flops 10737418240 | bytes 12582912 | tf_op jit(solution)/shard_map/attend/pallas_call | solution.py:82
  813.4 0.1 copy.45
  813.5 81.9 %all_to_all.42 = bf16[512,4,256]{2,0,1:T(8,128)(2,1)S(1)} all-to-all(bf16[512,4,256]{2,0,1:T(8,128)(2,1)S(1)} %bitcast.26), channel_id=1, replica_groups=mesh['span'=64,'head'=4] {'head'}, dimensions={1} | all-to-all | bytes 2097152 | tf_op jit(solution)/shard_map/all_to_all | solution.py:150
  895.3 0.1 slice.16
  895.4 1.2 concatenate.7
  (4 shorter events, 0.0 us)
Async XLA Ops:
  6.5 1.0 copy-start
  6.5 775.5 %all-gather.3.cloned.1.call-start = ((), (), s32[]{:S(2)}) async-start(), calls=%async_computation.4 | async-start | bytes 8421376 | tf_op jit(solution)/shard_map/all_gather | solution.py:128
  32.3 60.7 %all-to-all-start.1 = ((bf16[64,32,1024]{2,1,0:T(8,128)(2,1)}), bf16[64,32,1024]{2,1,0:T(8,128)(2,1)}, u32[]{:S(2)}, u32[]{:S(2)}) async-start(bf16[64,32,1024]{2,1,0:T(8,128)(2,1)} %gather_fusion), calls=%async_computation.1 | async-start | bytes 8388608 | tf_op jit(solution)/shard_map/all_to_all | solution.py:138
  97.9 102.1 %all-to-all-start.2 = ((bf16[4,16,32,1024]{3,2,1,0:T(8,128)(2,1)}), bf16[4,16,32,1024]{3,2,1,0:T(8,128)(2,1)}, u32[]{:S(2)}, u32[]{:S(2)}) async-start(bf16[4,16,32,1024]{3,2,1,0:T(8,128)(2,1)} %bitcast.25), calls=%async_computation.2 | async-start | bytes 8388608 | tf_op jit(solution)/shard_map/all_to_all | solution.py:142
Sparse Core Ops, SparseCore 0:
  9.9 772.1 all-gather.2

commit v2 on v1

--- a/solution.py
+++ b/solution.py
@@ -10,6 +10,7 @@
 HEAD_DIM = 64
 SPAN_LEN = 64
 SPANS_STEP = 2
+SPAN = ("y", "x", "z", "core")
 
 
 def attention_kernel(head_ref, x_ref, now_ref, next_ref, w_ref, out_ref, k_ref, v_ref):
@@ -110,9 +111,9 @@
 def body(
     decoder_states, encodings, neighbor_table, query_weight, key_weight, value_weight, out_weight
 ):
-    peers = lax.axis_size("span")
+    peers = lax.axis_size(SPAN)
     groups = lax.axis_size("head")
-    span = lax.axis_index("span")
+    span = lax.axis_index(("core", "y", "z", "x"))
     head = lax.axis_index("head")
     width = decoder_states.shape[1]
 
@@ -125,7 +126,11 @@
         + [lax.dynamic_slice_in_dim(out_weight, span * depth, depth, 1).T],
         axis=1,
     )
-    weights = lax.all_gather(part, ("span", "head"), axis=0, tiled=False)
+    near = ("x", "head")
+    copies = jnp.broadcast_to(part[None], (lax.axis_size(near), depth, width))
+    weights = lax.all_to_all(copies, near, split_axis=0, concat_axis=0, tiled=True)
+    weights = lax.all_gather(weights, ("y", "z"), axis=0, tiled=True)
+    weights = lax.all_gather(weights, "core", axis=0, tiled=True)
     weights = weights.reshape(peers, groups, depth, width)
 
     shard_ids = neighbor_table[:, :, 0].reshape(-1)
@@ -134,9 +139,9 @@
     numbering = jnp.arange(entries, dtype=jnp.int32)
     placed = shard_ids[None, :] == numbering[:, None]
     request = jnp.sum(jnp.where(placed, slot_ids[None, :], 0), axis=1)
-    wanted = lax.all_to_all(request, "span", split_axis=0, concat_axis=0, tiled=True)
+    wanted = lax.all_to_all(request, SPAN, split_axis=0, concat_axis=0, tiled=True)
     arrived = lax.all_to_all(
-        encodings[wanted], "span", split_axis=0, concat_axis=0, tiled=True
+        encodings[wanted], SPAN, split_axis=0, concat_axis=0, tiled=True
     )
     ordered = arrived[shard_ids]
     own = lax.all_to_all(
@@ -156,18 +161,19 @@
 
 
 def solution(mesh):
+    fine = jax.sharding.Mesh(mesh.devices.reshape(4, 4, 2, 2, 4), SPAN + ("head",))
     return jax.shard_map(
         body,
-        mesh=mesh,
+        mesh=fine,
         in_specs=(
-            P("span", None),
-            P("span", "head", None),
-            P("span", None, None),
+            P(SPAN, None),
+            P(SPAN, "head", None),
+            P(SPAN, None, None),
             P(None, "head"),
             P(None, "head"),
             P(None, "head"),
             P("head", None),
         ),
-        out_specs=P("span", "head"),
+        out_specs=P(SPAN, "head"),
         check_vma=False,
     )

time: 904 us -> 351 us (0.39)
  waiting for transfers between devices: 731 us -> 202 us
  blocking collectives: 96.7 us -> 71.5 us
    all_gather x1 -> x2, waiting for transfers between devices: 582 us -> 110 us  [the longest x1 110 us: body(): weights = lax.all_gather(weights, ('y', 'z'), axis=0, tiled=True)]
    all_to_all x1, waiting for transfers between devices: 53.1 us -> 0.01 us  [body(): lax.all_to_all(encodings[wanted], SPAN, split_axis=0, concat_axis=0, tile...]
    all_to_all x1, blocking collectives: 81.9 us -> 29.9 us  [body(): lax.all_to_all(result, 'head', split_axis=1, concat_axis=0, tiled=True)]
    all_to_all x1 -> x2, blocking collectives: 14.9 us -> 41.7 us  [the longest x1 27.1 us: body(): lax.all_to_all(copies, near, split_axis=0, concat_axis=0, tiled=True)]
  transfers between devices with their start and end apart: 3 -> 4, of which waited for: 3 -> 2; matrix products, arithmetic and copies ran while one was open for 1% -> 4% of each run, Pallas kernels for 0% -> 0%
where the time goes in v2:
time: 351 us; the launch traced here: 349 us
  waiting for transfers between devices  202 us (58%)
  blocking collectives  71.5 us (20%)
  Pallas kernels  31.3 us (9%)
  local copies, waits for them, and re-layouts  15.3 us (4%)
  starting transfers between devices  14.2 us (4%)
  between operations  13.5 us (4%)
    all_gather x1, waiting for transfers between devices, body(): weights = lax.all_gather(weights, ('y', 'z'), axis=0, tiled=True)  110 us
    all_to_all x1, waiting for transfers between devices, body(): lax.all_to_all(ordered.reshape(groups, entries // groups, *arrived.shape[...  91.4 us
    pallas_call x1, Pallas kernels, attend(): pl.pallas_call(attention_kernel, out_shape=jax.ShapeDtypeStruct((spans *...  31.3 us
    all_to_all x1, blocking collectives, body(): lax.all_to_all(result, 'head', split_axis=1, concat_axis=0, tiled=True)  29.9 us
    all_to_all x1, blocking collectives, body(): lax.all_to_all(copies, near, split_axis=0, concat_axis=0, tiled=True)  27.1 us
    all_to_all x1, blocking collectives, body(): lax.all_to_all(request, SPAN, split_axis=0, concat_axis=0, tiled=True)  14.6 us
    all_to_all x1, starting transfers between devices, body(): lax.all_to_all(encodings[wanted], SPAN, split_axis=0, concat_axis=0, tile...  7.41 us
  transfers between devices with their start and end apart: 4, of which 2 were waited for; matrix products, arithmetic and copies ran while one was open for 4% of the time, Pallas kernels for 0%

profile of v2, /device:TPU:34, one launch (start us, length us, event | category | flops | bytes accessed | tf_op | source)
XLA Modules:
  0.0 349.0 jit_solution(13610370060962042081)
XLA Ops:
  6.5 0.0 copy-start
  6.5 0.0 all-gather.3.cloned.1.call-start
  6.5 1.0 copy-done
  7.6 0.1 constant_dynamic-slice_fusion
  7.7 0.1 copy.42
  7.7 0.7 constant_dynamic-slice_fusion.3
  8.5 0.7 constant_dynamic-slice_fusion.1
  9.2 0.1 broadcast_in_dim.27
  9.2 27.1 %all_to_all.46 = bf16[16,16,1024]{2,1,0:T(8,128)(2,1)} all-to-all(bf16[16,16,1024]{2,1,0:T(8,128)(2,1)S(1)} %broadcast_in_dim.27), channel_id=1, replica_groups=mesh['y'=4,'x'=4,'z'=2,'core'=2,'head'=4] {'x','head'}, dimensions={0} | all-to-all | bytes 1048576 | tf_op jit(solution)/shard_map/all_to_all | solution.py:131
  36.4 0.0 all-gather.3.cloned.1.call-update
  36.4 0.8 fusion.2
  37.1 0.1 copy.37
  37.2 0.1 broadcast_in_dim.24
  37.3 0.1 copy.36
  37.4 0.1 eq.15
  37.5 0.1 select_reduce_fusion
  37.7 0.1 copy.38
  37.8 14.6 %all_to_all.47 = s32[64,1,1]{2,1,0:T(1,128)S(1)} all-to-all(s32[64,1,1]{2,1,0:T(1,128)S(1)} %copy.38), channel_id=1, replica_groups=mesh['y'=4,'x'=4,'z'=2,'core'=2,'head'=4] {'y','x','z','core'}, dimensions={0} | all-to-all | bytes 512 | tf_op jit(solution)/shard_map/all_to_all | solution.py:142
  52.3 1.2 reduce
  53.6 5.0 %gather_fusion = bf16[64,32,1024]{2,1,0:T(8,128)(2,1)} fusion(bf16[64,32,1024]{2,1,0:T(8,128)(2,1)} %param.8, s32[1024]{0:T(1024)S(1)} %pad_clamp_fusion.1), kind=kCustom, calls=%fused_computation | custom fusion | bytes 8388864 | tf_op jit(solution)/shard_map/gather | solution.py:144
  58.5 7.4 %all-to-all-start.1 = ((bf16[64,32,1024]{2,1,0:T(8,128)(2,1)}), bf16[64,32,1024]{2,1,0:T(8,128)(2,1)}, u32[]{:S(2)}, u32[]{:S(2)}) async-start(bf16[64,32,1024]{2,1,0:T(8,128)(2,1)} %gather_fusion), calls=%async_computation.1 | async-start | bytes 8388608 | tf_op jit(solution)/shard_map/all_to_all | solution.py:143
  66.0 0.0 all-gather.5.cloned.1.call-start
  66.0 110.4 %all-gather.3.cloned.1.call-done = bf16[128,16,1024]{2,1,0:T(8,128)(2,1)} async-done(((bf16[16,16,1024]{2,1,0:T(8,128)(2,1)}), bf16[128,16,1024]{2,1,0:T(8,128)(2,1)}) %all-gather.3.cloned.1.call-update) | async-done | bytes 4194320 | tf_op jit(solution)/shard_map/all_gather | solution.py:132
  176.4 0.0 all-gather.5.cloned.1.call-update
  176.4 0.1 reshape_squeeze.3
  176.6 0.0 all-to-all-done.1
  176.6 4.9 %gather_fusion.1 = bf16[64,32,1024]{2,1,0:T(8,128)(2,1)} fusion(bf16[64,32,1024]{2,1,0:T(8,128)(2,1)} %all-to-all-done.1, s32[1024]{0:T(1024)S(1)} %pad_clamp_fusion), kind=kCustom, calls=%fused_computation.1 | custom fusion | bytes 8388864 | tf_op jit(solution)/shard_map/gather | solution.py:146
  181.5 6.7 %all-to-all-start.2 = ((bf16[4,16,32,1024]{3,2,1,0:T(8,128)(2,1)}), bf16[4,16,32,1024]{3,2,1,0:T(8,128)(2,1)}, u32[]{:S(2)}, u32[]{:S(2)}) async-start(bf16[4,16,32,1024]{3,2,1,0:T(8,128)(2,1)} %bitcast.25), calls=%async_computation.2 | async-start | bytes 8388608 | tf_op jit(solution)/shard_map/all_to_all | solution.py:147
  188.2 91.4 %all-to-all-done.2.x_ref = bf16[4,16,32,1024]{3,2,1,0:T(8,128)(2,1)} async-done(((bf16[4,16,32,1024]{3,2,1,0:T(8,128)(2,1)}), bf16[4,16,32,1024]{3,2,1,0:T(8,128)(2,1)}, u32[]{:S(2)}, u32[]{:S(2)}) %all-to-all-start.2) | async-done | bytes 4194336 | tf_op jit(solution)/shard_map/all_to_all | solution.py:147
  279.6 0.0 all-gather.5.cloned.1.call-done
  279.6 31.3 %attend.1 = bf16[512,1024]{1,0:T(8,128)(2,1)S(1)} custom-call(s32[1]{0:T(128)} %bitcast.head_ref, bf16[4,16,32,1024]{3,2,1,0:T(8,128)(2,1)} %all-to-all-done.2.x_ref, bf16[2048,1024]{1,0:T(8,128)(2,1)} %next_ref.1, bf16[2048,1024]{1,0:T(8,128)(2,1)} %next_ref.1, bf16[64,4,16,1024]{3,2,1,0:T(8,128)(2,1)} %bitcast.30), custom_call_target="tpu_custom_call" | custom-call | flops 10737418240 | bytes 12582912 | tf_op jit(solution)/shard_map/attend/pallas_call | solution.py:83
  311.0 0.1 copy.45
  311.1 29.9 %all_to_all.48 = bf16[512,4,256]{2,0,1:T(8,128)(2,1)S(1)} all-to-all(bf16[512,4,256]{2,0,1:T(8,128)(2,1)S(1)} %bitcast.26), channel_id=1, replica_groups=mesh['y'=4,'x'=4,'z'=2,'core'=2,'head'=4] {'head'}, dimensions={1} | all-to-all | bytes 2097152 | tf_op jit(solution)/shard_map/all_to_all | solution.py:155
  340.9 0.1 slice.16
  341.0 1.2 concatenate.7
  (5 shorter events, 0.0 us)
Async XLA Ops:
  6.5 1.0 copy-start
  6.5 169.9 %all-gather.3.cloned.1.call-start = ((), (), s32[]{:S(2)}) async-start(), calls=%async_computation.5 | async-start | bytes 4718592 | tf_op jit(solution)/shard_map/all_gather | solution.py:132
  58.5 118.0 %all-to-all-start.1 = ((bf16[64,32,1024]{2,1,0:T(8,128)(2,1)}), bf16[64,32,1024]{2,1,0:T(8,128)(2,1)}, u32[]{:S(2)}, u32[]{:S(2)}) async-start(bf16[64,32,1024]{2,1,0:T(8,128)(2,1)} %gather_fusion), calls=%async_computation.1 | async-start | bytes 8388608 | tf_op jit(solution)/shard_map/all_to_all | solution.py:143
  66.0 213.7 %all-gather.5.cloned.1.call-start = ((), (), s32[]{:S(2)}) async-start(), calls=%async_computation.6 | async-start | bytes 12582912 | tf_op jit(solution)/shard_map/all_gather | solution.py:133
  181.5 98.1 %all-to-all-start.2 = ((bf16[4,16,32,1024]{3,2,1,0:T(8,128)(2,1)}), bf16[4,16,32,1024]{3,2,1,0:T(8,128)(2,1)}, u32[]{:S(2)}, u32[]{:S(2)}) async-start(bf16[4,16,32,1024]{3,2,1,0:T(8,128)(2,1)} %bitcast.25), calls=%async_computation.2 | async-start | bytes 8388608 | tf_op jit(solution)/shard_map/all_to_all | solution.py:147
Sparse Core Ops, SparseCore 0:
  36.5 139.8 all-gather.2
  178.2 25.2 all-gather.4

commit v3 on v2

v3 whole, which is shorter than its diff:
```python
import jax
import jax.numpy as jnp
from jax import lax
from jax.experimental import pallas as pl
from jax.experimental.pallas import tpu as pltpu
from jax.sharding import PartitionSpec as P


HEAD_DIM = 64
SPAN_LEN = 64
SPANS_STEP = 2
CHUNKS = 2
SPAN = ("y", "x", "z", "core")


def attention_kernel(where_ref, *refs):
    x_refs = refs[:-8]
    now_ref, next_ref, own_ref, other_ref, out_ref, k_ref, v_ref, w_ref = refs[-8:]
    f32, bf16 = jnp.float32, jnp.bfloat16
    entries, piece, width = x_refs[0].shape
    spans = entries // 2
    some = 2 * piece
    keys = len(x_refs) * some
    groups = own_ref.shape[1]
    cols = width // groups

    @pl.when(pl.program_id(0) == 0)
    def _():
        core = where_ref[1]
        w_ref[core] = own_ref[...]
        w_ref[1 - core] = other_ref[...]

    rows = spans * SPAN_LEN

    x = jnp.concatenate(
        [
            x_ref[2 * i : 2 * i + 2].reshape(some, width)
            for i in range(spans)
            for x_ref in x_refs
        ],
        axis=0,
    )
    both = jnp.concatenate([now_ref[...], next_ref[...]], axis=0)
    row = lax.broadcasted_iota(jnp.int32, (rows, rows + SPAN_LEN), 0)
    col = lax.broadcasted_iota(jnp.int32, (rows, rows + SPAN_LEN), 1)
    shift = jnp.where(col == row + SPAN_LEN - 1, 1.0, 0.0).astype(bf16)
    states = jnp.dot(shift, both, preferred_element_type=f32).astype(bf16)

    def weight(which, g):
        return w_ref[:, :, g, :, which * cols : (which + 1) * cols].reshape(width, cols)

    total = jnp.zeros((rows, width), f32)
    lane = lax.broadcasted_iota(jnp.int32, (SPAN_LEN, 128), 1)
    low = lane < HEAD_DIM
    for g in range(groups):
        k_ref[...] = jnp.dot(x, weight(0, g), preferred_element_type=f32).astype(bf16)
        v_ref[...] = jnp.dot(x, weight(1, g), preferred_element_type=f32).astype(bf16)
        q = jnp.dot(states, weight(2, g), preferred_element_type=f32).astype(bf16)
        context_rows = []
        for i in range(spans):
            pieces = []
            for pair in range(cols // 128):
                here = slice(pair * 128, pair * 128 + 128)
                qp = q[i * SPAN_LEN : (i + 1) * SPAN_LEN, here]
                zero = jnp.zeros_like(qp)
                two = jnp.concatenate([jnp.where(low, qp, zero), jnp.where(low, zero, qp)], axis=0)
                kp = k_ref[i * keys : (i + 1) * keys, here]
                vp = v_ref[i * keys : (i + 1) * keys, here]
                scores = lax.dot_general(
                    two, kp, (((1,), (1,)), ((), ())), preferred_element_type=f32
                ) * (HEAD_DIM ** -0.5)
                top = jnp.max(scores, axis=1, keepdims=True)
                raised = jnp.exp(scores - top)
                weights = raised * (1.0 / jnp.sum(raised, axis=1, keepdims=True))
                mixed = jnp.dot(weights.astype(bf16), vp, preferred_element_type=f32)
                pieces.append(jnp.where(low, mixed[:SPAN_LEN], mixed[SPAN_LEN:]).astype(bf16))
            context_rows.append(jnp.concatenate(pieces, axis=1))
        context = jnp.concatenate(context_rows, axis=0)
        total = total + lax.dot_general(
            context, weight(3, g), (((1,), (1,)), ((), ())), preferred_element_type=f32
        )
    for g in range(groups):
        out_ref[g] = total[:, g * cols : (g + 1) * cols].astype(bf16)


def attend(where, chunks, states, weights, other):
    entries, piece, width = chunks[0].shape
    spans = entries // 2
    steps = spans // SPANS_STEP
    rows = SPANS_STEP * SPAN_LEN
    last = states.shape[0] // SPAN_LEN - 1
    keys = 2 * piece * len(chunks)
    groups = weights.shape[1]
    cols = width // groups

    def after(i, where_ref):
        return jnp.minimum((where_ref[0] * steps + i + 1) * SPANS_STEP, last), 0

    flops = 2 * spans * (keys * width * 2 * width + SPAN_LEN * 2 * width * width)
    return pl.pallas_call(
        attention_kernel,
        out_shape=jax.ShapeDtypeStruct((groups, spans * SPAN_LEN, cols), jnp.bfloat16),
        grid_spec=pltpu.PrefetchScalarGridSpec(
            num_scalar_prefetch=1,
            grid=(steps,),
            in_specs=[
                pl.BlockSpec((2 * SPANS_STEP, piece, width), lambda i, h: (i, 0, 0))
                for _ in chunks
            ]
            + [
                pl.BlockSpec((rows, width), lambda i, h: (h[0] * steps + i, 0)),
                pl.BlockSpec((SPAN_LEN, width), after),
                pl.BlockSpec(memory_space=pltpu.VMEM),
                pl.BlockSpec(memory_space=pltpu.VMEM),
            ],
            out_specs=pl.BlockSpec((groups, rows, cols), lambda i, h: (0, i, 0)),
            scratch_shapes=[
                pltpu.VMEM((SPANS_STEP * keys, cols), jnp.bfloat16),
                pltpu.VMEM((SPANS_STEP * keys, cols), jnp.bfloat16),
                pltpu.VMEM((2, *weights.shape), jnp.bfloat16),
            ],
        ),
        compiler_params=pltpu.CompilerParams(
            dimension_semantics=("arbitrary",), vmem_limit_bytes=48 * 1024 * 1024
        ),
        cost_estimate=pl.CostEstimate(
            flops=flops, bytes_accessed=2 * (len(chunks) * chunks[0].size + 2 * weights.size), transcendentals=0
        ),
        name="attend",
    )(where, *chunks, states, states, weights, other)


def layer(
    decoder_states, encodings, neighbor_table, query_weight, key_weight, value_weight, out_weight
):
    peers = lax.axis_size(SPAN)
    groups = lax.axis_size("head")
    span = lax.axis_index(("core", "y", "x", "z"))
    head = lax.axis_index("head")
    width = decoder_states.shape[1]

    depth = width // peers
    part = jnp.concatenate(
        [
            lax.dynamic_slice_in_dim(w, span * depth, depth, 0)
            for w in (key_weight, value_weight, query_weight)
        ]
        + [lax.dynamic_slice_in_dim(out_weight, span * depth, depth, 1).T],
        axis=1,
    )
    column = ("z", "head")
    planes = lax.axis_size(column)
    place = lax.axis_index(column)
    passed = [part] + [
        lax.ppermute(part, column, [(i, (i + step) % planes) for i in range(planes)])
        for step in range(1, planes)
    ]
    order = (place - jnp.arange(planes, dtype=jnp.int32)) % planes
    stacked = jnp.stack(passed)[order]
    shard_ids = neighbor_table[:, :, 0].reshape(-1)
    slot_ids = neighbor_table[:, :, 1].reshape(-1)
    entries = shard_ids.shape[0]
    numbering = jnp.arange(entries, dtype=jnp.int32)
    placed = shard_ids[None, :] == numbering[:, None]
    request = jnp.sum(jnp.where(placed, slot_ids[None, :], 0), axis=1)
    wanted = lax.all_to_all(request, SPAN, split_axis=0, concat_axis=0, tiled=True)
    stacked, wanted = lax.optimization_barrier((stacked, wanted))
    weights = lax.all_gather(stacked, ("y", "x"), axis=0, tiled=True)
    piece = encodings.shape[1] // CHUNKS
    pieces = encodings.reshape(-1, piece, width)
    sources = shard_ids.reshape(groups, -1)
    owned = []
    for c in range(CHUNKS):
        arrived = lax.all_to_all(
            pieces[CHUNKS * wanted + c], SPAN, split_axis=0, concat_axis=0, tiled=True
        )
        for step in range(groups):
            block = arrived[sources[(head + step) % groups]]
            if step:
                block = lax.ppermute(
                    block, "head", [(i, (i + step) % groups) for i in range(groups)]
                )
            owned.append(block)
    weights = weights.reshape(peers // 2, groups, depth, width)
    other = lax.ppermute(weights, "core", [(0, 1), (1, 0)])
    where = jnp.stack([head, lax.axis_index("core")])
    result = attend(where, owned, decoder_states, weights, other)
    columns = lax.all_to_all(result, "head", split_axis=0, concat_axis=0, tiled=True)
    columns = columns.reshape(decoder_states.shape[0], width // groups)
    offset = SPAN_LEN - 1
    return jnp.concatenate(
        [jnp.zeros((offset, columns.shape[1]), columns.dtype), columns[: columns.shape[0] - offset]],
        axis=0,
    )


def solution(mesh):
    fine = jax.sharding.Mesh(mesh.devices.reshape(4, 4, 2, 2, 4), SPAN + ("head",))
    return jax.shard_map(
        layer,
        mesh=fine,
        in_specs=(
            P(SPAN, None),
            P(SPAN, "head", None),
            P(SPAN, None, None),
            P(None, "head"),
            P(None, "head"),
            P(None, "head"),
            P("head", None),
        ),
        out_specs=P(SPAN, "head"),
        check_vma=False,
    )
```

time: 351 us -> 339 us (0.966)
  blocking collectives: 71.5 us -> 24.8 us
  starting transfers between devices: 14.2 us -> 54.7 us
  waiting for transfers between devices: 202 us -> 175 us
  local copies, waits for them, and re-layouts: 15.3 us -> 34.8 us
    ppermute x0 -> x14, waiting for transfers between devices: none -> 100 us  [the longest x6 93.3 us: layer(): lax.ppermute(block, 'head', [(i, (i + step) % groups) for i in range(grou...]
    all_gather x2 -> x1, waiting for transfers between devices: 110 us -> 43.6 us  [layer(): weights = lax.all_gather(stacked, ('y', 'x'), axis=0, tiled=True)]
    all_to_all x2 -> x3, waiting for transfers between devices: 91.4 us -> 31.6 us  [the longest x2 25.6 us: layer(): lax.all_to_all(pieces[CHUNKS * wanted + c], SPAN, split_axis=0, concat_ax...]
    all_to_all x3 -> x1, blocking collectives: 71.5 us -> 24.8 us  [layer(): lax.all_to_all(result, 'head', split_axis=0, concat_axis=0, tiled=True)]
    ppermute x0 -> x14, starting transfers between devices: none -> 31.4 us  [the longest x7 18.7 us: layer(): lax.ppermute(part, column, [(i, (i + step) % planes) for i in range(plane...]
    gather x2 -> x11, local copies, waits for them, and re-layouts: 9.92 us -> 28.8 us  [the longest x8 19 us: layer(): block = arrived[sources[(head + step) % groups]]]
    all_to_all x2 -> x3, starting transfers between devices: 14.1 us -> 23.2 us  [the longest x2 14.3 us: layer(): lax.all_to_all(pieces[CHUNKS * wanted + c], SPAN, split_axis=0, concat_ax...]
  transfers between devices with their start and end apart: 4 -> 18, of which waited for: 2 -> 9; matrix products, arithmetic and copies ran while one was open for 4% -> 9% of each run, Pallas kernels for 0% -> 0%
where the time goes in v3:
time: 339 us; the launch traced here: 337 us
  waiting for transfers between devices  175 us (52%)
  starting transfers between devices  54.7 us (16%)
  local copies, waits for them, and re-layouts  34.8 us (10%)
  Pallas kernels  32.5 us (10%)
  blocking collectives  24.8 us (7%)
  between operations  13.6 us (4%)
    ppermute x6, waiting for transfers between devices, layer(): lax.ppermute(block, 'head', [(i, (i + step) % groups) for i in range(grou...  93.3 us
    all_gather x1, waiting for transfers between devices, layer(): weights = lax.all_gather(stacked, ('y', 'x'), axis=0, tiled=True)  43.6 us
    pallas_call x1, Pallas kernels, attend(): pl.pallas_call(attention_kernel, out_shape=jax.ShapeDtypeStruct((groups,...  32.5 us
    all_to_all x2, waiting for transfers between devices, layer(): lax.all_to_all(pieces[CHUNKS * wanted + c], SPAN, split_axis=0, concat_ax...  25.6 us
    all_to_all x1, blocking collectives, layer(): lax.all_to_all(result, 'head', split_axis=0, concat_axis=0, tiled=True)  24.8 us
    gather x8, local copies, waits for them, and re-layouts, layer(): block = arrived[sources[(head + step) % groups]]  19 us
    ppermute x7, starting transfers between devices, layer(): lax.ppermute(part, column, [(i, (i + step) % planes) for i in range(plane...  18.7 us
    all_to_all x2, starting transfers between devices, layer(): lax.all_to_all(pieces[CHUNKS * wanted + c], SPAN, split_axis=0, concat_ax...  14.3 us
  transfers between devices with their start and end apart: 18, of which 9 were waited for; matrix products, arithmetic and copies ran while one was open for 9% of the time, Pallas kernels for 0%

profile of v3, /device:TPU:34, one launch (start us, length us, event | category | flops | bytes accessed | tf_op | source)
XLA Modules:
  0.0 337.2 jit_solution(4072034029598280288)
XLA Ops:
  6.5 1.0 copy-done
  7.6 0.9 constant_dynamic-slice_fusion.4
  8.5 0.1 copy.37
  8.6 0.7 constant_dynamic-slice_fusion.5
  9.3 5.8 %collective-permute-start.5 = (bf16[16,1024]{1,0:T(8,128)(2,1)S(1)}, bf16[16,1024]{1,0:T(8,128)(2,1)S(1)}, u32[]{:S(2)}, u32[]{:S(2)}) collective-permute-start(bf16[16,1024]{1,0:T(8,128)(2,1)S(1)} %pad_maximum_fusion), channel_id=1, source_target_pairs={{0,10},{1,11},{2,0},{3,1},{8,2},{9,3},{10,8},{11,9},{4,14},{5,15},... | collective-permute-start | bytes 98312 | tf_op jit(solution)/shard_map/ppermute | solution.py:155
  15.2 1.0 collective-permute-start.4
  16.2 1.9 collective-permute-start.3
  18.1 2.2 collective-permute-start.2
  20.3 0.3 collective-permute-start
  20.6 0.8 fusion.10
  21.3 0.1 copy.33
  21.4 0.1 eq.26
  21.5 0.1 copy.34
  21.6 0.1 broadcast_in_dim.18
  21.7 0.1 select_reduce_fusion
  21.8 0.7 copy.35
  22.6 8.9 %all-to-all-start = ((s32[64,1,1]{2,1,0:T(1,128)}), s32[64,1,1]{2,1,0:T(1,128)S(1)}, u32[]{:S(2)}, u32[]{:S(2)}) async-start(s32[64,1,1]{2,1,0:T(1,128)} %copy.35), calls=%async_computation | async-start | bytes 65536 | tf_op jit(solution)/shard_map/all_to_all | solution.py:166
  31.5 0.0 all-gather.2.cloned.1.call-start
  31.6 6.0 %all-to-all-done = s32[64,1,1]{2,1,0:T(1,128)S(1)} async-done(((s32[64,1,1]{2,1,0:T(1,128)}), s32[64,1,1]{2,1,0:T(1,128)S(1)}, u32[]{:S(2)}, u32[]{:S(2)}) %all-to-all-start) | async-done | bytes 288 | tf_op jit(solution)/shard_map/all_to_all | solution.py:166
  37.6 1.2 reduce
  38.8 0.0 collective-permute-done
  38.8 2.2 collective-permute-start.1
  41.0 5.2 %collective-permute-done.1 = bf16[16,1024]{1,0:T(8,128)(2,1)S(1)} collective-permute-done((bf16[16,1024]{1,0:T(8,128)(2,1)S(1)}, bf16[16,1024]{1,0:T(8,128)(2,1)S(1)}, u32[]{:S(2)}, u32[]{:S(2)}) %collective-permute-start.1) | collective-permute-done | bytes 32800 | tf_op jit(solution)/shard_map/ppermute | solution.py:155
  46.2 5.3 %collective-permute-start.6 = (bf16[16,1024]{1,0:T(8,128)(2,1)S(1)}, bf16[16,1024]{1,0:T(8,128)(2,1)S(1)}, u32[]{:S(2)}, u32[]{:S(2)}) collective-permute-start(bf16[16,1024]{1,0:T(8,128)(2,1)S(1)} %pad_maximum_fusion), channel_id=1, source_target_pairs={{0,11},{1,0},{2,1},{3,2},{8,3},{9,8},{10,9},{11,10},{4,15},{5,4},{... | collective-permute-start | bytes 98312 | tf_op jit(solution)/shard_map/ppermute | solution.py:155
  51.5 0.0 collective-permute-done.2
  51.5 0.0 collective-permute-done.3
  51.5 0.0 collective-permute-done.4
  51.6 0.0 collective-permute-done.5
  51.6 1.5 collective-permute-done.6
  53.1 1.3 gather_fusion
  54.4 0.0 all-gather.2.cloned.1.call-update
  54.4 4.2 %gather_fusion.1 = bf16[64,16,1024]{2,1,0:T(8,128)(2,1)} fusion(bf16[128,16,1024]{2,1,0:T(8,128)(2,1)} %bitcast.63, s32[1024]{0:T(1024)S(1)} %pad_clamp_fusion.5), kind=kCustom, calls=%fused_computation.1 | custom fusion | bytes 4194560 | tf_op jit(solution)/shard_map/gather | solution.py:175
  58.6 6.2 %all-to-all-start.1 = ((bf16[64,16,1024]{2,1,0:T(8,128)(2,1)}), bf16[64,16,1024]{2,1,0:T(8,128)(2,1)S(1)}, u32[]{:S(2)}, u32[]{:S(2)}) async-start(bf16[64,16,1024]{2,1,0:T(8,128)(2,1)} %gather_fusion.1), calls=%async_computation.1 | async-start | bytes 4194304 | tf_op jit(solution)/shard_map/all_to_all | solution.py:174
  64.8 4.4 %gather_fusion.6 = bf16[64,16,1024]{2,1,0:T(8,128)(2,1)} fusion(bf16[128,16,1024]{2,1,0:T(8,128)(2,1)} %bitcast.64, s32[1024]{0:T(1024)S(1)} %pad_clamp_fusion), kind=kCustom, calls=%fused_computation.6 | custom fusion | bytes 4194560 | tf_op jit(solution)/shard_map/gather | solution.py:175
  69.2 25.6 %all-to-all-done.1 = bf16[64,16,1024]{2,1,0:T(8,128)(2,1)S(1)} async-done(((bf16[64,16,1024]{2,1,0:T(8,128)(2,1)}), bf16[64,16,1024]{2,1,0:T(8,128)(2,1)S(1)}, u32[]{:S(2)}, u32[]{:S(2)}) %all-to-all-start.1) | async-done | bytes 2097184 | tf_op jit(solution)/shard_map/all_to_all | solution.py:174
  94.8 8.1 %all-to-all-start.2 = ((bf16[64,16,1024]{2,1,0:T(8,128)(2,1)}), bf16[64,16,1024]{2,1,0:T(8,128)(2,1)}, u32[]{:S(2)}, u32[]{:S(2)}) async-start(bf16[64,16,1024]{2,1,0:T(8,128)(2,1)} %gather_fusion.6), calls=%async_computation.2 | async-start | bytes 4194304 | tf_op jit(solution)/shard_map/all_to_all | solution.py:174
  102.9 43.6 %all-gather.2.cloned.1.call-done = bf16[128,16,1024]{2,1,0:T(8,128)(2,1)} async-done(((bf16[8,16,1024]{2,1,0:T(8,128)(2,1)}), bf16[128,16,1024]{2,1,0:T(8,128)(2,1)}) %all-gather.2.cloned.1.call-update) | async-done | bytes 4194320 | tf_op jit(solution)/shard_map/all_gather | solution.py:168
  146.5 0.0 collective-permute-start.13
  146.5 0.1 reshape_reshape_squeeze.3
  146.6 1.4 gather_fusion.3
  148.0 0.6 collective-permute-start.7
  148.6 1.4 gather_fusion.4
  149.9 6.0 %collective-permute-start.8 = (bf16[16,16,1024]{2,1,0:T(8,128)(2,1)}, bf16[16,16,1024]{2,1,0:T(8,128)(2,1)S(1)}, u32[]{:S(2)}, u32[]{:S(2)}) collective-permute-start(bf16[16,16,1024]{2,1,0:T(8,128)(2,1)} %gather_fusion.4), channel_id=1, source_target_pairs={{0,2},{1,3},{2,0},{3,1},{4,6},{5,7},{6,4},{7,5},{8,10},{9,11},{10,... | collective-permute-start | bytes 1572872 | tf_op jit(solution)/shard_map/ppermute | solution.py:180
  155.9 3.0 gather_fusion.5
  158.9 0.0 collective-permute-start.9
  158.9 3.0 gather_fusion.8
  161.9 2.9 collective-permute-start.10
  164.8 3.0 gather_fusion.10
  167.8 3.0 gather_fusion.9
  170.8 61.1 %collective-permute-done.7.refs_1_ = bf16[16,16,1024]{2,1,0:T(8,128)(2,1)S(1)} collective-permute-done((bf16[16,16,1024]{2,1,0:T(8,128)(2,1)}, bf16[16,16,1024]{2,1,0:T(8,128)(2,1)S(1)}, u32[]{:S(2)}, u32[]{:S(2)}) %collective-permute-start.7) | collective-permute-done | bytes 524320 | tf_op jit(solution)/shard_map/ppermute | solution.py:180
  231.8 2.6 collective-permute-start.11
  234.5 0.6 collective-permute-start.12
  235.1 0.1 pad_add_fusion.where_ref
  235.2 2.2 gather_fusion.2
  237.3 2.2 gather_fusion.7
  239.5 0.0 collective-permute-done.9.refs_3_
  239.5 3.6 %collective-permute-done.10.refs_5_ = bf16[16,16,1024]{2,1,0:T(8,128)(2,1)} collective-permute-done((bf16[16,16,1024]{2,1,0:T(8,128)(2,1)}, bf16[16,16,1024]{2,1,0:T(8,128)(2,1)}, u32[]{:S(2)}, u32[]{:S(2)}) %collective-permute-start.10) | collective-permute-done | bytes 524320 | tf_op jit(solution)/shard_map/ppermute | solution.py:180
  243.2 17.3 %collective-permute-done.11.refs_6_ = bf16[16,16,1024]{2,1,0:T(8,128)(2,1)} collective-permute-done((bf16[16,16,1024]{2,1,0:T(8,128)(2,1)}, bf16[16,16,1024]{2,1,0:T(8,128)(2,1)}, u32[]{:S(2)}, u32[]{:S(2)}) %collective-permute-start.11) | collective-permute-done | bytes 524320 | tf_op jit(solution)/shard_map/ppermute | solution.py:180
  260.5 11.3 %collective-permute-done.12.refs_7_ = bf16[16,16,1024]{2,1,0:T(8,128)(2,1)} collective-permute-done((bf16[16,16,1024]{2,1,0:T(8,128)(2,1)}, bf16[16,16,1024]{2,1,0:T(8,128)(2,1)}, u32[]{:S(2)}, u32[]{:S(2)}) %collective-permute-start.12) | collective-permute-done | bytes 524320 | tf_op jit(solution)/shard_map/ppermute | solution.py:180
  271.7 0.0 collective-permute-done.13.refs_11_
  271.7 32.5 %attend.1 = bf16[4,512,256]{2,1,0:T(8,128)(2,1)S(1)} custom-call(s32[2]{0:T(128)S(1)} %pad_add_fusion.where_ref, bf16[16,16,1024]{2,1,0:T(8,128)(2,1)S(1)} %gather_fusion.2, bf16[16,16,1024]{2,1,0:T(8,128)(2,1)S(1)} %collective-permute-done.7.refs_1_, bf16[16,16,1024]{2,1,0:T(8,128)(2,1)S(1)} %collective-permute-done.8.refs_2_, ...), custom_call_target="tpu_custom_call" | custom-call | flops 10737418240 | bytes 12582912 | tf_op jit(solution)/shard_map/attend/pallas_call | solution.py:100
  304.3 24.8 %all_to_all.27 = bf16[4,512,256]{2,1,0:T(8,128)(2,1)S(1)} all-to-all(bf16[4,512,256]{2,1,0:T(8,128)(2,1)S(1)} %attend.1), channel_id=1, replica_groups=mesh['y'=4,'x'=4,'z'=2,'core'=2,'head'=4] {'head'}, dimensions={0} | all-to-all | bytes 2097152 | tf_op jit(solution)/shard_map/all_to_all | solution.py:188
  329.1 0.1 slice.34
  329.1 1.2 concatenate.7
  (25 shorter events, 0.1 us)
Async XLA Ops:
  6.5 1.0 copy-start
  9.3 42.3 %collective-permute-start.5 = (bf16[16,1024]{1,0:T(8,128)(2,1)S(1)}, bf16[16,1024]{1,0:T(8,128)(2,1)S(1)}, u32[]{:S(2)}, u32[]{:S(2)}) collective-permute-start(bf16[16,1024]{1,0:T(8,128)(2,1)S(1)} %pad_maximum_fusion), channel_id=1, source_target_pairs={{0,10},{1,11},{2,0},{3,1},{8,2},{9,3},{10,8},{11,9},{4,14},{5,15},... | collective-permute-start | bytes 98312 | tf_op jit(solution)/shard_map/ppermute | solution.py:155
  15.2 36.4 %collective-permute-start.4 = (bf16[16,1024]{1,0:T(8,128)(2,1)S(1)}, bf16[16,1024]{1,0:T(8,128)(2,1)S(1)}, u32[]{:S(2)}, u32[]{:S(2)}) collective-permute-start(bf16[16,1024]{1,0:T(8,128)(2,1)S(1)} %pad_maximum_fusion), channel_id=1, source_target_pairs={{0,9},{1,10},{2,11},{3,0},{8,1},{9,2},{10,3},{11,8},{4,13},{5,14},... | collective-permute-start | bytes 98312 | tf_op jit(solution)/shard_map/ppermute | solution.py:155
  16.2 35.3 %collective-permute-start.3 = (bf16[16,1024]{1,0:T(8,128)(2,1)S(1)}, bf16[16,1024]{1,0:T(8,128)(2,1)S(1)}, u32[]{:S(2)}, u32[]{:S(2)}) collective-permute-start(bf16[16,1024]{1,0:T(8,128)(2,1)S(1)} %pad_maximum_fusion), channel_id=1, source_target_pairs={{0,8},{1,9},{2,10},{3,11},{8,0},{9,1},{10,2},{11,3},{4,12},{5,13},... | collective-permute-start | bytes 98312 | tf_op jit(solution)/shard_map/ppermute | solution.py:155
  18.1 33.4 %collective-permute-start.2 = (bf16[16,1024]{1,0:T(8,128)(2,1)S(1)}, bf16[16,1024]{1,0:T(8,128)(2,1)S(1)}, u32[]{:S(2)}, u32[]{:S(2)}) collective-permute-start(bf16[16,1024]{1,0:T(8,128)(2,1)S(1)} %pad_maximum_fusion), channel_id=1, source_target_pairs={{0,3},{1,8},{2,9},{3,10},{8,11},{9,0},{10,1},{11,2},{4,7},{5,12},{... | collective-permute-start | bytes 98312 | tf_op jit(solution)/shard_map/ppermute | solution.py:155
  20.3 18.5 %collective-permute-start = (bf16[16,1024]{1,0:T(8,128)(2,1)S(1)}, bf16[16,1024]{1,0:T(8,128)(2,1)S(1)}, u32[]{:S(2)}, u32[]{:S(2)}) collective-permute-start(bf16[16,1024]{1,0:T(8,128)(2,1)S(1)} %pad_maximum_fusion), channel_id=1, source_target_pairs={{0,1},{1,2},{2,3},{3,8},{8,9},{9,10},{10,11},{11,0},{4,5},{5,6},{6... | collective-permute-start | bytes 98312 | tf_op jit(solution)/shard_map/ppermute | solution.py:155
  22.6 15.0 %all-to-all-start = ((s32[64,1,1]{2,1,0:T(1,128)}), s32[64,1,1]{2,1,0:T(1,128)S(1)}, u32[]{:S(2)}, u32[]{:S(2)}) async-start(s32[64,1,1]{2,1,0:T(1,128)} %copy.35), calls=%async_computation | async-start | bytes 65536 | tf_op jit(solution)/shard_map/all_to_all | solution.py:166
  31.5 115.0 %all-gather.2.cloned.1.call-start = ((), (), s32[]{:S(2)}) async-start(), calls=%async_computation.4 | async-start | bytes 4456448 | tf_op jit(solution)/shard_map/all_gather | solution.py:168
  38.8 7.4 %collective-permute-start.1 = (bf16[16,1024]{1,0:T(8,128)(2,1)S(1)}, bf16[16,1024]{1,0:T(8,128)(2,1)S(1)}, u32[]{:S(2)}, u32[]{:S(2)}) collective-permute-start(bf16[16,1024]{1,0:T(8,128)(2,1)S(1)} %pad_maximum_fusion), channel_id=1, source_target_pairs={{0,2},{1,3},{2,8},{3,9},{8,10},{9,11},{10,0},{11,1},{4,6},{5,7},{6... | collective-permute-start | bytes 98312 | tf_op jit(solution)/shard_map/ppermute | solution.py:155
  46.2 6.9 %collective-permute-start.6 = (bf16[16,1024]{1,0:T(8,128)(2,1)S(1)}, bf16[16,1024]{1,0:T(8,128)(2,1)S(1)}, u32[]{:S(2)}, u32[]{:S(2)}) collective-permute-start(bf16[16,1024]{1,0:T(8,128)(2,1)S(1)} %pad_maximum_fusion), channel_id=1, source_target_pairs={{0,11},{1,0},{2,1},{3,2},{8,3},{9,8},{10,9},{11,10},{4,15},{5,4},{... | collective-permute-start | bytes 98312 | tf_op jit(solution)/shard_map/ppermute | solution.py:155
  58.6 36.2 %all-to-all-start.1 = ((bf16[64,16,1024]{2,1,0:T(8,128)(2,1)}), bf16[64,16,1024]{2,1,0:T(8,128)(2,1)S(1)}, u32[]{:S(2)}, u32[]{:S(2)}) async-start(bf16[64,16,1024]{2,1,0:T(8,128)(2,1)} %gather_fusion.1), calls=%async_computation.1 | async-start | bytes 4194304 | tf_op jit(solution)/shard_map/all_to_all | solution.py:174
  94.8 53.8 %copy-start.1 = (bf16[64,16,1024]{2,1,0:T(8,128)(2,1)}, bf16[64,16,1024]{2,1,0:T(8,128)(2,1)S(1)}, u32[]{:S(2)}) copy-start(bf16[64,16,1024]{2,1,0:T(8,128)(2,1)S(1)} %all-to-all-done.1) | copy-start | bytes 6291460
  94.8 64.1 %all-to-all-start.2 = ((bf16[64,16,1024]{2,1,0:T(8,128)(2,1)}), bf16[64,16,1024]{2,1,0:T(8,128)(2,1)}, u32[]{:S(2)}, u32[]{:S(2)}) async-start(bf16[64,16,1024]{2,1,0:T(8,128)(2,1)} %gather_fusion.6), calls=%async_computation.2 | async-start | bytes 4194304 | tf_op jit(solution)/shard_map/all_to_all | solution.py:174
  146.5 125.2 %collective-permute-start.13 = (bf16[32,4,16,1024]{3,2,1,0:T(8,128)(2,1)}, bf16[32,4,16,1024]{3,2,1,0:T(8,128)(2,1)}, u32[]{:S(2)}, u32[]{:S(2)}) collective-permute-start(bf16[32,4,16,1024]{3,2,1,0:T(8,128)(2,1)} %bitcast.69), channel_id=1, source_target_pairs={{0,4},{4,0},{1,5},{5,1},{2,6},{6,2},{3,7},{7,3},{8,12},{12,8},{9,1... | collective-permute-start | bytes 12582920 | tf_op jit(solution)/shard_map/ppermute | solution.py:185
  148.0 83.8 %collective-permute-start.7 = (bf16[16,16,1024]{2,1,0:T(8,128)(2,1)}, bf16[16,16,1024]{2,1,0:T(8,128)(2,1)S(1)}, u32[]{:S(2)}, u32[]{:S(2)}) collective-permute-start(bf16[16,16,1024]{2,1,0:T(8,128)(2,1)} %gather_fusion.3), channel_id=1, source_target_pairs={{0,1},{1,2},{2,3},{3,0},{4,5},{5,6},{6,7},{7,4},{8,9},{9,10},{10,1... | collective-permute-start | bytes 1572872 | tf_op jit(solution)/shard_map/ppermute | solution.py:180
  149.9 84.5 %collective-permute-start.8 = (bf16[16,16,1024]{2,1,0:T(8,128)(2,1)}, bf16[16,16,1024]{2,1,0:T(8,128)(2,1)S(1)}, u32[]{:S(2)}, u32[]{:S(2)}) collective-permute-start(bf16[16,16,1024]{2,1,0:T(8,128)(2,1)} %gather_fusion.4), channel_id=1, source_target_pairs={{0,2},{1,3},{2,0},{3,1},{4,6},{5,7},{6,4},{7,5},{8,10},{9,11},{10,... | collective-permute-start | bytes 1572872 | tf_op jit(solution)/shard_map/ppermute | solution.py:180
  158.9 80.6 %collective-permute-start.9 = (bf16[16,16,1024]{2,1,0:T(8,128)(2,1)}, bf16[16,16,1024]{2,1,0:T(8,128)(2,1)S(1)}, u32[]{:S(2)}, u32[]{:S(2)}) collective-permute-start(bf16[16,16,1024]{2,1,0:T(8,128)(2,1)} %gather_fusion.5), channel_id=1, source_target_pairs={{0,3},{1,0},{2,1},{3,2},{4,7},{5,4},{6,5},{7,6},{8,11},{9,8},{10,9... | collective-permute-start | bytes 1572872 | tf_op jit(solution)/shard_map/ppermute | solution.py:180
  161.9 81.3 %collective-permute-start.10 = (bf16[16,16,1024]{2,1,0:T(8,128)(2,1)}, bf16[16,16,1024]{2,1,0:T(8,128)(2,1)}, u32[]{:S(2)}, u32[]{:S(2)}) collective-permute-start(bf16[16,16,1024]{2,1,0:T(8,128)(2,1)} %gather_fusion.8), channel_id=1, source_target_pairs={{0,1},{1,2},{2,3},{3,0},{4,5},{5,6},{6,7},{7,4},{8,9},{9,10},{10,1... | collective-permute-start | bytes 1572872 | tf_op jit(solution)/shard_map/ppermute | solution.py:180
  231.8 28.6 %collective-permute-start.11 = (bf16[16,16,1024]{2,1,0:T(8,128)(2,1)}, bf16[16,16,1024]{2,1,0:T(8,128)(2,1)}, u32[]{:S(2)}, u32[]{:S(2)}) collective-permute-start(bf16[16,16,1024]{2,1,0:T(8,128)(2,1)} %gather_fusion.9), channel_id=1, source_target_pairs={{0,2},{1,3},{2,0},{3,1},{4,6},{5,7},{6,4},{7,5},{8,10},{9,11},{10,... | collective-permute-start | bytes 1572872 | tf_op jit(solution)/shard_map/ppermute | solution.py:180
  234.5 37.3 %collective-permute-start.12 = (bf16[16,16,1024]{2,1,0:T(8,128)(2,1)}, bf16[16,16,1024]{2,1,0:T(8,128)(2,1)}, u32[]{:S(2)}, u32[]{:S(2)}) collective-permute-start(bf16[16,16,1024]{2,1,0:T(8,128)(2,1)} %gather_fusion.10), channel_id=1, source_target_pairs={{0,3},{1,0},{2,1},{3,2},{4,7},{5,4},{6,5},{7,6},{8,11},{9,8},{10,9... | collective-permute-start | bytes 1572872 | tf_op jit(solution)/shard_map/ppermute | solution.py:180
Sparse Core Ops, SparseCore 0:
  54.5 91.9 all-gather.1

commit v4 on v3

--- a/solution.py
+++ b/solution.py
@@ -130,6 +130,14 @@
     )(where, *chunks, states, states, weights, other)
 
 
+def span_groups(peers, groups, turn):
+    low = [(s // 2) % 2 == 0 for s in range(peers)]
+    return [
+        [s * groups + (h + (turn if low[s] else 0)) % groups for s in range(peers)]
+        for h in range(groups)
+    ]
+
+
 def layer(
     decoder_states, encodings, neighbor_table, query_weight, key_weight, value_weight, out_weight
 ):
@@ -151,10 +159,9 @@
     column = ("z", "head")
     planes = lax.axis_size(column)
     place = lax.axis_index(column)
-    passed = [part] + [
-        lax.ppermute(part, column, [(i, (i + step) % planes) for i in range(planes)])
-        for step in range(1, planes)
-    ]
+    passed = [part]
+    for step in range(1, planes):
+        passed.append(lax.ppermute(part, column, [(i, (i + step) % planes) for i in range(planes)]))
     order = (place - jnp.arange(planes, dtype=jnp.int32)) % planes
     stacked = jnp.stack(passed)[order]
     shard_ids = neighbor_table[:, :, 0].reshape(-1)
@@ -164,7 +171,6 @@
     placed = shard_ids[None, :] == numbering[:, None]
     request = jnp.sum(jnp.where(placed, slot_ids[None, :], 0), axis=1)
     wanted = lax.all_to_all(request, SPAN, split_axis=0, concat_axis=0, tiled=True)
-    stacked, wanted = lax.optimization_barrier((stacked, wanted))
     weights = lax.all_gather(stacked, ("y", "x"), axis=0, tiled=True)
     piece = encodings.shape[1] // CHUNKS
     pieces = encodings.reshape(-1, piece, width)
@@ -172,7 +178,12 @@
     owned = []
     for c in range(CHUNKS):
         arrived = lax.all_to_all(
-            pieces[CHUNKS * wanted + c], SPAN, split_axis=0, concat_axis=0, tiled=True
+            pieces[CHUNKS * wanted + c],
+            SPAN + ("head",),
+            split_axis=0,
+            concat_axis=0,
+            axis_index_groups=span_groups(peers, groups, c % 2),
+            tiled=True,
         )
         for step in range(groups):
             block = arrived[sources[(head + step) % groups]]

time: 339 us -> 302 us (0.89)
  the two profiles are of different devices: /device:TPU:34 before, /device:TPU:1 now
where the time goes in v4:
time: 302 us; the launch traced here: 301 us
  waiting for transfers between devices  135 us (45%)
  blocking collectives  48.1 us (16%)
  starting transfers between devices  36.3 us (12%)
  local copies, waits for them, and re-layouts  34.1 us (11%)
  Pallas kernels  32.6 us (11%)
  between operations  13.6 us (5%)
    all_to_all x2, waiting for transfers between devices, layer(): lax.all_to_all(pieces[CHUNKS * wanted + c], SPAN + ('head',), split_axis=...  81.3 us
    ppermute x6, waiting for transfers between devices, layer(): lax.ppermute(block, 'head', [(i, (i + step) % groups) for i in range(grou...  40.6 us
    pallas_call x1, Pallas kernels, attend(): pl.pallas_call(attention_kernel, out_shape=jax.ShapeDtypeStruct((groups,...  32.6 us
    all_to_all x1, blocking collectives, layer(): lax.all_to_all(result, 'head', split_axis=0, concat_axis=0, tiled=True)  25.4 us
    all_to_all x1, blocking collectives, layer(): lax.all_to_all(request, SPAN, split_axis=0, concat_axis=0, tiled=True)  22.7 us
    gather x8, local copies, waits for them, and re-layouts, layer(): block = arrived[sources[(head + step) % groups]]  19 us
    ppermute x7, starting transfers between devices, layer(): lax.ppermute(part, column, [(i, (i + step) % planes) for i in range(plane...  14 us
    all_to_all x2, starting transfers between devices, layer(): lax.all_to_all(pieces[CHUNKS * wanted + c], SPAN + ('head',), split_axis=...  12.6 us
  transfers between devices with their start and end apart: 17, of which 9 were waited for; matrix products, arithmetic and copies ran while one was open for 10% of the time, Pallas kernels for 0%

profile of v4, /device:TPU:1, one launch (start us, length us, event | category | flops | bytes accessed | tf_op | source)
XLA Modules:
  0.0 301.2 jit_solution(17883467362821445528)
XLA Ops:
  6.5 1.0 copy-done
  7.6 0.9 constant_dynamic-slice_fusion
  8.5 0.1 copy.37
  8.6 0.7 constant_dynamic-slice_fusion.1
  9.3 7.3 %collective-permute-start.11 = (bf16[16,1024]{1,0:T(8,128)(2,1)S(1)}, bf16[16,1024]{1,0:T(8,128)(2,1)S(1)}, u32[]{:S(2)}, u32[]{:S(2)}) collective-permute-start(bf16[16,1024]{1,0:T(8,128)(2,1)S(1)} %pad_maximum_fusion), channel_id=1, source_target_pairs={{0,10},{1,11},{2,0},{3,1},{8,2},{9,3},{10,8},{11,9},{4,14},{5,15},... | collective-permute-start | bytes 98312 | tf_op jit(solution)/shard_map/ppermute | solution.py:164
  16.6 1.6 collective-permute-start.10
  18.2 0.0 collective-permute-start.9
  18.2 2.7 collective-permute-start.8
  20.9 0.0 collective-permute-start.6
  20.9 4.0 %collective-permute-done.6 = bf16[16,1024]{1,0:T(8,128)(2,1)S(1)} collective-permute-done((bf16[16,1024]{1,0:T(8,128)(2,1)S(1)}, bf16[16,1024]{1,0:T(8,128)(2,1)S(1)}, u32[]{:S(2)}, u32[]{:S(2)}) %collective-permute-start.6) | collective-permute-done | bytes 32800 | tf_op jit(solution)/shard_map/ppermute | solution.py:164
  25.0 1.8 collective-permute-start.7
  26.8 3.9 %collective-permute-done.7 = bf16[16,1024]{1,0:T(8,128)(2,1)S(1)} collective-permute-done((bf16[16,1024]{1,0:T(8,128)(2,1)S(1)}, bf16[16,1024]{1,0:T(8,128)(2,1)S(1)}, u32[]{:S(2)}, u32[]{:S(2)}) %collective-permute-start.7) | collective-permute-done | bytes 32800 | tf_op jit(solution)/shard_map/ppermute | solution.py:164
  30.7 0.6 collective-permute-start.12
  31.3 0.0 collective-permute-done.8
  31.3 0.0 collective-permute-done.9
  31.3 0.0 collective-permute-done.10
  31.3 0.0 collective-permute-done.11
  31.4 3.0 %collective-permute-done.12 = bf16[16,1024]{1,0:T(8,128)(2,1)S(1)} collective-permute-done((bf16[16,1024]{1,0:T(8,128)(2,1)S(1)}, bf16[16,1024]{1,0:T(8,128)(2,1)S(1)}, u32[]{:S(2)}, u32[]{:S(2)}) %collective-permute-start.12) | collective-permute-done | bytes 32800 | tf_op jit(solution)/shard_map/ppermute | solution.py:164
  34.4 1.3 gather_fusion.10
  35.7 0.0 all-gather.3.cloned.1.call-update
  35.7 0.8 fusion.12
  36.4 0.1 copy.32
  36.5 0.1 eq.26
  36.6 0.1 copy.33
  36.7 0.1 broadcast_in_dim.14
  36.8 0.1 select_reduce_fusion
  37.0 0.1 copy.34
  37.1 22.7 %all_to_all.24 = s32[64,1,1]{2,1,0:T(1,128)S(1)} all-to-all(s32[64,1,1]{2,1,0:T(1,128)S(1)} %copy.34), channel_id=1, replica_groups=mesh['y'=4,'x'=4,'z'=2,'core'=2,'head'=4] {'y','x','z','core'}, dimensions={0} | all-to-all | bytes 512 | tf_op jit(solution)/shard_map/all_to_all | solution.py:173
  59.8 1.2 multiply_reduce_fusion
  61.0 4.3 %gather_fusion = bf16[64,16,1024]{2,1,0:T(8,128)(2,1)} fusion(bf16[128,16,1024]{2,1,0:T(8,128)(2,1)} %bitcast.75, s32[1024]{0:T(1024)S(1)} %pad_clamp_fusion.6), kind=kCustom, calls=%fused_computation | custom fusion | bytes 4194560 | tf_op jit(solution)/shard_map/gather | solution.py:181
  65.3 4.8 %all-to-all-start.1 = ((bf16[64,16,1024]{2,1,0:T(8,128)(2,1)}), bf16[64,16,1024]{2,1,0:T(8,128)(2,1)S(1)}, u32[]{:S(2)}, u32[]{:S(2)}) async-start(bf16[64,16,1024]{2,1,0:T(8,128)(2,1)} %gather_fusion), calls=%async_computation.1 | async-start | bytes 4194304 | tf_op jit(solution)/shard_map/all_to_all | solution.py:180
  70.1 4.2 %gather_fusion.5 = bf16[64,16,1024]{2,1,0:T(8,128)(2,1)} fusion(bf16[128,16,1024]{2,1,0:T(8,128)(2,1)} %bitcast.76, s32[1024]{0:T(1024)S(1)} %pad_clamp_fusion.1), kind=kCustom, calls=%fused_computation.5 | custom fusion | bytes 4194560 | tf_op jit(solution)/shard_map/gather | solution.py:181
  74.3 29.8 %all-to-all-done.1 = bf16[64,16,1024]{2,1,0:T(8,128)(2,1)S(1)} async-done(((bf16[64,16,1024]{2,1,0:T(8,128)(2,1)}), bf16[64,16,1024]{2,1,0:T(8,128)(2,1)S(1)}, u32[]{:S(2)}, u32[]{:S(2)}) %all-to-all-start.1) | async-done | bytes 2097184 | tf_op jit(solution)/shard_map/all_to_all | solution.py:180
  104.1 7.8 %all-to-all-start.2 = ((bf16[64,16,1024]{2,1,0:T(8,128)(2,1)}), bf16[64,16,1024]{2,1,0:T(8,128)(2,1)}, u32[]{:S(2)}, u32[]{:S(2)}) async-start(bf16[64,16,1024]{2,1,0:T(8,128)(2,1)} %gather_fusion.5), calls=%async_computation.2 | async-start | bytes 4194304 | tf_op jit(solution)/shard_map/all_to_all | solution.py:180
  112.0 2.2 all-gather.3.cloned.1.call-done
  114.2 0.5 collective-permute-start.13
  114.6 0.1 reshape_reshape_squeeze.3
  114.8 1.4 gather_fusion.2
  116.1 0.0 collective-permute-start
  116.2 1.4 gather_fusion.3
  117.5 3.6 %collective-permute-start.1 = (bf16[16,16,1024]{2,1,0:T(8,128)(2,1)}, bf16[16,16,1024]{2,1,0:T(8,128)(2,1)S(1)}, u32[]{:S(2)}, u32[]{:S(2)}) collective-permute-start(bf16[16,16,1024]{2,1,0:T(8,128)(2,1)} %gather_fusion.3), channel_id=1, source_target_pairs={{0,2},{1,3},{2,0},{3,1},{4,6},{5,7},{6,4},{7,5},{8,10},{9,11},{10,... | collective-permute-start | bytes 1572872 | tf_op jit(solution)/shard_map/ppermute | solution.py:191
  121.2 3.0 gather_fusion.4
  124.1 1.1 collective-permute-start.2
  125.2 51.4 %all-to-all-done.2 = bf16[64,16,1024]{2,1,0:T(8,128)(2,1)} async-done(((bf16[64,16,1024]{2,1,0:T(8,128)(2,1)}), bf16[64,16,1024]{2,1,0:T(8,128)(2,1)}, u32[]{:S(2)}, u32[]{:S(2)}) %all-to-all-start.2) | async-done | bytes 2097184 | tf_op jit(solution)/shard_map/all_to_all | solution.py:180
  176.7 3.0 gather_fusion.7
  179.7 0.5 collective-permute-start.3
  180.2 3.0 gather_fusion.9
  183.1 3.0 gather_fusion.8
  186.1 0.0 collective-permute-done.refs_1_
  186.1 0.4 collective-permute-start.4
  186.5 0.0 collective-permute-done.1.refs_2_
  186.5 3.6 %collective-permute-start.5 = (bf16[16,16,1024]{2,1,0:T(8,128)(2,1)}, bf16[16,16,1024]{2,1,0:T(8,128)(2,1)}, u32[]{:S(2)}, u32[]{:S(2)}) collective-permute-start(bf16[16,16,1024]{2,1,0:T(8,128)(2,1)} %gather_fusion.9), channel_id=1, source_target_pairs={{0,3},{1,0},{2,1},{3,2},{4,7},{5,4},{6,5},{7,6},{8,11},{9,8},{10,9... | collective-permute-start | bytes 1572872 | tf_op jit(solution)/shard_map/ppermute | solution.py:191
  190.0 0.1 pad_add_fusion.where_ref
  190.1 2.2 gather_fusion.1
  192.3 2.2 gather_fusion.6
  194.5 0.0 collective-permute-done.2.refs_3_
  194.5 9.6 %collective-permute-done.3.refs_5_ = bf16[16,16,1024]{2,1,0:T(8,128)(2,1)} collective-permute-done((bf16[16,16,1024]{2,1,0:T(8,128)(2,1)}, bf16[16,16,1024]{2,1,0:T(8,128)(2,1)}, u32[]{:S(2)}, u32[]{:S(2)}) %collective-permute-start.3) | collective-permute-done | bytes 524320 | tf_op jit(solution)/shard_map/ppermute | solution.py:191
  204.1 23.0 %collective-permute-done.4.refs_6_ = bf16[16,16,1024]{2,1,0:T(8,128)(2,1)} collective-permute-done((bf16[16,16,1024]{2,1,0:T(8,128)(2,1)}, bf16[16,16,1024]{2,1,0:T(8,128)(2,1)}, u32[]{:S(2)}, u32[]{:S(2)}) %collective-permute-start.4) | collective-permute-done | bytes 524320 | tf_op jit(solution)/shard_map/ppermute | solution.py:191
  227.1 8.0 %collective-permute-done.5.refs_7_ = bf16[16,16,1024]{2,1,0:T(8,128)(2,1)} collective-permute-done((bf16[16,16,1024]{2,1,0:T(8,128)(2,1)}, bf16[16,16,1024]{2,1,0:T(8,128)(2,1)}, u32[]{:S(2)}, u32[]{:S(2)}) %collective-permute-start.5) | collective-permute-done | bytes 524320 | tf_op jit(solution)/shard_map/ppermute | solution.py:191
  235.1 0.0 collective-permute-done.13.refs_11_
  235.1 32.6 %attend.1 = bf16[4,512,256]{2,1,0:T(8,128)(2,1)S(1)} custom-call(s32[2]{0:T(128)S(1)} %pad_add_fusion.where_ref, bf16[16,16,1024]{2,1,0:T(8,128)(2,1)S(1)} %gather_fusion.1, bf16[16,16,1024]{2,1,0:T(8,128)(2,1)S(1)} %collective-permute-done.refs_1_, bf16[16,16,1024]{2,1,0:T(8,128)(2,1)S(1)} %collective-permute-done.1.refs_2_, ...), custom_call_target="tpu_custom_call" | custom-call | flops 10737418240 | bytes 12582912 | tf_op jit(solution)/shard_map/attend/pallas_call | solution.py:100
  267.6 25.4 %all_to_all.25 = bf16[4,512,256]{2,1,0:T(8,128)(2,1)S(1)} all-to-all(bf16[4,512,256]{2,1,0:T(8,128)(2,1)S(1)} %attend.1), channel_id=1, replica_groups=mesh['y'=4,'x'=4,'z'=2,'core'=2,'head'=4] {'head'}, dimensions={0} | all-to-all | bytes 2097152 | tf_op jit(solution)/shard_map/all_to_all | solution.py:199
  293.1 0.1 slice.34
  293.1 1.2 concatenate.7
  (24 shorter events, 0.1 us)
Async XLA Ops:
  6.5 1.0 copy-start
  6.5 107.6 %all-gather.3.cloned.1.call-start = ((), (), s32[]{:S(2)}) async-start(), calls=%async_computation.4 | async-start | bytes 4456448 | tf_op jit(solution)/shard_map/all_gather | solution.py:174
  9.3 22.0 %collective-permute-start.11 = (bf16[16,1024]{1,0:T(8,128)(2,1)S(1)}, bf16[16,1024]{1,0:T(8,128)(2,1)S(1)}, u32[]{:S(2)}, u32[]{:S(2)}) collective-permute-start(bf16[16,1024]{1,0:T(8,128)(2,1)S(1)} %pad_maximum_fusion), channel_id=1, source_target_pairs={{0,10},{1,11},{2,0},{3,1},{8,2},{9,3},{10,8},{11,9},{4,14},{5,15},... | collective-permute-start | bytes 98312 | tf_op jit(solution)/shard_map/ppermute | solution.py:164
  16.6 14.7 %collective-permute-start.10 = (bf16[16,1024]{1,0:T(8,128)(2,1)S(1)}, bf16[16,1024]{1,0:T(8,128)(2,1)S(1)}, u32[]{:S(2)}, u32[]{:S(2)}) collective-permute-start(bf16[16,1024]{1,0:T(8,128)(2,1)S(1)} %pad_maximum_fusion), channel_id=1, source_target_pairs={{0,9},{1,10},{2,11},{3,0},{8,1},{9,2},{10,3},{11,8},{4,13},{5,14},... | collective-permute-start | bytes 98312 | tf_op jit(solution)/shard_map/ppermute | solution.py:164
  18.2 13.1 %collective-permute-start.9 = (bf16[16,1024]{1,0:T(8,128)(2,1)S(1)}, bf16[16,1024]{1,0:T(8,128)(2,1)S(1)}, u32[]{:S(2)}, u32[]{:S(2)}) collective-permute-start(bf16[16,1024]{1,0:T(8,128)(2,1)S(1)} %pad_maximum_fusion), channel_id=1, source_target_pairs={{0,8},{1,9},{2,10},{3,11},{8,0},{9,1},{10,2},{11,3},{4,12},{5,13},... | collective-permute-start | bytes 98312 | tf_op jit(solution)/shard_map/ppermute | solution.py:164
  18.2 13.0 %collective-permute-start.8 = (bf16[16,1024]{1,0:T(8,128)(2,1)S(1)}, bf16[16,1024]{1,0:T(8,128)(2,1)S(1)}, u32[]{:S(2)}, u32[]{:S(2)}) collective-permute-start(bf16[16,1024]{1,0:T(8,128)(2,1)S(1)} %pad_maximum_fusion), channel_id=1, source_target_pairs={{0,3},{1,8},{2,9},{3,10},{8,11},{9,0},{10,1},{11,2},{4,7},{5,12},{... | collective-permute-start | bytes 98312 | tf_op jit(solution)/shard_map/ppermute | solution.py:164
  20.9 4.0 %collective-permute-start.6 = (bf16[16,1024]{1,0:T(8,128)(2,1)S(1)}, bf16[16,1024]{1,0:T(8,128)(2,1)S(1)}, u32[]{:S(2)}, u32[]{:S(2)}) collective-permute-start(bf16[16,1024]{1,0:T(8,128)(2,1)S(1)} %pad_maximum_fusion), channel_id=1, source_target_pairs={{0,1},{1,2},{2,3},{3,8},{8,9},{9,10},{10,11},{11,0},{4,5},{5,6},{6... | collective-permute-start | bytes 98312 | tf_op jit(solution)/shard_map/ppermute | solution.py:164
  25.0 5.8 %collective-permute-start.7 = (bf16[16,1024]{1,0:T(8,128)(2,1)S(1)}, bf16[16,1024]{1,0:T(8,128)(2,1)S(1)}, u32[]{:S(2)}, u32[]{:S(2)}) collective-permute-start(bf16[16,1024]{1,0:T(8,128)(2,1)S(1)} %pad_maximum_fusion), channel_id=1, source_target_pairs={{0,2},{1,3},{2,8},{3,9},{8,10},{9,11},{10,0},{11,1},{4,6},{5,7},{6... | collective-permute-start | bytes 98312 | tf_op jit(solution)/shard_map/ppermute | solution.py:164
  30.7 3.7 %collective-permute-start.12 = (bf16[16,1024]{1,0:T(8,128)(2,1)S(1)}, bf16[16,1024]{1,0:T(8,128)(2,1)S(1)}, u32[]{:S(2)}, u32[]{:S(2)}) collective-permute-start(bf16[16,1024]{1,0:T(8,128)(2,1)S(1)} %pad_maximum_fusion), channel_id=1, source_target_pairs={{0,11},{1,0},{2,1},{3,2},{8,3},{9,8},{10,9},{11,10},{4,15},{5,4},{... | collective-permute-start | bytes 98312 | tf_op jit(solution)/shard_map/ppermute | solution.py:164
  65.3 38.8 %all-to-all-start.1 = ((bf16[64,16,1024]{2,1,0:T(8,128)(2,1)}), bf16[64,16,1024]{2,1,0:T(8,128)(2,1)S(1)}, u32[]{:S(2)}, u32[]{:S(2)}) async-start(bf16[64,16,1024]{2,1,0:T(8,128)(2,1)} %gather_fusion), calls=%async_computation.1 | async-start | bytes 4194304 | tf_op jit(solution)/shard_map/all_to_all | solution.py:180
  104.1 12.0 %copy-start.1 = (bf16[64,16,1024]{2,1,0:T(8,128)(2,1)}, bf16[64,16,1024]{2,1,0:T(8,128)(2,1)S(1)}, u32[]{:S(2)}) copy-start(bf16[64,16,1024]{2,1,0:T(8,128)(2,1)S(1)} %all-to-all-done.1) | copy-start | bytes 6291460
  104.1 72.6 %all-to-all-start.2 = ((bf16[64,16,1024]{2,1,0:T(8,128)(2,1)}), bf16[64,16,1024]{2,1,0:T(8,128)(2,1)}, u32[]{:S(2)}, u32[]{:S(2)}) async-start(bf16[64,16,1024]{2,1,0:T(8,128)(2,1)} %gather_fusion.5), calls=%async_computation.2 | async-start | bytes 4194304 | tf_op jit(solution)/shard_map/all_to_all | solution.py:180
  114.2 120.9 %collective-permute-start.13 = (bf16[32,4,16,1024]{3,2,1,0:T(8,128)(2,1)}, bf16[32,4,16,1024]{3,2,1,0:T(8,128)(2,1)}, u32[]{:S(2)}, u32[]{:S(2)}) collective-permute-start(bf16[32,4,16,1024]{3,2,1,0:T(8,128)(2,1)} %bitcast.81), channel_id=1, source_target_pairs={{0,4},{4,0},{1,5},{5,1},{2,6},{6,2},{3,7},{7,3},{8,12},{12,8},{9,1... | collective-permute-start | bytes 12582920 | tf_op jit(solution)/shard_map/ppermute | solution.py:196
  116.1 69.9 %collective-permute-start = (bf16[16,16,1024]{2,1,0:T(8,128)(2,1)}, bf16[16,16,1024]{2,1,0:T(8,128)(2,1)S(1)}, u32[]{:S(2)}, u32[]{:S(2)}) collective-permute-start(bf16[16,16,1024]{2,1,0:T(8,128)(2,1)} %gather_fusion.2), channel_id=1, source_target_pairs={{0,1},{1,2},{2,3},{3,0},{4,5},{5,6},{6,7},{7,4},{8,9},{9,10},{10,1... | collective-permute-start | bytes 1572872 | tf_op jit(solution)/shard_map/ppermute | solution.py:191
  117.5 68.9 %collective-permute-start.1 = (bf16[16,16,1024]{2,1,0:T(8,128)(2,1)}, bf16[16,16,1024]{2,1,0:T(8,128)(2,1)S(1)}, u32[]{:S(2)}, u32[]{:S(2)}) collective-permute-start(bf16[16,16,1024]{2,1,0:T(8,128)(2,1)} %gather_fusion.3), channel_id=1, source_target_pairs={{0,2},{1,3},{2,0},{3,1},{4,6},{5,7},{6,4},{7,5},{8,10},{9,11},{10,... | collective-permute-start | bytes 1572872 | tf_op jit(solution)/shard_map/ppermute | solution.py:191
  124.1 70.3 %collective-permute-start.2 = (bf16[16,16,1024]{2,1,0:T(8,128)(2,1)}, bf16[16,16,1024]{2,1,0:T(8,128)(2,1)S(1)}, u32[]{:S(2)}, u32[]{:S(2)}) collective-permute-start(bf16[16,16,1024]{2,1,0:T(8,128)(2,1)} %gather_fusion.4), channel_id=1, source_target_pairs={{0,3},{1,0},{2,1},{3,2},{4,7},{5,4},{6,5},{7,6},{8,11},{9,8},{10,9... | collective-permute-start | bytes 1572872 | tf_op jit(solution)/shard_map/ppermute | solution.py:191
  179.7 24.5 %collective-permute-start.3 = (bf16[16,16,1024]{2,1,0:T(8,128)(2,1)}, bf16[16,16,1024]{2,1,0:T(8,128)(2,1)}, u32[]{:S(2)}, u32[]{:S(2)}) collective-permute-start(bf16[16,16,1024]{2,1,0:T(8,128)(2,1)} %gather_fusion.7), channel_id=1, source_target_pairs={{0,1},{1,2},{2,3},{3,0},{4,5},{5,6},{6,7},{7,4},{8,9},{9,10},{10,1... | collective-permute-start | bytes 1572872 | tf_op jit(solution)/shard_map/ppermute | solution.py:191
  186.1 41.0 %collective-permute-start.4 = (bf16[16,16,1024]{2,1,0:T(8,128)(2,1)}, bf16[16,16,1024]{2,1,0:T(8,128)(2,1)}, u32[]{:S(2)}, u32[]{:S(2)}) collective-permute-start(bf16[16,16,1024]{2,1,0:T(8,128)(2,1)} %gather_fusion.8), channel_id=1, source_target_pairs={{0,2},{1,3},{2,0},{3,1},{4,6},{5,7},{6,4},{7,5},{8,10},{9,11},{10,... | collective-permute-start | bytes 1572872 | tf_op jit(solution)/shard_map/ppermute | solution.py:191
  186.5 48.6 %collective-permute-start.5 = (bf16[16,16,1024]{2,1,0:T(8,128)(2,1)}, bf16[16,16,1024]{2,1,0:T(8,128)(2,1)}, u32[]{:S(2)}, u32[]{:S(2)}) collective-permute-start(bf16[16,16,1024]{2,1,0:T(8,128)(2,1)} %gather_fusion.9), channel_id=1, source_target_pairs={{0,3},{1,0},{2,1},{3,2},{4,7},{5,4},{6,5},{7,6},{8,11},{9,8},{10,9... | collective-permute-start | bytes 1572872 | tf_op jit(solution)/shard_map/ppermute | solution.py:191
Sparse Core Ops, SparseCore 0:
  35.8 78.3 all-gather.2

commit v5 on v4

--- a/solution.py
+++ b/solution.py
@@ -9,7 +9,7 @@
 HEAD_DIM = 64
 SPAN_LEN = 64
 SPANS_STEP = 2
-CHUNKS = 2
+CHUNKS = 4
 SPAN = ("y", "x", "z", "core")
 
 
@@ -17,9 +17,9 @@
     x_refs = refs[:-8]
     now_ref, next_ref, own_ref, other_ref, out_ref, k_ref, v_ref, w_ref = refs[-8:]
     f32, bf16 = jnp.float32, jnp.bfloat16
-    entries, piece, width = x_refs[0].shape
-    spans = entries // 2
-    some = 2 * piece
+    spans = SPANS_STEP
+    some, width = x_refs[0].shape
+    some //= spans
     keys = len(x_refs) * some
     groups = own_ref.shape[1]
     cols = width // groups
@@ -34,7 +34,7 @@
 
     x = jnp.concatenate(
         [
-            x_ref[2 * i : 2 * i + 2].reshape(some, width)
+            x_ref[i * some : (i + 1) * some]
             for i in range(spans)
             for x_ref in x_refs
         ],
@@ -84,12 +84,13 @@
 
 
 def attend(where, chunks, states, weights, other):
-    entries, piece, width = chunks[0].shape
-    spans = entries // 2
+    total, width = chunks[0].shape
+    spans = states.shape[0] // SPAN_LEN // weights.shape[1]
+    some = total // spans
     steps = spans // SPANS_STEP
     rows = SPANS_STEP * SPAN_LEN
     last = states.shape[0] // SPAN_LEN - 1
-    keys = 2 * piece * len(chunks)
+    keys = some * len(chunks)
     groups = weights.shape[1]
     cols = width // groups
 
@@ -104,7 +105,7 @@
             num_scalar_prefetch=1,
             grid=(steps,),
             in_specs=[
-                pl.BlockSpec((2 * SPANS_STEP, piece, width), lambda i, h: (i, 0, 0))
+                pl.BlockSpec((SPANS_STEP * some, width), lambda i, h: (i, 0))
                 for _ in chunks
             ]
             + [
@@ -143,26 +144,23 @@
 ):
     peers = lax.axis_size(SPAN)
     groups = lax.axis_size("head")
-    span = lax.axis_index(("core", "y", "x", "z"))
+    share = lax.axis_index(("core", "y", "x"))
     head = lax.axis_index("head")
     width = decoder_states.shape[1]
 
-    depth = width // peers
+    depth = width // lax.axis_size(("core", "y", "x"))
     part = jnp.concatenate(
         [
-            lax.dynamic_slice_in_dim(w, span * depth, depth, 0)
+            lax.dynamic_slice_in_dim(w, share * depth, depth, 0)
             for w in (key_weight, value_weight, query_weight)
         ]
-        + [lax.dynamic_slice_in_dim(out_weight, span * depth, depth, 1).T],
+        + [lax.dynamic_slice_in_dim(out_weight, share * depth, depth, 1).T],
         axis=1,
     )
-    column = ("z", "head")
-    planes = lax.axis_size(column)
-    place = lax.axis_index(column)
     passed = [part]
-    for step in range(1, planes):
-        passed.append(lax.ppermute(part, column, [(i, (i + step) % planes) for i in range(planes)]))
-    order = (place - jnp.arange(planes, dtype=jnp.int32)) % planes
+    for step in range(1, groups):
+        passed.append(lax.ppermute(part, "head", [(i, (i + step) % groups) for i in range(groups)]))
+    order = (head - jnp.arange(groups, dtype=jnp.int32)) % groups
     stacked = jnp.stack(passed)[order]
     shard_ids = neighbor_table[:, :, 0].reshape(-1)
     slot_ids = neighbor_table[:, :, 1].reshape(-1)
@@ -191,8 +189,8 @@
                 block = lax.ppermute(
                     block, "head", [(i, (i + step) % groups) for i in range(groups)]
                 )
-            owned.append(block)
-    weights = weights.reshape(peers // 2, groups, depth, width)
+            owned.append(block.reshape(-1, width))
+    weights = weights.reshape(-1, groups, depth, width)
     other = lax.ppermute(weights, "core", [(0, 1), (1, 0)])
     where = jnp.stack([head, lax.axis_index("core")])
     result = attend(where, owned, decoder_states, weights, other)

time: 302 us -> 336 us (1.11)
  the two profiles are of different devices: /device:TPU:1 before, /device:TPU:4 now
where the time goes in v5:
time: 336 us; the launch traced here: 335 us
  waiting for transfers between devices  121 us (36%)
  starting transfers between devices  73.6 us (22%)
  local copies, waits for them, and re-layouts  51.2 us (15%)
  blocking collectives  42.1 us (13%)
  Pallas kernels  32.5 us (10%)
  between operations  13.7 us (4%)
    all_to_all x4, waiting for transfers between devices, layer(): lax.all_to_all(pieces[CHUNKS * wanted + c], SPAN + ('head',), split_axis=...  61.4 us
    ppermute x12, waiting for transfers between devices, layer(): lax.ppermute(block, 'head', [(i, (i + step) % groups) for i in range(grou...  56.5 us
    all_to_all x4, starting transfers between devices, layer(): lax.all_to_all(pieces[CHUNKS * wanted + c], SPAN + ('head',), split_axis=...  33.1 us
    pallas_call x1, Pallas kernels, attend(): pl.pallas_call(attention_kernel, out_shape=jax.ShapeDtypeStruct((groups,...  32.5 us
    ppermute x12, starting transfers between devices, layer(): lax.ppermute(block, 'head', [(i, (i + step) % groups) for i in range(grou...  28.9 us
    gather x16, local copies, waits for them, and re-layouts, layer(): block = arrived[sources[(head + step) % groups]]  27.6 us
    all_to_all x1, blocking collectives, layer(): lax.all_to_all(result, 'head', split_axis=0, concat_axis=0, tiled=True)  27 us
    gather x4, local copies, waits for them, and re-layouts, layer(): pieces[CHUNKS * wanted + c]  15.3 us
  transfers between devices with their start and end apart: 21, of which 9 were waited for; matrix products, arithmetic and copies ran while one was open for 14% of the time, Pallas kernels for 0%

profile of v5, /device:TPU:4, one launch (start us, length us, event | category | flops | bytes accessed | tf_op | source)
XLA Modules:
  0.0 335.2 jit_solution(10803084207121001391)
XLA Ops:
  6.5 1.0 copy-done
  7.6 0.9 constant_dynamic-slice_fusion
  8.6 0.8 constant_dynamic-slice_fusion.1
  9.3 7.3 %collective-permute-start.13 = (bf16[32,1024]{1,0:T(8,128)(2,1)S(1)}, bf16[32,1024]{1,0:T(8,128)(2,1)S(1)}, u32[]{:S(2)}, u32[]{:S(2)}) collective-permute-start(bf16[32,1024]{1,0:T(8,128)(2,1)S(1)} %get-tuple-element.6), channel_id=1, source_target_pairs={{0,2},{1,3},{2,0},{3,1},{4,6},{5,7},{6,4},{7,5},{8,10},{9,11},{10,... | collective-permute-start | bytes 196616 | tf_op jit(solution)/shard_map/ppermute | solution.py:162
  16.6 1.5 collective-permute-start.12
  18.1 2.7 collective-permute-start.14
  20.8 2.3 collective-permute-done.12
  23.1 0.4 collective-permute-done.14
  23.5 1.3 gather_fusion.20
  24.8 0.8 fusion.15
  25.7 0.1 eq.34
  25.9 0.1 broadcast_in_dim.14
  26.0 0.1 select_reduce_fusion
  26.1 0.1 copy.34
  26.2 15.0 %all_to_all.34 = s32[64,1,1]{2,1,0:T(1,128)S(1)} all-to-all(s32[64,1,1]{2,1,0:T(1,128)S(1)} %copy.34), channel_id=1, replica_groups=mesh['y'=4,'x'=4,'z'=2,'core'=2,'head'=4] {'y','x','z','core'}, dimensions={0} | all-to-all | bytes 512 | tf_op jit(solution)/shard_map/all_to_all | solution.py:171
  41.2 1.2 multiply_reduce_fusion
  42.4 3.9 %gather_fusion.5 = bf16[64,8,1024]{2,1,0:T(8,128)(2,1)} fusion(bf16[256,8,1024]{2,1,0:T(8,128)(2,1)} %bitcast.108, s32[1024]{0:T(1024)S(1)} %pad_clamp_fusion.3), kind=kCustom, calls=%fused_computation.5 | custom fusion | bytes 2097408 | tf_op jit(solution)/shard_map/gather | solution.py:179
  46.3 8.2 %all-to-all-start.2 = ((bf16[64,8,1024]{2,1,0:T(8,128)(2,1)}), bf16[64,8,1024]{2,1,0:T(8,128)(2,1)S(1)}, u32[]{:S(2)}, u32[]{:S(2)}) async-start(bf16[64,8,1024]{2,1,0:T(8,128)(2,1)} %gather_fusion.5), calls=%async_computation.2 | async-start | bytes 2097152 | tf_op jit(solution)/shard_map/all_to_all | solution.py:178
  54.5 3.8 %gather_fusion.10 = bf16[64,8,1024]{2,1,0:T(8,128)(2,1)} fusion(bf16[256,8,1024]{2,1,0:T(8,128)(2,1)} %bitcast.109, s32[1024]{0:T(1024)S(1)} %pad_clamp_fusion.2), kind=kCustom, calls=%fused_computation.10 | custom fusion | bytes 2097408 | tf_op jit(solution)/shard_map/gather | solution.py:179
  58.3 12.7 %all-to-all-done.2 = bf16[64,8,1024]{2,1,0:T(8,128)(2,1)S(1)} async-done(((bf16[64,8,1024]{2,1,0:T(8,128)(2,1)}), bf16[64,8,1024]{2,1,0:T(8,128)(2,1)S(1)}, u32[]{:S(2)}, u32[]{:S(2)}) %all-to-all-start.2) | async-done | bytes 1048608 | tf_op jit(solution)/shard_map/all_to_all | solution.py:178
  71.1 7.6 %all-to-all-start.3 = ((bf16[64,8,1024]{2,1,0:T(8,128)(2,1)}), bf16[64,8,1024]{2,1,0:T(8,128)(2,1)S(1)}, u32[]{:S(2)}, u32[]{:S(2)}) async-start(bf16[64,8,1024]{2,1,0:T(8,128)(2,1)} %gather_fusion.10), calls=%async_computation.3 | async-start | bytes 2097152 | tf_op jit(solution)/shard_map/all_to_all | solution.py:178
  78.7 3.9 %gather_fusion = bf16[64,8,1024]{2,1,0:T(8,128)(2,1)} fusion(bf16[256,8,1024]{2,1,0:T(8,128)(2,1)} %bitcast.110, s32[1024]{0:T(1024)S(1)} %pad_clamp_fusion.8), kind=kCustom, calls=%fused_computation | custom fusion | bytes 2097408 | tf_op jit(solution)/shard_map/gather | solution.py:179
  82.6 14.2 %all-to-all-done.3 = bf16[64,8,1024]{2,1,0:T(8,128)(2,1)S(1)} async-done(((bf16[64,8,1024]{2,1,0:T(8,128)(2,1)}), bf16[64,8,1024]{2,1,0:T(8,128)(2,1)S(1)}, u32[]{:S(2)}, u32[]{:S(2)}) %all-to-all-start.3) | async-done | bytes 1048608 | tf_op jit(solution)/shard_map/all_to_all | solution.py:178
  96.8 7.7 %all-to-all-start.1 = ((bf16[64,8,1024]{2,1,0:T(8,128)(2,1)}), bf16[64,8,1024]{2,1,0:T(8,128)(2,1)}, u32[]{:S(2)}, u32[]{:S(2)}) async-start(bf16[64,8,1024]{2,1,0:T(8,128)(2,1)} %gather_fusion), calls=%async_computation.1 | async-start | bytes 2097152 | tf_op jit(solution)/shard_map/all_to_all | solution.py:178
  104.5 0.2 collective-permute-start.15
  104.7 3.8 %gather_fusion.15 = bf16[64,8,1024]{2,1,0:T(8,128)(2,1)} fusion(bf16[256,8,1024]{2,1,0:T(8,128)(2,1)} %bitcast.111, s32[1024]{0:T(1024)S(1)} %pad_clamp_fusion.1), kind=kCustom, calls=%fused_computation.15 | custom fusion | bytes 2097408 | tf_op jit(solution)/shard_map/gather | solution.py:179
  108.5 11.2 %all-to-all-done.1 = bf16[64,8,1024]{2,1,0:T(8,128)(2,1)} async-done(((bf16[64,8,1024]{2,1,0:T(8,128)(2,1)}), bf16[64,8,1024]{2,1,0:T(8,128)(2,1)}, u32[]{:S(2)}, u32[]{:S(2)}) %all-to-all-start.1) | async-done | bytes 1048608 | tf_op jit(solution)/shard_map/all_to_all | solution.py:178
  119.7 9.6 %all-to-all-start.4 = ((bf16[64,8,1024]{2,1,0:T(8,128)(2,1)}), bf16[64,8,1024]{2,1,0:T(8,128)(2,1)}, u32[]{:S(2)}, u32[]{:S(2)}) async-start(bf16[64,8,1024]{2,1,0:T(8,128)(2,1)} %gather_fusion.15), calls=%async_computation.4 | async-start | bytes 2097152 | tf_op jit(solution)/shard_map/all_to_all | solution.py:178
  129.6 1.3 gather_fusion.7
  130.8 1.3 gather_fusion.8
  132.1 4.6 %collective-permute-start.4 = (bf16[16,8,1024]{2,1,0:T(8,128)(2,1)}, bf16[16,8,1024]{2,1,0:T(8,128)(2,1)S(1)}, u32[]{:S(2)}, u32[]{:S(2)}) collective-permute-start(bf16[16,8,1024]{2,1,0:T(8,128)(2,1)} %gather_fusion.8), channel_id=1, source_target_pairs={{0,2},{1,3},{2,0},{3,1},{4,6},{5,7},{6,4},{7,5},{8,10},{9,11},{10,... | collective-permute-start | bytes 786440 | tf_op jit(solution)/shard_map/ppermute | solution.py:189
  136.7 1.3 gather_fusion.9
  137.9 1.7 collective-permute-start.5
  139.7 1.3 gather_fusion.12
  140.9 1.2 collective-permute-start.6
  142.1 0.6 gather_fusion.14
  142.7 1.3 gather_fusion.13
  144.0 1.8 gather_fusion.3
  145.8 1.8 gather_fusion.2
  147.6 2.7 collective-permute-start.7
  150.2 5.6 %collective-permute-start.8 = (bf16[16,8,1024]{2,1,0:T(8,128)(2,1)S(1)}, bf16[16,8,1024]{2,1,0:T(8,128)(2,1)S(1)}, u32[]{:S(2)}, u32[]{:S(2)}) collective-permute-start(bf16[16,8,1024]{2,1,0:T(8,128)(2,1)S(1)} %gather_fusion.14), channel_id=1, source_target_pairs={{0,3},{1,0},{2,1},{3,2},{4,7},{5,4},{6,5},{7,6},{8,11},{9,8},{10,9... | collective-permute-start | bytes 786440 | tf_op jit(solution)/shard_map/ppermute | solution.py:189
  155.9 8.4 %collective-permute-done.5 = bf16[16,8,1024]{2,1,0:T(8,128)(2,1)S(1)} collective-permute-done((bf16[16,8,1024]{2,1,0:T(8,128)(2,1)}, bf16[16,8,1024]{2,1,0:T(8,128)(2,1)S(1)}, u32[]{:S(2)}, u32[]{:S(2)}) %collective-permute-start.5) | collective-permute-done | bytes 262176 | tf_op jit(solution)/shard_map/ppermute | solution.py:189
  164.3 2.7 collective-permute-start
  167.0 3.7 %collective-permute-start.1 = (bf16[16,8,1024]{2,1,0:T(8,128)(2,1)S(1)}, bf16[16,8,1024]{2,1,0:T(8,128)(2,1)S(1)}, u32[]{:S(2)}, u32[]{:S(2)}) collective-permute-start(bf16[16,8,1024]{2,1,0:T(8,128)(2,1)S(1)} %gather_fusion.3), channel_id=1, source_target_pairs={{0,2},{1,3},{2,0},{3,1},{4,6},{5,7},{6,4},{7,5},{8,10},{9,11},{10,... | collective-permute-start | bytes 786440 | tf_op jit(solution)/shard_map/ppermute | solution.py:189
  170.8 2.5 gather_fusion.4
  173.2 23.2 %all-to-all-done.4 = bf16[64,8,1024]{2,1,0:T(8,128)(2,1)} async-done(((bf16[64,8,1024]{2,1,0:T(8,128)(2,1)}), bf16[64,8,1024]{2,1,0:T(8,128)(2,1)}, u32[]{:S(2)}, u32[]{:S(2)}) %all-to-all-start.4) | async-done | bytes 1048608 | tf_op jit(solution)/shard_map/all_to_all | solution.py:178
  196.4 2.5 gather_fusion.19
  198.9 2.5 gather_fusion.18
  201.4 2.5 gather_fusion.17
  203.9 1.1 collective-permute-start.2
  205.0 1.8 collective-permute-start.9
  206.9 2.3 collective-permute-start.10
  209.1 0.7 copy-done.1
  209.8 1.4 collective-permute-start.11
  211.3 1.8 gather_fusion.6
  213.1 1.8 gather_fusion.11
  214.9 1.8 gather_fusion.1
  216.7 1.8 gather_fusion.16
  218.5 42.5 %collective-permute-done.2 = bf16[16,8,1024]{2,1,0:T(8,128)(2,1)} collective-permute-done((bf16[16,8,1024]{2,1,0:T(8,128)(2,1)}, bf16[16,8,1024]{2,1,0:T(8,128)(2,1)}, u32[]{:S(2)}, u32[]{:S(2)}) %collective-permute-start.2) | collective-permute-done | bytes 262176 | tf_op jit(solution)/shard_map/ppermute | solution.py:189
  261.0 5.6 %collective-permute-done.11 = bf16[16,8,1024]{2,1,0:T(8,128)(2,1)} collective-permute-done((bf16[16,8,1024]{2,1,0:T(8,128)(2,1)}, bf16[16,8,1024]{2,1,0:T(8,128)(2,1)}, u32[]{:S(2)}, u32[]{:S(2)}) %collective-permute-start.11) | collective-permute-done | bytes 262176 | tf_op jit(solution)/shard_map/ppermute | solution.py:189
  266.6 0.9 copy-done.2
  267.6 32.5 %attend.1 = bf16[4,512,256]{2,1,0:T(8,128)(2,1)S(1)} custom-call(s32[2]{0:T(128)S(1)} %pad_add_fusion.where_ref, bf16[128,1024]{1,0:T(8,128)(2,1)S(1)} %bitcast.98, bf16[128,1024]{1,0:T(8,128)(2,1)S(1)} %bitcast.106, bf16[128,1024]{1,0:T(8,128)(2,1)S(1)} %bitcast.107, bf16[128,1024]{1,0:T(8,128)(2,1)} %bitcast.16.refs_3_, bf16[128,1024]{1,0:T(8,128)(2,1)S(1)} %bitcast.96, ...), custom_call_target="tpu_custom_call" | custom-call | flops 10737418240 | bytes 12582912 | tf_op jit(solution)/shard_map/attend/pallas_call | solution.py:101
  300.1 27.0 %all_to_all.35 = bf16[4,512,256]{2,1,0:T(8,128)(2,1)S(1)} all-to-all(bf16[4,512,256]{2,1,0:T(8,128)(2,1)S(1)} %attend.1), channel_id=1, replica_groups=mesh['y'=4,'x'=4,'z'=2,'core'=2,'head'=4] {'head'}, dimensions={0} | all-to-all | bytes 2097152 | tf_op jit(solution)/shard_map/all_to_all | solution.py:197
  327.2 1.2 concatenate.7
  (43 shorter events, 0.7 us)
Async XLA Ops:
  6.5 1.0 copy-start
  6.5 97.9 %all-gather.3.cloned.1.call-start = ((), (), s32[]{:S(2)}) async-start(), calls=%async_computation.6 | async-start | bytes 4456448 | tf_op jit(solution)/shard_map/all_gather | solution.py:172
  9.3 11.4 %collective-permute-start.13 = (bf16[32,1024]{1,0:T(8,128)(2,1)S(1)}, bf16[32,1024]{1,0:T(8,128)(2,1)S(1)}, u32[]{:S(2)}, u32[]{:S(2)}) collective-permute-start(bf16[32,1024]{1,0:T(8,128)(2,1)S(1)} %get-tuple-element.6), channel_id=1, source_target_pairs={{0,2},{1,3},{2,0},{3,1},{4,6},{5,7},{6,4},{7,5},{8,10},{9,11},{10,... | collective-permute-start | bytes 196616 | tf_op jit(solution)/shard_map/ppermute | solution.py:162
  16.6 6.4 %collective-permute-start.12 = (bf16[32,1024]{1,0:T(8,128)(2,1)S(1)}, bf16[32,1024]{1,0:T(8,128)(2,1)S(1)}, u32[]{:S(2)}, u32[]{:S(2)}) collective-permute-start(bf16[32,1024]{1,0:T(8,128)(2,1)S(1)} %get-tuple-element.6), channel_id=1, source_target_pairs={{0,1},{1,2},{2,3},{3,0},{4,5},{5,6},{6,7},{7,4},{8,9},{9,10},{10,1... | collective-permute-start | bytes 196616 | tf_op jit(solution)/shard_map/ppermute | solution.py:162
  18.1 5.4 %collective-permute-start.14 = (bf16[32,1024]{1,0:T(8,128)(2,1)S(1)}, bf16[32,1024]{1,0:T(8,128)(2,1)S(1)}, u32[]{:S(2)}, u32[]{:S(2)}) collective-permute-start(bf16[32,1024]{1,0:T(8,128)(2,1)S(1)} %get-tuple-element.6), channel_id=1, source_target_pairs={{0,3},{1,0},{2,1},{3,2},{4,7},{5,4},{6,5},{7,6},{8,11},{9,8},{10,9... | collective-permute-start | bytes 196616 | tf_op jit(solution)/shard_map/ppermute | solution.py:162
  46.3 24.8 %all-to-all-start.2 = ((bf16[64,8,1024]{2,1,0:T(8,128)(2,1)}), bf16[64,8,1024]{2,1,0:T(8,128)(2,1)S(1)}, u32[]{:S(2)}, u32[]{:S(2)}) async-start(bf16[64,8,1024]{2,1,0:T(8,128)(2,1)} %gather_fusion.5), calls=%async_computation.2 | async-start | bytes 2097152 | tf_op jit(solution)/shard_map/all_to_all | solution.py:178
  71.1 65.6 %copy-start.3 = (bf16[64,8,1024]{2,1,0:T(8,128)(2,1)}, bf16[64,8,1024]{2,1,0:T(8,128)(2,1)S(1)}, u32[]{:S(2)}) copy-start(bf16[64,8,1024]{2,1,0:T(8,128)(2,1)S(1)} %all-to-all-done.2) | copy-start | bytes 3145732
  71.1 25.7 %all-to-all-start.3 = ((bf16[64,8,1024]{2,1,0:T(8,128)(2,1)}), bf16[64,8,1024]{2,1,0:T(8,128)(2,1)S(1)}, u32[]{:S(2)}, u32[]{:S(2)}) async-start(bf16[64,8,1024]{2,1,0:T(8,128)(2,1)} %gather_fusion.10), calls=%async_computation.3 | async-start | bytes 2097152 | tf_op jit(solution)/shard_map/all_to_all | solution.py:178
  96.8 45.9 %copy-start.4 = (bf16[64,8,1024]{2,1,0:T(8,128)(2,1)}, bf16[64,8,1024]{2,1,0:T(8,128)(2,1)S(1)}, u32[]{:S(2)}) copy-start(bf16[64,8,1024]{2,1,0:T(8,128)(2,1)S(1)} %all-to-all-done.3) | copy-start | bytes 3145732
  96.8 22.9 %all-to-all-start.1 = ((bf16[64,8,1024]{2,1,0:T(8,128)(2,1)}), bf16[64,8,1024]{2,1,0:T(8,128)(2,1)}, u32[]{:S(2)}, u32[]{:S(2)}) async-start(bf16[64,8,1024]{2,1,0:T(8,128)(2,1)} %gather_fusion), calls=%async_computation.1 | async-start | bytes 2097152 | tf_op jit(solution)/shard_map/all_to_all | solution.py:178
  104.5 162.1 %collective-permute-start.15 = (bf16[16,4,32,1024]{3,2,1,0:T(8,128)(2,1)}, bf16[16,4,32,1024]{3,2,1,0:T(8,128)(2,1)}, u32[]{:S(2)}, u32[]{:S(2)}) collective-permute-start(bf16[16,4,32,1024]{3,2,1,0:T(8,128)(2,1)} %bitcast.118), channel_id=1, source_target_pairs={{0,4},{4,0},{1,5},{5,1},{2,6},{6,2},{3,7},{7,3},{8,12},{12,8},{9,1... | collective-permute-start | bytes 12582920 | tf_op jit(solution)/shard_map/ppermute | solution.py:194
  119.7 76.7 %all-to-all-start.4 = ((bf16[64,8,1024]{2,1,0:T(8,128)(2,1)}), bf16[64,8,1024]{2,1,0:T(8,128)(2,1)}, u32[]{:S(2)}, u32[]{:S(2)}) async-start(bf16[64,8,1024]{2,1,0:T(8,128)(2,1)} %gather_fusion.15), calls=%async_computation.4 | async-start | bytes 2097152 | tf_op jit(solution)/shard_map/all_to_all | solution.py:178
  130.8 16.8 %collective-permute-start.3 = (bf16[16,8,1024]{2,1,0:T(8,128)(2,1)}, bf16[16,8,1024]{2,1,0:T(8,128)(2,1)S(1)}, u32[]{:S(2)}, u32[]{:S(2)}) collective-permute-start(bf16[16,8,1024]{2,1,0:T(8,128)(2,1)} %gather_fusion.7), channel_id=1, source_target_pairs={{0,1},{1,2},{2,3},{3,0},{4,5},{5,6},{6,7},{7,4},{8,9},{9,10},{10,1... | collective-permute-start | bytes 786440 | tf_op jit(solution)/shard_map/ppermute | solution.py:189
  132.1 18.1 %collective-permute-start.4 = (bf16[16,8,1024]{2,1,0:T(8,128)(2,1)}, bf16[16,8,1024]{2,1,0:T(8,128)(2,1)S(1)}, u32[]{:S(2)}, u32[]{:S(2)}) collective-permute-start(bf16[16,8,1024]{2,1,0:T(8,128)(2,1)} %gather_fusion.8), channel_id=1, source_target_pairs={{0,2},{1,3},{2,0},{3,1},{4,6},{5,7},{6,4},{7,5},{8,10},{9,11},{10,... | collective-permute-start | bytes 786440 | tf_op jit(solution)/shard_map/ppermute | solution.py:189
  137.9 26.3 %collective-permute-start.5 = (bf16[16,8,1024]{2,1,0:T(8,128)(2,1)}, bf16[16,8,1024]{2,1,0:T(8,128)(2,1)S(1)}, u32[]{:S(2)}, u32[]{:S(2)}) collective-permute-start(bf16[16,8,1024]{2,1,0:T(8,128)(2,1)} %gather_fusion.9), channel_id=1, source_target_pairs={{0,3},{1,0},{2,1},{3,2},{4,7},{5,4},{6,5},{7,6},{8,11},{9,8},{10,9... | collective-permute-start | bytes 786440 | tf_op jit(solution)/shard_map/ppermute | solution.py:189
  140.9 26.1 %collective-permute-start.6 = (bf16[16,8,1024]{2,1,0:T(8,128)(2,1)}, bf16[16,8,1024]{2,1,0:T(8,128)(2,1)S(1)}, u32[]{:S(2)}, u32[]{:S(2)}) collective-permute-start(bf16[16,8,1024]{2,1,0:T(8,128)(2,1)} %gather_fusion.12), channel_id=1, source_target_pairs={{0,1},{1,2},{2,3},{3,0},{4,5},{5,6},{6,7},{7,4},{8,9},{9,10},{10,1... | collective-permute-start | bytes 786440 | tf_op jit(solution)/shard_map/ppermute | solution.py:189
  147.6 56.3 %collective-permute-start.7 = (bf16[16,8,1024]{2,1,0:T(8,128)(2,1)}, bf16[16,8,1024]{2,1,0:T(8,128)(2,1)S(1)}, u32[]{:S(2)}, u32[]{:S(2)}) collective-permute-start(bf16[16,8,1024]{2,1,0:T(8,128)(2,1)} %gather_fusion.13), channel_id=1, source_target_pairs={{0,2},{1,3},{2,0},{3,1},{4,6},{5,7},{6,4},{7,5},{8,10},{9,11},{10,... | collective-permute-start | bytes 786440 | tf_op jit(solution)/shard_map/ppermute | solution.py:189
  150.2 54.8 %collective-permute-start.8 = (bf16[16,8,1024]{2,1,0:T(8,128)(2,1)S(1)}, bf16[16,8,1024]{2,1,0:T(8,128)(2,1)S(1)}, u32[]{:S(2)}, u32[]{:S(2)}) collective-permute-start(bf16[16,8,1024]{2,1,0:T(8,128)(2,1)S(1)} %gather_fusion.14), channel_id=1, source_target_pairs={{0,3},{1,0},{2,1},{3,2},{4,7},{5,4},{6,5},{7,6},{8,11},{9,8},{10,9... | collective-permute-start | bytes 786440 | tf_op jit(solution)/shard_map/ppermute | solution.py:189
  164.3 42.6 %collective-permute-start = (bf16[16,8,1024]{2,1,0:T(8,128)(2,1)S(1)}, bf16[16,8,1024]{2,1,0:T(8,128)(2,1)S(1)}, u32[]{:S(2)}, u32[]{:S(2)}) collective-permute-start(bf16[16,8,1024]{2,1,0:T(8,128)(2,1)S(1)} %gather_fusion.2), channel_id=1, source_target_pairs={{0,1},{1,2},{2,3},{3,0},{4,5},{5,6},{6,7},{7,4},{8,9},{9,10},{10,1... | collective-permute-start | bytes 786440 | tf_op jit(solution)/shard_map/ppermute | solution.py:189
  167.0 42.1 %collective-permute-start.1 = (bf16[16,8,1024]{2,1,0:T(8,128)(2,1)S(1)}, bf16[16,8,1024]{2,1,0:T(8,128)(2,1)S(1)}, u32[]{:S(2)}, u32[]{:S(2)}) collective-permute-start(bf16[16,8,1024]{2,1,0:T(8,128)(2,1)S(1)} %gather_fusion.3), channel_id=1, source_target_pairs={{0,2},{1,3},{2,0},{3,1},{4,6},{5,7},{6,4},{7,5},{8,10},{9,11},{10,... | collective-permute-start | bytes 786440 | tf_op jit(solution)/shard_map/ppermute | solution.py:189
  203.9 57.1 %collective-permute-start.2 = (bf16[16,8,1024]{2,1,0:T(8,128)(2,1)}, bf16[16,8,1024]{2,1,0:T(8,128)(2,1)}, u32[]{:S(2)}, u32[]{:S(2)}) collective-permute-start(bf16[16,8,1024]{2,1,0:T(8,128)(2,1)} %gather_fusion.4), channel_id=1, source_target_pairs={{0,3},{1,0},{2,1},{3,2},{4,7},{5,4},{6,5},{7,6},{8,11},{9,8},{10,9... | collective-permute-start | bytes 786440 | tf_op jit(solution)/shard_map/ppermute | solution.py:189
  205.0 56.0 %collective-permute-start.9 = (bf16[16,8,1024]{2,1,0:T(8,128)(2,1)}, bf16[16,8,1024]{2,1,0:T(8,128)(2,1)}, u32[]{:S(2)}, u32[]{:S(2)}) collective-permute-start(bf16[16,8,1024]{2,1,0:T(8,128)(2,1)} %gather_fusion.17), channel_id=1, source_target_pairs={{0,1},{1,2},{2,3},{3,0},{4,5},{5,6},{6,7},{7,4},{8,9},{9,10},{10,1... | collective-permute-start | bytes 786440 | tf_op jit(solution)/shard_map/ppermute | solution.py:189
  206.9 54.2 %collective-permute-start.10 = (bf16[16,8,1024]{2,1,0:T(8,128)(2,1)}, bf16[16,8,1024]{2,1,0:T(8,128)(2,1)}, u32[]{:S(2)}, u32[]{:S(2)}) collective-permute-start(bf16[16,8,1024]{2,1,0:T(8,128)(2,1)} %gather_fusion.18), channel_id=1, source_target_pairs={{0,2},{1,3},{2,0},{3,1},{4,6},{5,7},{6,4},{7,5},{8,10},{9,11},{10,... | collective-permute-start | bytes 786440 | tf_op jit(solution)/shard_map/ppermute | solution.py:189
  209.1 0.7 copy-start.1
  209.8 56.8 %collective-permute-start.11 = (bf16[16,8,1024]{2,1,0:T(8,128)(2,1)}, bf16[16,8,1024]{2,1,0:T(8,128)(2,1)}, u32[]{:S(2)}, u32[]{:S(2)}) collective-permute-start(bf16[16,8,1024]{2,1,0:T(8,128)(2,1)} %gather_fusion.19), channel_id=1, source_target_pairs={{0,3},{1,0},{2,1},{3,2},{4,7},{5,4},{6,5},{7,6},{8,11},{9,8},{10,9... | collective-permute-start | bytes 786440 | tf_op jit(solution)/shard_map/ppermute | solution.py:189
  266.6 1.0 copy-start.2
Sparse Core Ops, SparseCore 0:
  24.9 73.1 all-gather.2

commit v6 on v5

--- a/solution.py
+++ b/solution.py
@@ -9,7 +9,7 @@
 HEAD_DIM = 64
 SPAN_LEN = 64
 SPANS_STEP = 2
-CHUNKS = 4
+CHUNKS = 2
 SPAN = ("y", "x", "z", "core")
 
 
@@ -131,18 +131,9 @@
     )(where, *chunks, states, states, weights, other)
 
 
-def span_groups(peers, groups, turn):
-    low = [(s // 2) % 2 == 0 for s in range(peers)]
-    return [
-        [s * groups + (h + (turn if low[s] else 0)) % groups for s in range(peers)]
-        for h in range(groups)
-    ]
-
-
 def layer(
     decoder_states, encodings, neighbor_table, query_weight, key_weight, value_weight, out_weight
 ):
-    peers = lax.axis_size(SPAN)
     groups = lax.axis_size("head")
     share = lax.axis_index(("core", "y", "x"))
     head = lax.axis_index("head")
@@ -177,10 +168,9 @@
     for c in range(CHUNKS):
         arrived = lax.all_to_all(
             pieces[CHUNKS * wanted + c],
-            SPAN + ("head",),
+            SPAN,
             split_axis=0,
             concat_axis=0,
-            axis_index_groups=span_groups(peers, groups, c % 2),
             tiled=True,
         )
         for step in range(groups):

time: 336 us -> 280 us (0.83)
  the two profiles are of different devices: /device:TPU:4 before, /device:TPU:2 now
where the time goes in v6:
time: 280 us; the launch traced here: 279 us
  waiting for transfers between devices  106 us (38%)
  starting transfers between devices  46.1 us (16%)
  blocking collectives  45.1 us (16%)
  local copies, waits for them, and re-layouts  34.2 us (12%)
  Pallas kernels  32.6 us (12%)
  between operations  13.5 us (5%)
    all_to_all x2, waiting for transfers between devices, layer(): lax.all_to_all(pieces[CHUNKS * wanted + c], SPAN, split_axis=0, concat_ax...  52.3 us
    ppermute x6, waiting for transfers between devices, layer(): lax.ppermute(block, 'head', [(i, (i + step) % groups) for i in range(grou...  49.1 us
    pallas_call x1, Pallas kernels, attend(): pl.pallas_call(attention_kernel, out_shape=jax.ShapeDtypeStruct((groups,...  32.6 us
    all_to_all x1, blocking collectives, layer(): lax.all_to_all(result, 'head', split_axis=0, concat_axis=0, tiled=True)  29.1 us
    ppermute x6, starting transfers between devices, layer(): lax.ppermute(block, 'head', [(i, (i + step) % groups) for i in range(grou...  19.5 us
    gather x8, local copies, waits for them, and re-layouts, layer(): block = arrived[sources[(head + step) % groups]]  19 us
    all_to_all x1, blocking collectives, layer(): lax.all_to_all(request, SPAN, split_axis=0, concat_axis=0, tiled=True)  16 us
    all_to_all x2, starting transfers between devices, layer(): lax.all_to_all(pieces[CHUNKS * wanted + c], SPAN, split_axis=0, concat_ax...  15.2 us
  transfers between devices with their start and end apart: 13, of which 9 were waited for; matrix products, arithmetic and copies ran while one was open for 11% of the time, Pallas kernels for 0%

profile of v6, /device:TPU:2, one launch (start us, length us, event | category | flops | bytes accessed | tf_op | source)
XLA Modules:
  0.0 279.4 jit_solution(15019273246463659924)
XLA Ops:
  6.5 0.0 copy-start
  6.5 0.0 all-gather.3.cloned.1.call-start
  6.5 1.0 copy-done
  7.6 0.9 constant_dynamic-slice_fusion
  8.5 0.1 copy.37
  8.6 0.8 constant_dynamic-slice_fusion.1
  9.3 7.3 %collective-permute-start.7 = (bf16[32,1024]{1,0:T(8,128)(2,1)S(1)}, bf16[32,1024]{1,0:T(8,128)(2,1)S(1)}, u32[]{:S(2)}, u32[]{:S(2)}) collective-permute-start(bf16[32,1024]{1,0:T(8,128)(2,1)S(1)} %get-tuple-element.6), channel_id=1, source_target_pairs={{0,2},{1,3},{2,0},{3,1},{4,6},{5,7},{6,4},{7,5},{8,10},{9,11},{10,... | collective-permute-start | bytes 196616 | tf_op jit(solution)/shard_map/ppermute | solution.py:153
  16.6 1.5 collective-permute-start.6
  18.1 2.7 collective-permute-start.8
  20.8 0.0 collective-permute-done.7
  20.8 2.3 collective-permute-done.6
  23.1 0.4 collective-permute-done.8
  23.5 1.3 gather_fusion.10
  24.8 0.0 all-gather.3.cloned.1.call-update
  24.8 0.8 fusion.13
  25.6 0.1 copy.32
  25.7 0.1 eq.26
  25.8 0.1 copy.33
  25.8 0.1 broadcast_in_dim.14
  26.0 0.1 select_reduce_fusion
  26.1 0.1 copy.34
  26.2 16.0 %all_to_all.24 = s32[64,1,1]{2,1,0:T(1,128)S(1)} all-to-all(s32[64,1,1]{2,1,0:T(1,128)S(1)} %copy.34), channel_id=1, replica_groups=mesh['y'=4,'x'=4,'z'=2,'core'=2,'head'=4] {'y','x','z','core'}, dimensions={0} | all-to-all | bytes 512 | tf_op jit(solution)/shard_map/all_to_all | solution.py:162
  42.1 1.2 multiply_reduce_fusion
  43.4 4.3 %gather_fusion = bf16[64,16,1024]{2,1,0:T(8,128)(2,1)} fusion(bf16[128,16,1024]{2,1,0:T(8,128)(2,1)} %bitcast.77, s32[1024]{0:T(1024)S(1)} %pad_clamp_fusion.6), kind=kCustom, calls=%fused_computation | custom fusion | bytes 4194560 | tf_op jit(solution)/shard_map/gather | solution.py:170
  47.7 5.6 %all-to-all-start.1 = ((bf16[64,16,1024]{2,1,0:T(8,128)(2,1)}), bf16[64,16,1024]{2,1,0:T(8,128)(2,1)S(1)}, u32[]{:S(2)}, u32[]{:S(2)}) async-start(bf16[64,16,1024]{2,1,0:T(8,128)(2,1)} %gather_fusion), calls=%async_computation.1 | async-start | bytes 4194304 | tf_op jit(solution)/shard_map/all_to_all | solution.py:169
  53.2 4.2 %gather_fusion.5 = bf16[64,16,1024]{2,1,0:T(8,128)(2,1)} fusion(bf16[128,16,1024]{2,1,0:T(8,128)(2,1)} %bitcast.78, s32[1024]{0:T(1024)S(1)} %pad_clamp_fusion.1), kind=kCustom, calls=%fused_computation.5 | custom fusion | bytes 4194560 | tf_op jit(solution)/shard_map/gather | solution.py:170
  57.4 27.7 %all-to-all-done.1 = bf16[64,16,1024]{2,1,0:T(8,128)(2,1)S(1)} async-done(((bf16[64,16,1024]{2,1,0:T(8,128)(2,1)}), bf16[64,16,1024]{2,1,0:T(8,128)(2,1)S(1)}, u32[]{:S(2)}, u32[]{:S(2)}) %all-to-all-start.1) | async-done | bytes 2097184 | tf_op jit(solution)/shard_map/all_to_all | solution.py:169
  85.1 0.0 copy-start.1
  85.1 9.7 %all-to-all-start.2 = ((bf16[64,16,1024]{2,1,0:T(8,128)(2,1)}), bf16[64,16,1024]{2,1,0:T(8,128)(2,1)}, u32[]{:S(2)}, u32[]{:S(2)}) async-start(bf16[64,16,1024]{2,1,0:T(8,128)(2,1)} %gather_fusion.5), calls=%async_computation.2 | async-start | bytes 4194304 | tf_op jit(solution)/shard_map/all_to_all | solution.py:169
  94.8 2.3 all-gather.3.cloned.1.call-done
  97.0 0.0 collective-permute-start.9
  97.0 0.1 reshape_reshape_squeeze.3
  97.2 1.4 gather_fusion.2
  98.5 1.3 collective-permute-start
  99.8 0.0 copy-done.1
  99.8 1.4 gather_fusion.3
  101.2 4.5 %collective-permute-start.1 = (bf16[16,16,1024]{2,1,0:T(8,128)(2,1)}, bf16[16,16,1024]{2,1,0:T(8,128)(2,1)S(1)}, u32[]{:S(2)}, u32[]{:S(2)}) collective-permute-start(bf16[16,16,1024]{2,1,0:T(8,128)(2,1)} %gather_fusion.3), channel_id=1, source_target_pairs={{0,2},{1,3},{2,0},{3,1},{4,6},{5,7},{6,4},{7,5},{8,10},{9,11},{10,... | collective-permute-start | bytes 1572872 | tf_op jit(solution)/shard_map/ppermute | solution.py:179
  105.7 3.0 %gather_fusion.4 = bf16[16,16,1024]{2,1,0:T(8,128)(2,1)} fusion(bf16[64,16,1024]{2,1,0:T(8,128)(2,1)} %copy-done.1, s32[1024]{0:T(1024)S(1)} %pad_clamp_fusion.2), kind=kCustom, calls=%fused_computation.4 | custom fusion | bytes 1048640 | tf_op jit(solution)/shard_map/gather | solution.py:177
  108.7 1.3 collective-permute-start.2
  110.0 24.6 %all-to-all-done.2 = bf16[64,16,1024]{2,1,0:T(8,128)(2,1)} async-done(((bf16[64,16,1024]{2,1,0:T(8,128)(2,1)}), bf16[64,16,1024]{2,1,0:T(8,128)(2,1)}, u32[]{:S(2)}, u32[]{:S(2)}) %all-to-all-start.2) | async-done | bytes 2097184 | tf_op jit(solution)/shard_map/all_to_all | solution.py:169
  134.6 3.0 %gather_fusion.7 = bf16[16,16,1024]{2,1,0:T(8,128)(2,1)} fusion(bf16[64,16,1024]{2,1,0:T(8,128)(2,1)} %all-to-all-done.2, s32[1024]{0:T(1024)S(1)} %pad_clamp_fusion.4), kind=kCustom, calls=%fused_computation.7 | custom fusion | bytes 1048640 | tf_op jit(solution)/shard_map/gather | solution.py:177
  137.6 0.6 collective-permute-start.3
  138.2 3.0 %gather_fusion.9 = bf16[16,16,1024]{2,1,0:T(8,128)(2,1)} fusion(bf16[64,16,1024]{2,1,0:T(8,128)(2,1)} %all-to-all-done.2, s32[1024]{0:T(1024)S(1)} %pad_clamp_fusion.2), kind=kCustom, calls=%fused_computation.9 | custom fusion | bytes 1048640 | tf_op jit(solution)/shard_map/gather | solution.py:177
  141.2 3.0 %gather_fusion.8 = bf16[16,16,1024]{2,1,0:T(8,128)(2,1)} fusion(bf16[64,16,1024]{2,1,0:T(8,128)(2,1)} %all-to-all-done.2, s32[1024]{0:T(1024)S(1)} %pad_clamp_fusion.3), kind=kCustom, calls=%fused_computation.8 | custom fusion | bytes 1048640 | tf_op jit(solution)/shard_map/gather | solution.py:177
  144.2 11.3 %collective-permute-done = bf16[16,16,1024]{2,1,0:T(8,128)(2,1)S(1)} collective-permute-done((bf16[16,16,1024]{2,1,0:T(8,128)(2,1)}, bf16[16,16,1024]{2,1,0:T(8,128)(2,1)S(1)}, u32[]{:S(2)}, u32[]{:S(2)}) %collective-permute-start) | collective-permute-done | bytes 524320 | tf_op jit(solution)/shard_map/ppermute | solution.py:179
  155.5 0.0 collective-permute-start.4
  155.6 0.9 collective-permute-done.1
  156.4 11.7 %collective-permute-start.5 = (bf16[16,16,1024]{2,1,0:T(8,128)(2,1)}, bf16[16,16,1024]{2,1,0:T(8,128)(2,1)}, u32[]{:S(2)}, u32[]{:S(2)}) collective-permute-start(bf16[16,16,1024]{2,1,0:T(8,128)(2,1)} %gather_fusion.9), channel_id=1, source_target_pairs={{0,3},{1,0},{2,1},{3,2},{4,7},{5,4},{6,5},{7,6},{8,11},{9,8},{10,9... | collective-permute-start | bytes 1572872 | tf_op jit(solution)/shard_map/ppermute | solution.py:179
  168.2 0.1 pad_add_fusion.where_ref
  168.2 2.2 gather_fusion.1
  170.4 2.2 gather_fusion.6
  172.6 0.0 collective-permute-done.2
  172.6 28.2 %collective-permute-done.3 = bf16[16,16,1024]{2,1,0:T(8,128)(2,1)} collective-permute-done((bf16[16,16,1024]{2,1,0:T(8,128)(2,1)}, bf16[16,16,1024]{2,1,0:T(8,128)(2,1)}, u32[]{:S(2)}, u32[]{:S(2)}) %collective-permute-start.3) | collective-permute-done | bytes 524320 | tf_op jit(solution)/shard_map/ppermute | solution.py:179
  200.8 0.0 collective-permute-done.4
  200.8 8.8 %collective-permute-done.5 = bf16[16,16,1024]{2,1,0:T(8,128)(2,1)} collective-permute-done((bf16[16,16,1024]{2,1,0:T(8,128)(2,1)}, bf16[16,16,1024]{2,1,0:T(8,128)(2,1)}, u32[]{:S(2)}, u32[]{:S(2)}) %collective-permute-start.5) | collective-permute-done | bytes 524320 | tf_op jit(solution)/shard_map/ppermute | solution.py:179
  209.5 0.0 collective-permute-done.9.refs_11_
  209.5 32.6 %attend.1 = bf16[4,512,256]{2,1,0:T(8,128)(2,1)S(1)} custom-call(s32[2]{0:T(128)S(1)} %pad_add_fusion.where_ref, bf16[256,1024]{1,0:T(8,128)(2,1)S(1)} %bitcast.72, bf16[256,1024]{1,0:T(8,128)(2,1)S(1)} %bitcast.74, bf16[256,1024]{1,0:T(8,128)(2,1)S(1)} %bitcast.75, bf16[256,1024]{1,0:T(8,128)(2,1)S(1)} %bitcast.76, bf16[256,1024]{1,0:T(8,128)(2,1)S(1)} %bitcast.73, ...), custom_call_target="tpu_custom_call" | custom-call | flops 10737418240 | bytes 12582912 | tf_op jit(solution)/shard_map/attend/pallas_call | solution.py:101
  242.1 29.1 %all_to_all.25 = bf16[4,512,256]{2,1,0:T(8,128)(2,1)S(1)} all-to-all(bf16[4,512,256]{2,1,0:T(8,128)(2,1)S(1)} %attend.1), channel_id=1, replica_groups=mesh['y'=4,'x'=4,'z'=2,'core'=2,'head'=4] {'head'}, dimensions={0} | all-to-all | bytes 2097152 | tf_op jit(solution)/shard_map/all_to_all | solution.py:187
  271.3 0.1 slice.34
  271.3 1.2 concatenate.7
  (13 shorter events, 0.1 us)
Async XLA Ops:
  6.5 1.0 copy-start
  6.5 90.5 %all-gather.3.cloned.1.call-start = ((), (), s32[]{:S(2)}) async-start(), calls=%async_computation.4 | async-start | bytes 4456448 | tf_op jit(solution)/shard_map/all_gather | solution.py:163
  9.3 11.4 %collective-permute-start.7 = (bf16[32,1024]{1,0:T(8,128)(2,1)S(1)}, bf16[32,1024]{1,0:T(8,128)(2,1)S(1)}, u32[]{:S(2)}, u32[]{:S(2)}) collective-permute-start(bf16[32,1024]{1,0:T(8,128)(2,1)S(1)} %get-tuple-element.6), channel_id=1, source_target_pairs={{0,2},{1,3},{2,0},{3,1},{4,6},{5,7},{6,4},{7,5},{8,10},{9,11},{10,... | collective-permute-start | bytes 196616 | tf_op jit(solution)/shard_map/ppermute | solution.py:153
  16.6 6.4 %collective-permute-start.6 = (bf16[32,1024]{1,0:T(8,128)(2,1)S(1)}, bf16[32,1024]{1,0:T(8,128)(2,1)S(1)}, u32[]{:S(2)}, u32[]{:S(2)}) collective-permute-start(bf16[32,1024]{1,0:T(8,128)(2,1)S(1)} %get-tuple-element.6), channel_id=1, source_target_pairs={{0,1},{1,2},{2,3},{3,0},{4,5},{5,6},{6,7},{7,4},{8,9},{9,10},{10,1... | collective-permute-start | bytes 196616 | tf_op jit(solution)/shard_map/ppermute | solution.py:153
  18.1 5.4 %collective-permute-start.8 = (bf16[32,1024]{1,0:T(8,128)(2,1)S(1)}, bf16[32,1024]{1,0:T(8,128)(2,1)S(1)}, u32[]{:S(2)}, u32[]{:S(2)}) collective-permute-start(bf16[32,1024]{1,0:T(8,128)(2,1)S(1)} %get-tuple-element.6), channel_id=1, source_target_pairs={{0,3},{1,0},{2,1},{3,2},{4,7},{5,4},{6,5},{7,6},{8,11},{9,8},{10,9... | collective-permute-start | bytes 196616 | tf_op jit(solution)/shard_map/ppermute | solution.py:153
  47.7 37.4 %all-to-all-start.1 = ((bf16[64,16,1024]{2,1,0:T(8,128)(2,1)}), bf16[64,16,1024]{2,1,0:T(8,128)(2,1)S(1)}, u32[]{:S(2)}, u32[]{:S(2)}) async-start(bf16[64,16,1024]{2,1,0:T(8,128)(2,1)} %gather_fusion), calls=%async_computation.1 | async-start | bytes 4194304 | tf_op jit(solution)/shard_map/all_to_all | solution.py:169
  85.1 14.8 %copy-start.1 = (bf16[64,16,1024]{2,1,0:T(8,128)(2,1)}, bf16[64,16,1024]{2,1,0:T(8,128)(2,1)S(1)}, u32[]{:S(2)}) copy-start(bf16[64,16,1024]{2,1,0:T(8,128)(2,1)S(1)} %all-to-all-done.1) | copy-start | bytes 6291460
  85.1 49.5 %all-to-all-start.2 = ((bf16[64,16,1024]{2,1,0:T(8,128)(2,1)}), bf16[64,16,1024]{2,1,0:T(8,128)(2,1)}, u32[]{:S(2)}, u32[]{:S(2)}) async-start(bf16[64,16,1024]{2,1,0:T(8,128)(2,1)} %gather_fusion.5), calls=%async_computation.2 | async-start | bytes 4194304 | tf_op jit(solution)/shard_map/all_to_all | solution.py:169
  97.0 112.5 %collective-permute-start.9 = (bf16[16,4,32,1024]{3,2,1,0:T(8,128)(2,1)}, bf16[16,4,32,1024]{3,2,1,0:T(8,128)(2,1)}, u32[]{:S(2)}, u32[]{:S(2)}) collective-permute-start(bf16[16,4,32,1024]{3,2,1,0:T(8,128)(2,1)} %bitcast.85), channel_id=1, source_target_pairs={{0,4},{4,0},{1,5},{5,1},{2,6},{6,2},{3,7},{7,3},{8,12},{12,8},{9,1... | collective-permute-start | bytes 12582920 | tf_op jit(solution)/shard_map/ppermute | solution.py:184
  98.5 57.0 %collective-permute-start = (bf16[16,16,1024]{2,1,0:T(8,128)(2,1)}, bf16[16,16,1024]{2,1,0:T(8,128)(2,1)S(1)}, u32[]{:S(2)}, u32[]{:S(2)}) collective-permute-start(bf16[16,16,1024]{2,1,0:T(8,128)(2,1)} %gather_fusion.2), channel_id=1, source_target_pairs={{0,1},{1,2},{2,3},{3,0},{4,5},{5,6},{6,7},{7,4},{8,9},{9,10},{10,1... | collective-permute-start | bytes 1572872 | tf_op jit(solution)/shard_map/ppermute | solution.py:179
  101.2 55.2 %collective-permute-start.1 = (bf16[16,16,1024]{2,1,0:T(8,128)(2,1)}, bf16[16,16,1024]{2,1,0:T(8,128)(2,1)S(1)}, u32[]{:S(2)}, u32[]{:S(2)}) collective-permute-start(bf16[16,16,1024]{2,1,0:T(8,128)(2,1)} %gather_fusion.3), channel_id=1, source_target_pairs={{0,2},{1,3},{2,0},{3,1},{4,6},{5,7},{6,4},{7,5},{8,10},{9,11},{10,... | collective-permute-start | bytes 1572872 | tf_op jit(solution)/shard_map/ppermute | solution.py:179
  108.7 63.9 %collective-permute-start.2 = (bf16[16,16,1024]{2,1,0:T(8,128)(2,1)}, bf16[16,16,1024]{2,1,0:T(8,128)(2,1)S(1)}, u32[]{:S(2)}, u32[]{:S(2)}) collective-permute-start(bf16[16,16,1024]{2,1,0:T(8,128)(2,1)} %gather_fusion.4), channel_id=1, source_target_pairs={{0,3},{1,0},{2,1},{3,2},{4,7},{5,4},{6,5},{7,6},{8,11},{9,8},{10,9... | collective-permute-start | bytes 1572872 | tf_op jit(solution)/shard_map/ppermute | solution.py:179
  137.6 63.2 %collective-permute-start.3 = (bf16[16,16,1024]{2,1,0:T(8,128)(2,1)}, bf16[16,16,1024]{2,1,0:T(8,128)(2,1)}, u32[]{:S(2)}, u32[]{:S(2)}) collective-permute-start(bf16[16,16,1024]{2,1,0:T(8,128)(2,1)} %gather_fusion.7), channel_id=1, source_target_pairs={{0,1},{1,2},{2,3},{3,0},{4,5},{5,6},{6,7},{7,4},{8,9},{9,10},{10,1... | collective-permute-start | bytes 1572872 | tf_op jit(solution)/shard_map/ppermute | solution.py:179
  155.5 45.2 %collective-permute-start.4 = (bf16[16,16,1024]{2,1,0:T(8,128)(2,1)}, bf16[16,16,1024]{2,1,0:T(8,128)(2,1)}, u32[]{:S(2)}, u32[]{:S(2)}) collective-permute-start(bf16[16,16,1024]{2,1,0:T(8,128)(2,1)} %gather_fusion.8), channel_id=1, source_target_pairs={{0,2},{1,3},{2,0},{3,1},{4,6},{5,7},{6,4},{7,5},{8,10},{9,11},{10,... | collective-permute-start | bytes 1572872 | tf_op jit(solution)/shard_map/ppermute | solution.py:179
  156.4 53.1 %collective-permute-start.5 = (bf16[16,16,1024]{2,1,0:T(8,128)(2,1)}, bf16[16,16,1024]{2,1,0:T(8,128)(2,1)}, u32[]{:S(2)}, u32[]{:S(2)}) collective-permute-start(bf16[16,16,1024]{2,1,0:T(8,128)(2,1)} %gather_fusion.9), channel_id=1, source_target_pairs={{0,3},{1,0},{2,1},{3,2},{4,7},{5,4},{6,5},{7,6},{8,11},{9,8},{10,9... | collective-permute-start | bytes 1572872 | tf_op jit(solution)/shard_map/ppermute | solution.py:179
Sparse Core Ops, SparseCore 0:
  24.9 72.0 all-gather.2

commit v7 on v6

--- a/solution.py
+++ b/solution.py
@@ -10,19 +10,30 @@
 SPAN_LEN = 64
 SPANS_STEP = 2
 CHUNKS = 2
+PARTS = 2
+MIB = 1024 * 1024
 SPAN = ("y", "x", "z", "core")
 
 
-def attention_kernel(where_ref, *refs):
+def weight_of(w_ref, which, g):
+    width, cols = w_ref.shape[-1], w_ref.shape[-1] // w_ref.shape[2]
+    return w_ref[:, :, g, :, which * cols : (which + 1) * cols].reshape(width, cols)
+
+
+def rows_of(x_refs):
+    some = x_refs[0].shape[0] // SPANS_STEP
+    return jnp.concatenate(
+        [x_ref[i * some : (i + 1) * some] for i in range(SPANS_STEP) for x_ref in x_refs], axis=0
+    )
+
+
+def prepare_kernel(where_ref, *refs):
     x_refs = refs[:-8]
-    now_ref, next_ref, own_ref, other_ref, out_ref, k_ref, v_ref, w_ref = refs[-8:]
+    now_ref, next_ref, own_ref, other_ref, q_ref, k_ref, v_ref, w_ref = refs[-8:]
     f32, bf16 = jnp.float32, jnp.bfloat16
-    spans = SPANS_STEP
-    some, width = x_refs[0].shape
-    some //= spans
-    keys = len(x_refs) * some
     groups = own_ref.shape[1]
-    cols = width // groups
+    cols = own_ref.shape[-1] // groups
+    rows = SPANS_STEP * SPAN_LEN
 
     @pl.when(pl.program_id(0) == 0)
     def _():
@@ -30,42 +41,51 @@
         w_ref[core] = own_ref[...]
         w_ref[1 - core] = other_ref[...]
 
-    rows = spans * SPAN_LEN
-
-    x = jnp.concatenate(
-        [
-            x_ref[i * some : (i + 1) * some]
-            for i in range(spans)
-            for x_ref in x_refs
-        ],
-        axis=0,
-    )
+    x = rows_of(x_refs)
     both = jnp.concatenate([now_ref[...], next_ref[...]], axis=0)
     row = lax.broadcasted_iota(jnp.int32, (rows, rows + SPAN_LEN), 0)
     col = lax.broadcasted_iota(jnp.int32, (rows, rows + SPAN_LEN), 1)
     shift = jnp.where(col == row + SPAN_LEN - 1, 1.0, 0.0).astype(bf16)
     states = jnp.dot(shift, both, preferred_element_type=f32).astype(bf16)
-
-    def weight(which, g):
-        return w_ref[:, :, g, :, which * cols : (which + 1) * cols].reshape(width, cols)
-
+    for g in range(groups):
+        here = slice(g * cols, (g + 1) * cols)
+        for source, target, which in ((x, k_ref, 0), (x, v_ref, 1), (states, q_ref, 2)):
+            target[:, here] = jnp.dot(
+                source, weight_of(w_ref, which, g), preferred_element_type=f32
+            ).astype(bf16)
+
+
+def attend_kernel(*refs):
+    x_refs = refs[:-7]
+    q_ref, k_ref, v_ref, w_ref, out_ref, late_k_ref, late_v_ref = refs[-7:]
+    f32, bf16 = jnp.float32, jnp.bfloat16
+    spans, width = SPANS_STEP, w_ref.shape[-1]
+    groups = w_ref.shape[2]
+    cols = width // groups
+    rows = spans * SPAN_LEN
+    early = k_ref.shape[0] // spans
+    late = late_k_ref.shape[0] // spans
+    x = rows_of(x_refs)
     total = jnp.zeros((rows, width), f32)
     lane = lax.broadcasted_iota(jnp.int32, (SPAN_LEN, 128), 1)
     low = lane < HEAD_DIM
     for g in range(groups):
-        k_ref[...] = jnp.dot(x, weight(0, g), preferred_element_type=f32).astype(bf16)
-        v_ref[...] = jnp.dot(x, weight(1, g), preferred_element_type=f32).astype(bf16)
-        q = jnp.dot(states, weight(2, g), preferred_element_type=f32).astype(bf16)
+        for target, which in ((late_k_ref, 0), (late_v_ref, 1)):
+            target[...] = jnp.dot(
+                x, weight_of(w_ref, which, g), preferred_element_type=f32
+            ).astype(bf16)
         context_rows = []
         for i in range(spans):
             pieces = []
             for pair in range(cols // 128):
                 here = slice(pair * 128, pair * 128 + 128)
-                qp = q[i * SPAN_LEN : (i + 1) * SPAN_LEN, here]
+                there = slice(g * cols + pair * 128, g * cols + pair * 128 + 128)
+                first, second = slice(i * early, (i + 1) * early), slice(i * late, (i + 1) * late)
+                qp = q_ref[i * SPAN_LEN : (i + 1) * SPAN_LEN, there]
                 zero = jnp.zeros_like(qp)
                 two = jnp.concatenate([jnp.where(low, qp, zero), jnp.where(low, zero, qp)], axis=0)
-                kp = k_ref[i * keys : (i + 1) * keys, here]
-                vp = v_ref[i * keys : (i + 1) * keys, here]
+                kp = jnp.concatenate([k_ref[first, there], late_k_ref[second, here]], axis=0)
+                vp = jnp.concatenate([v_ref[first, there], late_v_ref[second, here]], axis=0)
                 scores = lax.dot_general(
                     two, kp, (((1,), (1,)), ((), ())), preferred_element_type=f32
                 ) * (HEAD_DIM ** -0.5)
@@ -77,58 +97,99 @@
             context_rows.append(jnp.concatenate(pieces, axis=1))
         context = jnp.concatenate(context_rows, axis=0)
         total = total + lax.dot_general(
-            context, weight(3, g), (((1,), (1,)), ((), ())), preferred_element_type=f32
+            context, weight_of(w_ref, 3, g), (((1,), (1,)), ((), ())), preferred_element_type=f32
         )
     for g in range(groups):
         out_ref[g] = total[:, g * cols : (g + 1) * cols].astype(bf16)
 
 
-def attend(where, chunks, states, weights, other):
-    total, width = chunks[0].shape
+def settings(room):
+    return pltpu.CompilerParams(
+        dimension_semantics=("arbitrary",), vmem_limit_bytes=room * MIB
+    )
+
+
+def prepare(where, chunks, states, weights, other):
+    held, width = chunks[0].shape
     spans = states.shape[0] // SPAN_LEN // weights.shape[1]
-    some = total // spans
+    some = held // spans
     steps = spans // SPANS_STEP
     rows = SPANS_STEP * SPAN_LEN
     last = states.shape[0] // SPAN_LEN - 1
     keys = some * len(chunks)
-    groups = weights.shape[1]
-    cols = width // groups
-
-    def after(i, where_ref):
-        return jnp.minimum((where_ref[0] * steps + i + 1) * SPANS_STEP, last), 0
-
-    flops = 2 * spans * (keys * width * 2 * width + SPAN_LEN * 2 * width * width)
+    whole = pl.BlockSpec(memory_space=pltpu.VMEM)
+    bf16 = jnp.bfloat16
+
+    def after(i, h):
+        return jnp.minimum((h[0] * steps + i + 1) * SPANS_STEP, last), 0
+
     return pl.pallas_call(
-        attention_kernel,
-        out_shape=jax.ShapeDtypeStruct((groups, spans * SPAN_LEN, cols), jnp.bfloat16),
+        prepare_kernel,
+        out_shape=(
+            jax.ShapeDtypeStruct((spans * SPAN_LEN, width), bf16),
+            jax.ShapeDtypeStruct((spans * keys, width), bf16),
+            jax.ShapeDtypeStruct((spans * keys, width), bf16),
+            jax.ShapeDtypeStruct((2, *weights.shape), bf16),
+        ),
         grid_spec=pltpu.PrefetchScalarGridSpec(
             num_scalar_prefetch=1,
             grid=(steps,),
-            in_specs=[
-                pl.BlockSpec((SPANS_STEP * some, width), lambda i, h: (i, 0))
-                for _ in chunks
-            ]
+            in_specs=[pl.BlockSpec((SPANS_STEP * some, width), lambda i, h: (i, 0)) for _ in chunks]
             + [
                 pl.BlockSpec((rows, width), lambda i, h: (h[0] * steps + i, 0)),
                 pl.BlockSpec((SPAN_LEN, width), after),
-                pl.BlockSpec(memory_space=pltpu.VMEM),
-                pl.BlockSpec(memory_space=pltpu.VMEM),
+                whole,
+                whole,
             ],
-            out_specs=pl.BlockSpec((groups, rows, cols), lambda i, h: (0, i, 0)),
-            scratch_shapes=[
-                pltpu.VMEM((SPANS_STEP * keys, cols), jnp.bfloat16),
-                pltpu.VMEM((SPANS_STEP * keys, cols), jnp.bfloat16),
-                pltpu.VMEM((2, *weights.shape), jnp.bfloat16),
-            ],
-        ),
-        compiler_params=pltpu.CompilerParams(
-            dimension_semantics=("arbitrary",), vmem_limit_bytes=48 * 1024 * 1024
-        ),
+            out_specs=(
+                pl.BlockSpec((rows, width), lambda i, h: (i, 0)),
+                pl.BlockSpec((SPANS_STEP * keys, width), lambda i, h: (i, 0)),
+                pl.BlockSpec((SPANS_STEP * keys, width), lambda i, h: (i, 0)),
+                whole,
+            ),
+        ),
+        compiler_params=settings(30),
         cost_estimate=pl.CostEstimate(
-            flops=flops, bytes_accessed=2 * (len(chunks) * chunks[0].size + 2 * weights.size), transcendentals=0
-        ),
-        name="attend",
+            flops=2 * spans * width * width * (2 * keys + SPAN_LEN),
+            bytes_accessed=2 * (len(chunks) * chunks[0].size + 4 * weights.size),
+            transcendentals=0,
+        ),
+        name="prepare",
     )(where, *chunks, states, states, weights, other)
+
+
+def attend(part, chunks, queries, keys, values, weights):
+    held, width = chunks[0].shape
+    spans = queries.shape[0] // SPAN_LEN
+    some = held // spans
+    steps = spans // SPANS_STEP // PARTS
+    rows = SPANS_STEP * SPAN_LEN
+    early = keys.shape[0] // spans
+    late = some * len(chunks)
+    groups = weights.shape[2]
+    cols = width // groups
+
+    def block(count):
+        return pl.BlockSpec((SPANS_STEP * count, width), lambda i: (part * steps + i, 0))
+
+    return pl.pallas_call(
+        attend_kernel,
+        out_shape=jax.ShapeDtypeStruct((groups, steps * rows, cols), jnp.bfloat16),
+        grid=(steps,),
+        in_specs=[block(some) for _ in chunks]
+        + [block(SPAN_LEN), block(early), block(early), pl.BlockSpec(memory_space=pltpu.VMEM)],
+        out_specs=pl.BlockSpec((groups, rows, cols), lambda i: (0, i, 0)),
+        scratch_shapes=[
+            pltpu.VMEM((SPANS_STEP * late, cols), jnp.bfloat16),
+            pltpu.VMEM((SPANS_STEP * late, cols), jnp.bfloat16),
+        ],
+        compiler_params=settings(30),
+        cost_estimate=pl.CostEstimate(
+            flops=2 * spans // PARTS * width * width * (2 * late + 6 * SPAN_LEN),
+            bytes_accessed=2 * (len(chunks) * chunks[0].size // PARTS + weights.size),
+            transcendentals=0,
+        ),
+    )(*chunks, queries, keys, values, weights)
 
 
 def layer(
@@ -183,8 +244,14 @@
     weights = weights.reshape(-1, groups, depth, width)
     other = lax.ppermute(weights, "core", [(0, 1), (1, 0)])
     where = jnp.stack([head, lax.axis_index("core")])
-    result = attend(where, owned, decoder_states, weights, other)
-    columns = lax.all_to_all(result, "head", split_axis=0, concat_axis=0, tiled=True)
+    queries, keys, values, weights = prepare(where, owned[:groups], decoder_states, weights, other)
+    returned = []
+    for p in range(PARTS):
+        result = attend(p, owned[groups:], queries, keys, values, weights)
+        returned.append(
+            lax.all_to_all(result, "head", split_axis=0, concat_axis=0, tiled=True)
+        )
+    columns = jnp.concatenate(returned, axis=1)
     columns = columns.reshape(decoder_states.shape[0], width // groups)
     offset = SPAN_LEN - 1
     return jnp.concatenate(

time: 280 us -> 280 us (level)
  the two profiles are of different devices: /device:TPU:2 before, /device:TPU:4 now
where the time goes in v7:
time: 280 us; the launch traced here: 279 us
  starting transfers between devices  76.7 us (27%)
  waiting for transfers between devices  68.3 us (24%)
  local copies, waits for them, and re-layouts  53.2 us (19%)
  blocking collectives  35 us (12%)
  Pallas kernels  30.7 us (11%)
  between operations  13.6 us (5%)
    all_to_all x2, waiting for transfers between devices, layer(): lax.all_to_all(pieces[CHUNKS * wanted + c], SPAN, split_axis=0, concat_ax...  48 us
    ppermute x6, starting transfers between devices, layer(): lax.ppermute(block, 'head', [(i, (i + step) % groups) for i in range(grou...  45.8 us
    all_to_all x1, blocking collectives, layer(): lax.all_to_all(result, 'head', split_axis=0, concat_axis=0, tiled=True)  21 us
    unnamed x25, local copies, waits for them, and re-layouts  20.3 us
    gather x8, local copies, waits for them, and re-layouts, layer(): block = arrived[sources[(head + step) % groups]]  19 us
    pallas_call x2, Pallas kernels, attend(): pl.pallas_call(attend_kernel, out_shape=jax.ShapeDtypeStruct((groups, ste...  18.9 us
    all_to_all x2, starting transfers between devices, layer(): lax.all_to_all(pieces[CHUNKS * wanted + c], SPAN, split_axis=0, concat_ax...  16 us
    all_to_all x1, blocking collectives, layer(): lax.all_to_all(request, SPAN, split_axis=0, concat_axis=0, tiled=True)  14 us
  transfers between devices with their start and end apart: 14, of which 7 were waited for; matrix products, arithmetic and copies ran while one was open for 11% of the time, Pallas kernels for 8%

profile of v7, /device:TPU:4, one launch (start us, length us, event | category | flops | bytes accessed | tf_op | source)
XLA Modules:
  0.0 279.1 jit_solution(6395280285564951834)
XLA Ops:
  6.5 1.0 copy-done
  7.6 0.1 constant_dynamic-slice_fusion
  7.7 0.1 copy.37
  7.7 0.7 constant_dynamic-slice_fusion.3
  8.5 0.7 constant_dynamic-slice_fusion.1
  9.2 3.3 %collective-permute-start.6 = (bf16[32,1024]{1,0:T(8,128)(2,1)S(1)}, bf16[32,1024]{1,0:T(8,128)(2,1)S(1)}, u32[]{:S(2)}, u32[]{:S(2)}) collective-permute-start(bf16[32,1024]{1,0:T(8,128)(2,1)S(1)} %get-tuple-element.14), channel_id=1, source_target_pairs={{0,1},{1,2},{2,3},{3,0},{4,5},{5,6},{6,7},{7,4},{8,9},{9,10},{10,1... | collective-permute-start | bytes 196616 | tf_op jit(solution)/shard_map/ppermute | solution.py:214
  12.6 5.4 %collective-permute-start.7 = (bf16[32,1024]{1,0:T(8,128)(2,1)S(1)}, bf16[32,1024]{1,0:T(8,128)(2,1)S(1)}, u32[]{:S(2)}, u32[]{:S(2)}) collective-permute-start(bf16[32,1024]{1,0:T(8,128)(2,1)S(1)} %get-tuple-element.14), channel_id=1, source_target_pairs={{0,2},{1,3},{2,0},{3,1},{4,6},{5,7},{6,4},{7,5},{8,10},{9,11},{10,... | collective-permute-start | bytes 196616 | tf_op jit(solution)/shard_map/ppermute | solution.py:214
  18.0 2.7 collective-permute-start.8
  20.7 1.4 collective-permute-done.7
  22.1 2.8 %collective-permute-done.8 = bf16[32,1024]{1,0:T(8,128)(2,1)S(1)} collective-permute-done((bf16[32,1024]{1,0:T(8,128)(2,1)S(1)}, bf16[32,1024]{1,0:T(8,128)(2,1)S(1)}, u32[]{:S(2)}, u32[]{:S(2)}) %collective-permute-start.8) | collective-permute-done | bytes 65568 | tf_op jit(solution)/shard_map/ppermute | solution.py:214
  24.9 1.3 gather_fusion.10
  26.2 0.0 all-gather.3.cloned.1.call-update
  26.2 0.8 fusion.13
  27.0 0.1 copy.32
  27.1 0.1 eq.26
  27.2 0.1 copy.33
  27.3 0.1 broadcast_in_dim.14
  27.4 0.1 select_reduce_fusion
  27.5 0.1 copy.34
  27.6 14.0 %all_to_all.29 = s32[64,1,1]{2,1,0:T(1,128)S(1)} all-to-all(s32[64,1,1]{2,1,0:T(1,128)S(1)} %copy.34), channel_id=1, replica_groups=mesh['y'=4,'x'=4,'z'=2,'core'=2,'head'=4] {'y','x','z','core'}, dimensions={0} | all-to-all | bytes 512 | tf_op jit(solution)/shard_map/all_to_all | solution.py:223
  41.6 1.2 multiply_reduce_fusion
  42.8 4.3 %gather_fusion.5 = bf16[64,16,1024]{2,1,0:T(8,128)(2,1)} fusion(bf16[128,16,1024]{2,1,0:T(8,128)(2,1)} %bitcast.81, s32[1024]{0:T(1024)S(1)} %pad_clamp_fusion.1), kind=kCustom, calls=%fused_computation.5 | custom fusion | bytes 4194560 | tf_op jit(solution)/shard_map/gather | solution.py:231
  47.1 6.5 %all-to-all-start.2 = ((bf16[64,16,1024]{2,1,0:T(8,128)(2,1)}), bf16[64,16,1024]{2,1,0:T(8,128)(2,1)S(1)}, u32[]{:S(2)}, u32[]{:S(2)}) async-start(bf16[64,16,1024]{2,1,0:T(8,128)(2,1)} %gather_fusion.5), calls=%async_computation.2 | async-start | bytes 4194304 | tf_op jit(solution)/shard_map/all_to_all | solution.py:230
  53.6 4.2 %gather_fusion = bf16[64,16,1024]{2,1,0:T(8,128)(2,1)} fusion(bf16[128,16,1024]{2,1,0:T(8,128)(2,1)} %bitcast.82, s32[1024]{0:T(1024)S(1)} %pad_clamp_fusion.6), kind=kCustom, calls=%fused_computation | custom fusion | bytes 4194560 | tf_op jit(solution)/shard_map/gather | solution.py:231
  57.8 27.7 %all-to-all-done.2 = bf16[64,16,1024]{2,1,0:T(8,128)(2,1)S(1)} async-done(((bf16[64,16,1024]{2,1,0:T(8,128)(2,1)}), bf16[64,16,1024]{2,1,0:T(8,128)(2,1)S(1)}, u32[]{:S(2)}, u32[]{:S(2)}) %all-to-all-start.2) | async-done | bytes 2097184 | tf_op jit(solution)/shard_map/all_to_all | solution.py:230
  85.5 9.5 %all-to-all-start.1 = ((bf16[64,16,1024]{2,1,0:T(8,128)(2,1)}), bf16[64,16,1024]{2,1,0:T(8,128)(2,1)}, u32[]{:S(2)}, u32[]{:S(2)}) async-start(bf16[64,16,1024]{2,1,0:T(8,128)(2,1)} %gather_fusion), calls=%async_computation.1 | async-start | bytes 4194304 | tf_op jit(solution)/shard_map/all_to_all | solution.py:230
  95.0 2.4 all-gather.3.cloned.1.call-done
  97.4 0.0 collective-permute-start.9
  97.4 0.1 reshape_reshape_squeeze.3
  97.5 0.6 gather_fusion.7
  98.1 2.1 collective-permute-start.3
  100.2 2.2 gather_fusion.8
  102.4 3.9 %collective-permute-start.4 = (bf16[16,16,1024]{2,1,0:T(8,128)(2,1)S(1)}, bf16[16,16,1024]{2,1,0:T(8,128)(2,1)S(1)}, u32[]{:S(2)}, u32[]{:S(2)}) collective-permute-start(bf16[16,16,1024]{2,1,0:T(8,128)(2,1)S(1)} %gather_fusion.8), channel_id=1, source_target_pairs={{0,2},{1,3},{2,0},{3,1},{4,6},{5,7},{6,4},{7,5},{8,10},{9,11},{10,... | collective-permute-start | bytes 1572872 | tf_op jit(solution)/shard_map/ppermute | solution.py:240
  106.3 3.0 %gather_fusion.9 = bf16[16,16,1024]{2,1,0:T(8,128)(2,1)} fusion(bf16[64,16,1024]{2,1,0:T(8,128)(2,1)} %copy-done.11, s32[1024]{0:T(1024)S(1)} %pad_clamp_fusion.2), kind=kCustom, calls=%fused_computation.9 | custom fusion | bytes 1048640 | tf_op jit(solution)/shard_map/gather | solution.py:238
  109.2 2.2 collective-permute-start.5
  111.5 20.3 %all-to-all-done.1 = bf16[64,16,1024]{2,1,0:T(8,128)(2,1)} async-done(((bf16[64,16,1024]{2,1,0:T(8,128)(2,1)}), bf16[64,16,1024]{2,1,0:T(8,128)(2,1)}, u32[]{:S(2)}, u32[]{:S(2)}) %all-to-all-start.1) | async-done | bytes 2097184 | tf_op jit(solution)/shard_map/all_to_all | solution.py:230
  131.8 3.0 %gather_fusion.3 = bf16[16,16,1024]{2,1,0:T(8,128)(2,1)} fusion(bf16[64,16,1024]{2,1,0:T(8,128)(2,1)} %all-to-all-done.1, s32[1024]{0:T(1024)S(1)} %pad_clamp_fusion.3), kind=kCustom, calls=%fused_computation.3 | custom fusion | bytes 1048640 | tf_op jit(solution)/shard_map/gather | solution.py:238
  134.7 3.4 %collective-permute-start.1 = (bf16[16,16,1024]{2,1,0:T(8,128)(2,1)}, bf16[16,16,1024]{2,1,0:T(8,128)(2,1)S(1)}, u32[]{:S(2)}, u32[]{:S(2)}) collective-permute-start(bf16[16,16,1024]{2,1,0:T(8,128)(2,1)} %gather_fusion.3), channel_id=1, source_target_pairs={{0,2},{1,3},{2,0},{3,1},{4,6},{5,7},{6,4},{7,5},{8,10},{9,11},{10,... | collective-permute-start | bytes 1572872 | tf_op jit(solution)/shard_map/ppermute | solution.py:240
  138.2 3.0 %gather_fusion.4 = bf16[16,16,1024]{2,1,0:T(8,128)(2,1)} fusion(bf16[64,16,1024]{2,1,0:T(8,128)(2,1)} %all-to-all-done.1, s32[1024]{0:T(1024)S(1)} %pad_clamp_fusion.2), kind=kCustom, calls=%fused_computation.4 | custom fusion | bytes 1048640 | tf_op jit(solution)/shard_map/gather | solution.py:238
  141.1 3.0 %gather_fusion.2 = bf16[16,16,1024]{2,1,0:T(8,128)(2,1)} fusion(bf16[64,16,1024]{2,1,0:T(8,128)(2,1)} %all-to-all-done.1, s32[1024]{0:T(1024)S(1)} %pad_clamp_fusion.4), kind=kCustom, calls=%fused_computation.2 | custom fusion | bytes 1048640 | tf_op jit(solution)/shard_map/gather | solution.py:238
  144.1 2.4 collective-permute-done.3
  146.5 11.3 %collective-permute-done.4 = bf16[16,16,1024]{2,1,0:T(8,128)(2,1)S(1)} collective-permute-done((bf16[16,16,1024]{2,1,0:T(8,128)(2,1)S(1)}, bf16[16,16,1024]{2,1,0:T(8,128)(2,1)S(1)}, u32[]{:S(2)}, u32[]{:S(2)}) %collective-permute-start.4) | collective-permute-done | bytes 524320 | tf_op jit(solution)/shard_map/ppermute | solution.py:240
  157.8 34.1 %collective-permute-start = (bf16[16,16,1024]{2,1,0:T(8,128)(2,1)}, bf16[16,16,1024]{2,1,0:T(8,128)(2,1)}, u32[]{:S(2)}, u32[]{:S(2)}) collective-permute-start(bf16[16,16,1024]{2,1,0:T(8,128)(2,1)} %gather_fusion.2), channel_id=1, source_target_pairs={{0,1},{1,2},{2,3},{3,0},{4,5},{5,6},{6,7},{7,4},{8,9},{9,10},{10,1... | collective-permute-start | bytes 1572872 | tf_op jit(solution)/shard_map/ppermute | solution.py:240
  192.0 0.1 pad_add_fusion.where_ref
  192.0 2.2 gather_fusion.6
  194.2 2.2 gather_fusion.1
  196.4 2.2 copy-done.1
  198.6 2.2 copy-done.2
  200.8 11.9 %prepare.1 = (bf16[512,1024]{1,0:T(8,128)(2,1)S(1)}, bf16[1024,1024]{1,0:T(8,128)(2,1)S(1)}, bf16[1024,1024]{1,0:T(8,128)(2,1)S(1)}, bf16[2,16,4,32,1024]{4,3,2,1,0:T(8,128)(2,1)}) custom-call(s32[2]{0:T(128)S(1)} %pad_add_fusion.where_ref, bf16[256,1024]{1,0:T(8,128)(2,1)S(1)} %bitcast.74, bf16[256,1024]{1,0:T(8,128)(2,1)S(1)} %bitcast.77, ...), custom_call_target="tpu_custom_call" | custom-call | flops 5368709120 | bytes 18874368 | tf_op jit(solution)/shard_map/prepare/pallas_call | solution.py:126
  212.7 3.4 %copy-done.3 = bf16[2,16,4,32,1024]{4,3,2,1,0:T(8,128)(2,1)S(1)} copy-done((bf16[2,16,4,32,1024]{4,3,2,1,0:T(8,128)(2,1)S(1)}, bf16[2,16,4,32,1024]{4,3,2,1,0:T(8,128)(2,1)}, u32[]{:S(2)}) %copy-start.3) | copy-done | bytes 8388632
  216.1 9.8 %shard_map.73 = bf16[4,256,256]{2,1,0:T(8,128)(2,1)} custom-call(bf16[256,1024]{1,0:T(8,128)(2,1)S(1)} %bitcast.72, bf16[256,1024]{1,0:T(8,128)(2,1)} %bitcast.8.refs_1_, bf16[256,1024]{1,0:T(8,128)(2,1)S(1)} %bitcast.78, bf16[256,1024]{1,0:T(8,128)(2,1)} %bitcast.14.refs_3_, bf16[512,1024]{1,0:T(8,128)(2,1)S(1)} %get-tuple-element.9.refs_4_, ...), custom_call_target="tpu_custom_call" | custom-call | flops 5368709120 | bytes 9437184 | tf_op jit(solution)/shard_map/pallas_call | solution.py:175
  225.8 1.4 copy-done.5
  227.2 1.3 copy-done.7
  228.5 1.0 copy-done.9
  229.5 3.5 %all-to-all-start.3 = ((bf16[4,256,256]{2,1,0:T(8,128)(2,1)}), bf16[4,256,256]{2,1,0:T(8,128)(2,1)S(1)}, u32[]{:S(2)}, u32[]{:S(2)}) async-start(bf16[4,256,256]{2,1,0:T(8,128)(2,1)} %shard_map.73), calls=%async_computation.3 | async-start | bytes 1048576 | tf_op jit(solution)/shard_map/all_to_all | solution.py:252
  233.0 3.4 %copy-done.4 = bf16[2,16,4,32,1024]{4,3,2,1,0:T(8,128)(2,1)S(1)} copy-done((bf16[2,16,4,32,1024]{4,3,2,1,0:T(8,128)(2,1)S(1)}, bf16[2,16,4,32,1024]{4,3,2,1,0:T(8,128)(2,1)}, u32[]{:S(2)}) %copy-start.4) | copy-done | bytes 8388632
  236.4 1.6 copy-done.6
  238.0 1.6 copy-done.8
  239.6 1.2 copy-done.10
  240.8 9.1 %shard_map.74 = bf16[4,256,256]{2,1,0:T(8,128)(2,1)S(1)} custom-call(bf16[256,1024]{1,0:T(8,128)(2,1)S(1)} %bitcast.73, bf16[256,1024]{1,0:T(8,128)(2,1)} %bitcast.8.refs_1_, bf16[256,1024]{1,0:T(8,128)(2,1)S(1)} %bitcast.79, bf16[256,1024]{1,0:T(8,128)(2,1)} %bitcast.14.refs_3_, bf16[512,1024]{1,0:T(8,128)(2,1)S(1)} %copy-done.10, ...), custom_call_target="tpu_custom_call" | custom-call | flops 5368709120 | bytes 9437184 | tf_op jit(solution)/shard_map/pallas_call | solution.py:175
  249.9 21.0 %all_to_all.30 = bf16[4,256,256]{2,1,0:T(8,128)(2,1)S(1)} all-to-all(bf16[4,256,256]{2,1,0:T(8,128)(2,1)S(1)} %shard_map.74), channel_id=1, replica_groups=mesh['y'=4,'x'=4,'z'=2,'core'=2,'head'=4] {'head'}, dimensions={0} | all-to-all | bytes 1048576 | tf_op jit(solution)/shard_map/all_to_all | solution.py:252
  270.9 0.1 pad_maximum_fusion
  271.0 0.1 slice.34
  271.0 1.2 concatenate.11
  (34 shorter events, 0.2 us)
Async XLA Ops:
  6.5 1.0 copy-start
  6.5 90.9 %all-gather.3.cloned.1.call-start = ((), (), s32[]{:S(2)}) async-start(), calls=%async_computation.5 | async-start | bytes 4456448 | tf_op jit(solution)/shard_map/all_gather | solution.py:224
  9.2 11.4 %collective-permute-start.6 = (bf16[32,1024]{1,0:T(8,128)(2,1)S(1)}, bf16[32,1024]{1,0:T(8,128)(2,1)S(1)}, u32[]{:S(2)}, u32[]{:S(2)}) collective-permute-start(bf16[32,1024]{1,0:T(8,128)(2,1)S(1)} %get-tuple-element.14), channel_id=1, source_target_pairs={{0,1},{1,2},{2,3},{3,0},{4,5},{5,6},{6,7},{7,4},{8,9},{9,10},{10,1... | collective-permute-start | bytes 196616 | tf_op jit(solution)/shard_map/ppermute | solution.py:214
  12.6 9.5 %collective-permute-start.7 = (bf16[32,1024]{1,0:T(8,128)(2,1)S(1)}, bf16[32,1024]{1,0:T(8,128)(2,1)S(1)}, u32[]{:S(2)}, u32[]{:S(2)}) collective-permute-start(bf16[32,1024]{1,0:T(8,128)(2,1)S(1)} %get-tuple-element.14), channel_id=1, source_target_pairs={{0,2},{1,3},{2,0},{3,1},{4,6},{5,7},{6,4},{7,5},{8,10},{9,11},{10,... | collective-permute-start | bytes 196616 | tf_op jit(solution)/shard_map/ppermute | solution.py:214
  18.0 6.9 %collective-permute-start.8 = (bf16[32,1024]{1,0:T(8,128)(2,1)S(1)}, bf16[32,1024]{1,0:T(8,128)(2,1)S(1)}, u32[]{:S(2)}, u32[]{:S(2)}) collective-permute-start(bf16[32,1024]{1,0:T(8,128)(2,1)S(1)} %get-tuple-element.14), channel_id=1, source_target_pairs={{0,3},{1,0},{2,1},{3,2},{4,7},{5,4},{6,5},{7,6},{8,11},{9,8},{10,9... | collective-permute-start | bytes 196616 | tf_op jit(solution)/shard_map/ppermute | solution.py:214
  47.1 38.4 %all-to-all-start.2 = ((bf16[64,16,1024]{2,1,0:T(8,128)(2,1)}), bf16[64,16,1024]{2,1,0:T(8,128)(2,1)S(1)}, u32[]{:S(2)}, u32[]{:S(2)}) async-start(bf16[64,16,1024]{2,1,0:T(8,128)(2,1)} %gather_fusion.5), calls=%async_computation.2 | async-start | bytes 4194304 | tf_op jit(solution)/shard_map/all_to_all | solution.py:230
  85.5 12.0 %copy-start.11 = (bf16[64,16,1024]{2,1,0:T(8,128)(2,1)}, bf16[64,16,1024]{2,1,0:T(8,128)(2,1)S(1)}, u32[]{:S(2)}) copy-start(bf16[64,16,1024]{2,1,0:T(8,128)(2,1)S(1)} %all-to-all-done.2) | copy-start | bytes 6291460
  85.5 46.2 %all-to-all-start.1 = ((bf16[64,16,1024]{2,1,0:T(8,128)(2,1)}), bf16[64,16,1024]{2,1,0:T(8,128)(2,1)}, u32[]{:S(2)}, u32[]{:S(2)}) async-start(bf16[64,16,1024]{2,1,0:T(8,128)(2,1)} %gather_fusion), calls=%async_computation.1 | async-start | bytes 4194304 | tf_op jit(solution)/shard_map/all_to_all | solution.py:230
  97.4 99.0 %collective-permute-start.9 = (bf16[16,4,32,1024]{3,2,1,0:T(8,128)(2,1)}, bf16[16,4,32,1024]{3,2,1,0:T(8,128)(2,1)}, u32[]{:S(2)}, u32[]{:S(2)}) collective-permute-start(bf16[16,4,32,1024]{3,2,1,0:T(8,128)(2,1)} %bitcast.75), channel_id=1, source_target_pairs={{0,4},{4,0},{1,5},{5,1},{2,6},{6,2},{3,7},{7,3},{8,12},{12,8},{9,1... | collective-permute-start | bytes 12582920 | tf_op jit(solution)/shard_map/ppermute | solution.py:245
  98.1 48.3 %collective-permute-start.3 = (bf16[16,16,1024]{2,1,0:T(8,128)(2,1)S(1)}, bf16[16,16,1024]{2,1,0:T(8,128)(2,1)S(1)}, u32[]{:S(2)}, u32[]{:S(2)}) collective-permute-start(bf16[16,16,1024]{2,1,0:T(8,128)(2,1)S(1)} %gather_fusion.7), channel_id=1, source_target_pairs={{0,1},{1,2},{2,3},{3,0},{4,5},{5,6},{6,7},{7,4},{8,9},{9,10},{10,1... | collective-permute-start | bytes 1572872 | tf_op jit(solution)/shard_map/ppermute | solution.py:240
  102.4 55.4 %collective-permute-start.4 = (bf16[16,16,1024]{2,1,0:T(8,128)(2,1)S(1)}, bf16[16,16,1024]{2,1,0:T(8,128)(2,1)S(1)}, u32[]{:S(2)}, u32[]{:S(2)}) collective-permute-start(bf16[16,16,1024]{2,1,0:T(8,128)(2,1)S(1)} %gather_fusion.8), channel_id=1, source_target_pairs={{0,2},{1,3},{2,0},{3,1},{4,6},{5,7},{6,4},{7,5},{8,10},{9,11},{10,... | collective-permute-start | bytes 1572872 | tf_op jit(solution)/shard_map/ppermute | solution.py:240
  109.2 87.1 %collective-permute-start.5 = (bf16[16,16,1024]{2,1,0:T(8,128)(2,1)}, bf16[16,16,1024]{2,1,0:T(8,128)(2,1)}, u32[]{:S(2)}, u32[]{:S(2)}) collective-permute-start(bf16[16,16,1024]{2,1,0:T(8,128)(2,1)} %gather_fusion.9), channel_id=1, source_target_pairs={{0,3},{1,0},{2,1},{3,2},{4,7},{5,4},{6,5},{7,6},{8,11},{9,8},{10,9... | collective-permute-start | bytes 1572872 | tf_op jit(solution)/shard_map/ppermute | solution.py:240
  134.7 77.9 %collective-permute-start.1 = (bf16[16,16,1024]{2,1,0:T(8,128)(2,1)}, bf16[16,16,1024]{2,1,0:T(8,128)(2,1)S(1)}, u32[]{:S(2)}, u32[]{:S(2)}) collective-permute-start(bf16[16,16,1024]{2,1,0:T(8,128)(2,1)} %gather_fusion.3), channel_id=1, source_target_pairs={{0,2},{1,3},{2,0},{3,1},{4,6},{5,7},{6,4},{7,5},{8,10},{9,11},{10,... | collective-permute-start | bytes 1572872 | tf_op jit(solution)/shard_map/ppermute | solution.py:240
  146.5 66.2 %collective-permute-start.2 = (bf16[16,16,1024]{2,1,0:T(8,128)(2,1)}, bf16[16,16,1024]{2,1,0:T(8,128)(2,1)}, u32[]{:S(2)}, u32[]{:S(2)}) collective-permute-start(bf16[16,16,1024]{2,1,0:T(8,128)(2,1)} %gather_fusion.4), channel_id=1, source_target_pairs={{0,3},{1,0},{2,1},{3,2},{4,7},{5,4},{6,5},{7,6},{8,11},{9,8},{10,9... | collective-permute-start | bytes 1572872 | tf_op jit(solution)/shard_map/ppermute | solution.py:240
  157.8 54.8 %collective-permute-start = (bf16[16,16,1024]{2,1,0:T(8,128)(2,1)}, bf16[16,16,1024]{2,1,0:T(8,128)(2,1)}, u32[]{:S(2)}, u32[]{:S(2)}) collective-permute-start(bf16[16,16,1024]{2,1,0:T(8,128)(2,1)} %gather_fusion.2), channel_id=1, source_target_pairs={{0,1},{1,2},{2,3},{3,0},{4,5},{5,6},{6,7},{7,4},{8,9},{9,10},{10,1... | collective-permute-start | bytes 1572872 | tf_op jit(solution)/shard_map/ppermute | solution.py:240
  196.4 2.2 copy-start.1
  198.6 2.2 copy-start.2
  212.7 3.4 %copy-start.3 = (bf16[2,16,4,32,1024]{4,3,2,1,0:T(8,128)(2,1)S(1)}, bf16[2,16,4,32,1024]{4,3,2,1,0:T(8,128)(2,1)}, u32[]{:S(2)}) copy-start(bf16[2,16,4,32,1024]{4,3,2,1,0:T(8,128)(2,1)} %get-tuple-element.12.refs_7_) | copy-start | bytes 25165828
  225.8 1.4 copy-start.5
  227.2 1.4 copy-start.7
  228.5 1.0 copy-start.9
  229.5 20.4 %all-to-all-start.3 = ((bf16[4,256,256]{2,1,0:T(8,128)(2,1)}), bf16[4,256,256]{2,1,0:T(8,128)(2,1)S(1)}, u32[]{:S(2)}, u32[]{:S(2)}) async-start(bf16[4,256,256]{2,1,0:T(8,128)(2,1)} %shard_map.73), calls=%async_computation.3 | async-start | bytes 1048576 | tf_op jit(solution)/shard_map/all_to_all | solution.py:252
  233.0 3.4 %copy-start.4 = (bf16[2,16,4,32,1024]{4,3,2,1,0:T(8,128)(2,1)S(1)}, bf16[2,16,4,32,1024]{4,3,2,1,0:T(8,128)(2,1)}, u32[]{:S(2)}) copy-start(bf16[2,16,4,32,1024]{4,3,2,1,0:T(8,128)(2,1)} %get-tuple-element.12.refs_7_) | copy-start | bytes 25165828
  236.4 1.6 copy-start.6
  238.0 1.6 copy-start.8
  239.6 1.2 copy-start.10
Sparse Core Ops, SparseCore 0:
  26.4 70.9 all-gather.2

commit v8 on v7

--- a/solution.py
+++ b/solution.py
@@ -11,7 +11,7 @@
 SPANS_STEP = 2
 CHUNKS = 2
 PARTS = 2
-MIB = 1024 * 1024
+VMEM_BYTES = 62 * 1024 * 1024
 SPAN = ("y", "x", "z", "core")
 
 
@@ -20,10 +20,10 @@
     return w_ref[:, :, g, :, which * cols : (which + 1) * cols].reshape(width, cols)
 
 
-def rows_of(x_refs):
-    some = x_refs[0].shape[0] // SPANS_STEP
+def rows_of(x_refs, spans):
+    some = x_refs[0].shape[0] // spans
     return jnp.concatenate(
-        [x_ref[i * some : (i + 1) * some] for i in range(SPANS_STEP) for x_ref in x_refs], axis=0
+        [x_ref[i * some : (i + 1) * some] for i in range(spans) for x_ref in x_refs], axis=0
     )
 
 
@@ -41,7 +41,7 @@
         w_ref[core] = own_ref[...]
         w_ref[1 - core] = other_ref[...]
 
-    x = rows_of(x_refs)
+    x = rows_of(x_refs, SPANS_STEP)
     both = jnp.concatenate([now_ref[...], next_ref[...]], axis=0)
     row = lax.broadcasted_iota(jnp.int32, (rows, rows + SPAN_LEN), 0)
     col = lax.broadcasted_iota(jnp.int32, (rows, rows + SPAN_LEN), 1)
@@ -56,56 +56,61 @@
 
 
 def attend_kernel(*refs):
-    x_refs = refs[:-7]
-    q_ref, k_ref, v_ref, w_ref, out_ref, late_k_ref, late_v_ref = refs[-7:]
+    x_refs = refs[:-9]
+    q_ref, k_ref, v_ref, w_ref, out_ref, x_ref, late_k_ref, late_v_ref, total_ref = refs[-9:]
     f32, bf16 = jnp.float32, jnp.bfloat16
-    spans, width = SPANS_STEP, w_ref.shape[-1]
-    groups = w_ref.shape[2]
-    cols = width // groups
-    rows = spans * SPAN_LEN
+    width, cols = x_ref.shape[1], q_ref.shape[1]
+    spans = q_ref.shape[0] // SPAN_LEN
     early = k_ref.shape[0] // spans
     late = late_k_ref.shape[0] // spans
-    x = rows_of(x_refs)
-    total = jnp.zeros((rows, width), f32)
+    group, groups = pl.program_id(0), width // cols
     lane = lax.broadcasted_iota(jnp.int32, (SPAN_LEN, 128), 1)
     low = lane < HEAD_DIM
-    for g in range(groups):
-        for target, which in ((late_k_ref, 0), (late_v_ref, 1)):
-            target[...] = jnp.dot(
-                x, weight_of(w_ref, which, g), preferred_element_type=f32
-            ).astype(bf16)
-        context_rows = []
-        for i in range(spans):
-            pieces = []
-            for pair in range(cols // 128):
-                here = slice(pair * 128, pair * 128 + 128)
-                there = slice(g * cols + pair * 128, g * cols + pair * 128 + 128)
-                first, second = slice(i * early, (i + 1) * early), slice(i * late, (i + 1) * late)
-                qp = q_ref[i * SPAN_LEN : (i + 1) * SPAN_LEN, there]
-                zero = jnp.zeros_like(qp)
-                two = jnp.concatenate([jnp.where(low, qp, zero), jnp.where(low, zero, qp)], axis=0)
-                kp = jnp.concatenate([k_ref[first, there], late_k_ref[second, here]], axis=0)
-                vp = jnp.concatenate([v_ref[first, there], late_v_ref[second, here]], axis=0)
-                scores = lax.dot_general(
-                    two, kp, (((1,), (1,)), ((), ())), preferred_element_type=f32
-                ) * (HEAD_DIM ** -0.5)
-                top = jnp.max(scores, axis=1, keepdims=True)
-                raised = jnp.exp(scores - top)
-                weights = raised * (1.0 / jnp.sum(raised, axis=1, keepdims=True))
-                mixed = jnp.dot(weights.astype(bf16), vp, preferred_element_type=f32)
-                pieces.append(jnp.where(low, mixed[:SPAN_LEN], mixed[SPAN_LEN:]).astype(bf16))
-            context_rows.append(jnp.concatenate(pieces, axis=1))
-        context = jnp.concatenate(context_rows, axis=0)
-        total = total + lax.dot_general(
-            context, weight_of(w_ref, 3, g), (((1,), (1,)), ((), ())), preferred_element_type=f32
-        )
-    for g in range(groups):
-        out_ref[g] = total[:, g * cols : (g + 1) * cols].astype(bf16)
-
-
-def settings(room):
+
+    @pl.when(group == 0)
+    def _():
+        x_ref[...] = rows_of(x_refs, spans)
+        total_ref[...] = jnp.zeros_like(total_ref)
+
+    def weight(which):
+        return w_ref[:, :, 0, :, which * cols : (which + 1) * cols].reshape(width, cols)
+
+    for target, which in ((late_k_ref, 0), (late_v_ref, 1)):
+        target[...] = jnp.dot(x_ref[...], weight(which), preferred_element_type=f32).astype(bf16)
+    context_rows = []
+    for i in range(spans):
+        pieces = []
+        first, second = slice(i * early, (i + 1) * early), slice(i * late, (i + 1) * late)
+        for pair in range(cols // 128):
+            here = slice(pair * 128, pair * 128 + 128)
+            qp = q_ref[i * SPAN_LEN : (i + 1) * SPAN_LEN, here]
+            zero = jnp.zeros_like(qp)
+            two = jnp.concatenate([jnp.where(low, qp, zero), jnp.where(low, zero, qp)], axis=0)
+            kp = jnp.concatenate([k_ref[first, here], late_k_ref[second, here]], axis=0)
+            vp = jnp.concatenate([v_ref[first, here], late_v_ref[second, here]], axis=0)
+            scores = lax.dot_general(
+                two, kp, (((1,), (1,)), ((), ())), preferred_element_type=f32
+            ) * (HEAD_DIM ** -0.5)
+            top = jnp.max(scores, axis=1, keepdims=True)
+            raised = jnp.exp(scores - top)
+            weights = raised * (1.0 / jnp.sum(raised, axis=1, keepdims=True))
+            mixed = jnp.dot(weights.astype(bf16), vp, preferred_element_type=f32)
+            pieces.append(jnp.where(low, mixed[:SPAN_LEN], mixed[SPAN_LEN:]).astype(bf16))
+        context_rows.append(jnp.concatenate(pieces, axis=1))
+    context = jnp.concatenate(context_rows, axis=0)
+    total_ref[...] += lax.dot_general(
+        context, weight(3), (((1,), (1,)), ((), ())), preferred_element_type=f32
+    )
+
+    @pl.when(group == groups - 1)
+    def _():
+        for g in range(groups):
+            out_ref[g] = total_ref[:, g * cols : (g + 1) * cols].astype(bf16)
+
+
+def settings():
     return pltpu.CompilerParams(
-        dimension_semantics=("arbitrary",), vmem_limit_bytes=room * MIB
+        dimension_semantics=("arbitrary",), vmem_limit_bytes=VMEM_BYTES
     )
 
 
@@ -148,7 +153,7 @@
                 whole,
             ),
         ),
-        compiler_params=settings(30),
+        compiler_params=settings(),
         cost_estimate=pl.CostEstimate(
             flops=2 * spans * width * width * (2 * keys + SPAN_LEN),
             bytes_accessed=2 * (len(chunks) * chunks[0].size + 4 * weights.size),
@@ -160,33 +165,39 @@
 
 def attend(part, chunks, queries, keys, values, weights):
     held, width = chunks[0].shape
-    spans = queries.shape[0] // SPAN_LEN
-    some = held // spans
-    steps = spans // SPANS_STEP // PARTS
-    rows = SPANS_STEP * SPAN_LEN
-    early = keys.shape[0] // spans
+    here = queries.shape[0] // SPAN_LEN // PARTS
+    some = held // PARTS
+    rows = here * SPAN_LEN
+    early = keys.shape[0] // PARTS
     late = some * len(chunks)
     groups = weights.shape[2]
     cols = width // groups
 
-    def block(count):
-        return pl.BlockSpec((SPANS_STEP * count, width), lambda i: (part * steps + i, 0))
+    def columns(count):
+        return pl.BlockSpec((count, cols), lambda g: (part, g))
 
     return pl.pallas_call(
         attend_kernel,
-        out_shape=jax.ShapeDtypeStruct((groups, steps * rows, cols), jnp.bfloat16),
-        grid=(steps,),
-        in_specs=[block(some) for _ in chunks]
-        + [block(SPAN_LEN), block(early), block(early), pl.BlockSpec(memory_space=pltpu.VMEM)],
-        out_specs=pl.BlockSpec((groups, rows, cols), lambda i: (0, i, 0)),
+        out_shape=jax.ShapeDtypeStruct((groups, rows, cols), jnp.bfloat16),
+        grid=(groups,),
+        in_specs=[pl.BlockSpec((some, width), lambda g: (part, 0)) for _ in chunks]
+        + [
+            columns(rows),
+            columns(early),
+            columns(early),
+            pl.BlockSpec(weights.shape[:2] + (1,) + weights.shape[3:], lambda g: (0, 0, g, 0, 0)),
+        ],
+        out_specs=pl.BlockSpec((groups, rows, cols), lambda g: (0, 0, 0)),
         scratch_shapes=[
-            pltpu.VMEM((SPANS_STEP * late, cols), jnp.bfloat16),
-            pltpu.VMEM((SPANS_STEP * late, cols), jnp.bfloat16),
+            pltpu.VMEM((late, width), jnp.bfloat16),
+            pltpu.VMEM((late, cols), jnp.bfloat16),
+            pltpu.VMEM((late, cols), jnp.bfloat16),
+            pltpu.VMEM((rows, width), jnp.float32),
         ],
-        compiler_params=settings(30),
+        compiler_params=settings(),
         cost_estimate=pl.CostEstimate(
-            flops=2 * spans // PARTS * width * width * (2 * late + 6 * SPAN_LEN),
-            bytes_accessed=2 * (len(chunks) * chunks[0].size // PARTS + weights.size),
+            flops=2 * width * width * (2 * late + 6 * rows),
+            bytes_accessed=2 * (late * width + weights.size),
             transcendentals=0,
         ),
     )(*chunks, queries, keys, values, weights)

time: 280 us -> 267 us (0.954)
  the two profiles are of different devices: /device:TPU:4 before, /device:TPU:6 now
where the time goes in v8:
time: 267 us; the launch traced here: 266 us
  starting transfers between devices  76.4 us (29%)
  waiting for transfers between devices  74.9 us (28%)
  Pallas kernels  35.7 us (13%)
  local copies, waits for them, and re-layouts  31.7 us (12%)
  blocking collectives  31.5 us (12%)
  between operations  13.5 us (5%)
    all_to_all x2, waiting for transfers between devices, layer(): lax.all_to_all(pieces[CHUNKS * wanted + c], SPAN, split_axis=0, concat_ax...  50 us
    ppermute x6, starting transfers between devices, layer(): lax.ppermute(block, 'head', [(i, (i + step) % groups) for i in range(grou...  45.7 us
    pallas_call x2, Pallas kernels, attend(): pl.pallas_call(attend_kernel, out_shape=jax.ShapeDtypeStruct((groups, row...  20.3 us
    all_to_all x1, blocking collectives, layer(): lax.all_to_all(result, 'head', split_axis=0, concat_axis=0, tiled=True)  17.4 us
    gather x8, local copies, waits for them, and re-layouts, layer(): block = arrived[sources[(head + step) % groups]]  16.7 us
    all_to_all x2, starting transfers between devices, layer(): lax.all_to_all(pieces[CHUNKS * wanted + c], SPAN, split_axis=0, concat_ax...  15.8 us
    pallas_call x1, Pallas kernels, prepare(): pl.pallas_call(prepare_kernel, out_shape=(jax.ShapeDtypeStruct((spans * S...  15.4 us
    ppermute x6, waiting for transfers between devices, layer(): lax.ppermute(block, 'head', [(i, (i + step) % groups) for i in range(grou...  14.2 us
  transfers between devices with their start and end apart: 14, of which 8 were waited for; matrix products, arithmetic and copies ran while one was open for 11% of the time, Pallas kernels for 10%

profile of v8, /device:TPU:6, one launch (start us, length us, event | category | flops | bytes accessed | tf_op | source)
XLA Modules:
  0.0 265.9 jit_solution(2967091161173510290)
XLA Ops:
  6.5 0.0 copy-start
  6.5 0.0 all-gather.3.cloned.1.call-start
  6.5 1.0 copy-done
  7.6 0.1 constant_dynamic-slice_fusion
  7.7 0.1 copy.37
  7.7 0.7 constant_dynamic-slice_fusion.3
  8.5 0.7 constant_dynamic-slice_fusion.1
  9.2 3.3 %collective-permute-start.6 = (bf16[32,1024]{1,0:T(8,128)(2,1)S(1)}, bf16[32,1024]{1,0:T(8,128)(2,1)S(1)}, u32[]{:S(2)}, u32[]{:S(2)}) collective-permute-start(bf16[32,1024]{1,0:T(8,128)(2,1)S(1)} %get-tuple-element.14), channel_id=1, source_target_pairs={{0,1},{1,2},{2,3},{3,0},{4,5},{5,6},{6,7},{7,4},{8,9},{9,10},{10,1... | collective-permute-start | bytes 196616 | tf_op jit(solution)/shard_map/ppermute | solution.py:225
  12.6 5.4 %collective-permute-start.7 = (bf16[32,1024]{1,0:T(8,128)(2,1)S(1)}, bf16[32,1024]{1,0:T(8,128)(2,1)S(1)}, u32[]{:S(2)}, u32[]{:S(2)}) collective-permute-start(bf16[32,1024]{1,0:T(8,128)(2,1)S(1)} %get-tuple-element.14), channel_id=1, source_target_pairs={{0,2},{1,3},{2,0},{3,1},{4,6},{5,7},{6,4},{7,5},{8,10},{9,11},{10,... | collective-permute-start | bytes 196616 | tf_op jit(solution)/shard_map/ppermute | solution.py:225
  18.0 2.7 %collective-permute-start.8 = (bf16[32,1024]{1,0:T(8,128)(2,1)S(1)}, bf16[32,1024]{1,0:T(8,128)(2,1)S(1)}, u32[]{:S(2)}, u32[]{:S(2)}) collective-permute-start(bf16[32,1024]{1,0:T(8,128)(2,1)S(1)} %get-tuple-element.14), channel_id=1, source_target_pairs={{0,3},{1,0},{2,1},{3,2},{4,7},{5,4},{6,5},{7,6},{8,11},{9,8},{10,9... | collective-permute-start | bytes 196616 | tf_op jit(solution)/shard_map/ppermute | solution.py:225
  20.7 0.0 collective-permute-done.6
  20.7 1.4 collective-permute-done.7
  22.1 2.8 %collective-permute-done.8 = bf16[32,1024]{1,0:T(8,128)(2,1)S(1)} collective-permute-done((bf16[32,1024]{1,0:T(8,128)(2,1)S(1)}, bf16[32,1024]{1,0:T(8,128)(2,1)S(1)}, u32[]{:S(2)}, u32[]{:S(2)}) %collective-permute-start.8) | collective-permute-done | bytes 65568 | tf_op jit(solution)/shard_map/ppermute | solution.py:225
  24.9 1.3 gather_fusion.10
  26.2 0.0 all-gather.3.cloned.1.call-update
  26.2 0.8 fusion.13
  27.0 0.1 copy.32
  27.1 0.1 eq.26
  27.2 0.1 copy.33
  27.3 0.1 broadcast_in_dim.14
  27.4 0.1 select_reduce_fusion
  27.5 0.1 copy.34
  27.6 14.2 %all_to_all.29 = s32[64,1,1]{2,1,0:T(1,128)S(1)} all-to-all(s32[64,1,1]{2,1,0:T(1,128)S(1)} %copy.34), channel_id=1, replica_groups=mesh['y'=4,'x'=4,'z'=2,'core'=2,'head'=4] {'y','x','z','core'}, dimensions={0} | all-to-all | bytes 512 | tf_op jit(solution)/shard_map/all_to_all | solution.py:234
  41.8 1.2 multiply_reduce_fusion
  43.0 4.3 %gather_fusion.5 = bf16[64,16,1024]{2,1,0:T(8,128)(2,1)} fusion(bf16[128,16,1024]{2,1,0:T(8,128)(2,1)} %bitcast.72, s32[1024]{0:T(1024)S(1)} %pad_clamp_fusion.1), kind=kCustom, calls=%fused_computation.5 | custom fusion | bytes 4194560 | tf_op jit(solution)/shard_map/gather | solution.py:242
  47.3 6.3 %all-to-all-start.2 = ((bf16[64,16,1024]{2,1,0:T(8,128)(2,1)}), bf16[64,16,1024]{2,1,0:T(8,128)(2,1)S(1)}, u32[]{:S(2)}, u32[]{:S(2)}) async-start(bf16[64,16,1024]{2,1,0:T(8,128)(2,1)} %gather_fusion.5), calls=%async_computation.2 | async-start | bytes 4194304 | tf_op jit(solution)/shard_map/all_to_all | solution.py:241
  53.6 4.2 %gather_fusion = bf16[64,16,1024]{2,1,0:T(8,128)(2,1)} fusion(bf16[128,16,1024]{2,1,0:T(8,128)(2,1)} %bitcast.73, s32[1024]{0:T(1024)S(1)} %pad_clamp_fusion.6), kind=kCustom, calls=%fused_computation | custom fusion | bytes 4194560 | tf_op jit(solution)/shard_map/gather | solution.py:242
  57.8 27.7 %all-to-all-done.2 = bf16[64,16,1024]{2,1,0:T(8,128)(2,1)S(1)} async-done(((bf16[64,16,1024]{2,1,0:T(8,128)(2,1)}), bf16[64,16,1024]{2,1,0:T(8,128)(2,1)S(1)}, u32[]{:S(2)}, u32[]{:S(2)}) %all-to-all-start.2) | async-done | bytes 2097184 | tf_op jit(solution)/shard_map/all_to_all | solution.py:241
  85.5 9.5 %all-to-all-start.1 = ((bf16[64,16,1024]{2,1,0:T(8,128)(2,1)}), bf16[64,16,1024]{2,1,0:T(8,128)(2,1)}, u32[]{:S(2)}, u32[]{:S(2)}) async-start(bf16[64,16,1024]{2,1,0:T(8,128)(2,1)} %gather_fusion), calls=%async_computation.1 | async-start | bytes 4194304 | tf_op jit(solution)/shard_map/all_to_all | solution.py:241
  95.0 2.4 all-gather.3.cloned.1.call-done
  97.4 0.0 collective-permute-start.9
  97.4 0.1 reshape_reshape_squeeze.3
  97.5 1.4 gather_fusion.7
  98.9 2.0 collective-permute-start.3
  100.9 1.4 gather_fusion.8
  102.3 3.8 %collective-permute-start.4 = (bf16[16,16,1024]{2,1,0:T(8,128)(2,1)}, bf16[16,16,1024]{2,1,0:T(8,128)(2,1)}, u32[]{:S(2)}, u32[]{:S(2)}) collective-permute-start(bf16[16,16,1024]{2,1,0:T(8,128)(2,1)} %gather_fusion.8), channel_id=1, source_target_pairs={{0,2},{1,3},{2,0},{3,1},{4,6},{5,7},{6,4},{7,5},{8,10},{9,11},{10,... | collective-permute-start | bytes 1572872 | tf_op jit(solution)/shard_map/ppermute | solution.py:251
  106.1 1.4 gather_fusion.9
  107.5 2.3 collective-permute-start.5
  109.7 22.3 %all-to-all-done.1 = bf16[64,16,1024]{2,1,0:T(8,128)(2,1)} async-done(((bf16[64,16,1024]{2,1,0:T(8,128)(2,1)}), bf16[64,16,1024]{2,1,0:T(8,128)(2,1)}, u32[]{:S(2)}, u32[]{:S(2)}) %all-to-all-start.1) | async-done | bytes 2097184 | tf_op jit(solution)/shard_map/all_to_all | solution.py:241
  132.0 2.2 gather_fusion.3
  134.2 3.5 %collective-permute-start.1 = (bf16[16,16,1024]{2,1,0:T(8,128)(2,1)S(1)}, bf16[16,16,1024]{2,1,0:T(8,128)(2,1)}, u32[]{:S(2)}, u32[]{:S(2)}) collective-permute-start(bf16[16,16,1024]{2,1,0:T(8,128)(2,1)S(1)} %gather_fusion.3), channel_id=1, source_target_pairs={{0,2},{1,3},{2,0},{3,1},{4,6},{5,7},{6,4},{7,5},{8,10},{9,11},{10,... | collective-permute-start | bytes 1572872 | tf_op jit(solution)/shard_map/ppermute | solution.py:251
  137.7 3.0 %gather_fusion.4 = bf16[16,16,1024]{2,1,0:T(8,128)(2,1)} fusion(bf16[64,16,1024]{2,1,0:T(8,128)(2,1)} %all-to-all-done.1, s32[1024]{0:T(1024)S(1)} %pad_clamp_fusion.2), kind=kCustom, calls=%fused_computation.4 | custom fusion | bytes 1048640 | tf_op jit(solution)/shard_map/gather | solution.py:249
  140.7 3.0 %gather_fusion.2 = bf16[16,16,1024]{2,1,0:T(8,128)(2,1)} fusion(bf16[64,16,1024]{2,1,0:T(8,128)(2,1)} %all-to-all-done.1, s32[1024]{0:T(1024)S(1)} %pad_clamp_fusion.4), kind=kCustom, calls=%fused_computation.2 | custom fusion | bytes 1048640 | tf_op jit(solution)/shard_map/gather | solution.py:249
  143.6 2.9 %collective-permute-done.3 = bf16[16,16,1024]{2,1,0:T(8,128)(2,1)} collective-permute-done((bf16[16,16,1024]{2,1,0:T(8,128)(2,1)}, bf16[16,16,1024]{2,1,0:T(8,128)(2,1)}, u32[]{:S(2)}, u32[]{:S(2)}) %collective-permute-start.3) | collective-permute-done | bytes 524320 | tf_op jit(solution)/shard_map/ppermute | solution.py:251
  146.5 0.0 collective-permute-start.2
  146.5 11.4 %collective-permute-done.4 = bf16[16,16,1024]{2,1,0:T(8,128)(2,1)} collective-permute-done((bf16[16,16,1024]{2,1,0:T(8,128)(2,1)}, bf16[16,16,1024]{2,1,0:T(8,128)(2,1)}, u32[]{:S(2)}, u32[]{:S(2)}) %collective-permute-start.4) | collective-permute-done | bytes 524320 | tf_op jit(solution)/shard_map/ppermute | solution.py:251
  157.9 34.1 %collective-permute-start = (bf16[16,16,1024]{2,1,0:T(8,128)(2,1)}, bf16[16,16,1024]{2,1,0:T(8,128)(2,1)}, u32[]{:S(2)}, u32[]{:S(2)}) collective-permute-start(bf16[16,16,1024]{2,1,0:T(8,128)(2,1)} %gather_fusion.2), channel_id=1, source_target_pairs={{0,1},{1,2},{2,3},{3,0},{4,5},{5,6},{6,7},{7,4},{8,9},{9,10},{10,1... | collective-permute-start | bytes 1572872 | tf_op jit(solution)/shard_map/ppermute | solution.py:251
  192.0 0.7 pad_add_fusion.where_ref
  192.7 1.4 gather_fusion.6
  194.1 3.0 %gather_fusion.1 = bf16[16,16,1024]{2,1,0:T(8,128)(2,1)} fusion(bf16[64,16,1024]{2,1,0:T(8,128)(2,1)} %all-to-all-done.1, s32[1024]{0:T(1024)S(1)} %pad_clamp_fusion.5), kind=kCustom, calls=%fused_computation.1 | custom fusion | bytes 1048640 | tf_op jit(solution)/shard_map/gather | solution.py:249
  197.1 0.0 collective-permute-done.5
  197.1 0.0 collective-permute-done.9.refs_7_
  197.1 15.4 %prepare.1 = (bf16[512,1024]{1,0:T(8,128)(2,1)}, bf16[1024,1024]{1,0:T(8,128)(2,1)}, bf16[1024,1024]{1,0:T(8,128)(2,1)}, bf16[2,16,4,32,1024]{4,3,2,1,0:T(8,128)(2,1)}) custom-call(s32[2]{0:T(128)} %pad_add_fusion.where_ref, bf16[256,1024]{1,0:T(8,128)(2,1)} %bitcast.77, bf16[256,1024]{1,0:T(8,128)(2,1)} %bitcast.19.refs_1_, ...), custom_call_target="tpu_custom_call" | custom-call | flops 5368709120 | bytes 18874368 | tf_op jit(solution)/shard_map/prepare/pallas_call | solution.py:131
  212.5 0.0 collective-permute-done.1
  212.5 0.0 collective-permute-done.2
  212.5 0.0 collective-permute-done
  212.5 10.2 %shard_map.73 = bf16[4,256,256]{2,1,0:T(8,128)(2,1)} custom-call(bf16[256,1024]{1,0:T(8,128)(2,1)} %bitcast.75, bf16[256,1024]{1,0:T(8,128)(2,1)} %bitcast.8.refs_1_, bf16[256,1024]{1,0:T(8,128)(2,1)} %bitcast.11.refs_2_, bf16[256,1024]{1,0:T(8,128)(2,1)} %bitcast.14.refs_3_, bf16[512,1024]{1,0:T(8,128)(2,1)} %get-tuple-element.9.refs_4_, ...), custom_call_target="tpu_custom_call" | custom-call | flops 5368709120 | bytes 9437184 | tf_op jit(solution)/shard_map/pallas_call | solution.py:179
  222.7 3.5 %all-to-all-start.3 = ((bf16[4,256,256]{2,1,0:T(8,128)(2,1)}), bf16[4,256,256]{2,1,0:T(8,128)(2,1)S(1)}, u32[]{:S(2)}, u32[]{:S(2)}) async-start(bf16[4,256,256]{2,1,0:T(8,128)(2,1)} %shard_map.73), calls=%async_computation.3 | async-start | bytes 1048576 | tf_op jit(solution)/shard_map/all_to_all | solution.py:263
  226.2 10.2 %shard_map.74 = bf16[4,256,256]{2,1,0:T(8,128)(2,1)} custom-call(bf16[256,1024]{1,0:T(8,128)(2,1)} %bitcast.76, bf16[256,1024]{1,0:T(8,128)(2,1)} %bitcast.8.refs_1_, bf16[256,1024]{1,0:T(8,128)(2,1)} %bitcast.11.refs_2_, bf16[256,1024]{1,0:T(8,128)(2,1)} %bitcast.14.refs_3_, bf16[512,1024]{1,0:T(8,128)(2,1)} %get-tuple-element.9.refs_4_, ...), custom_call_target="tpu_custom_call" | custom-call | flops 5368709120 | bytes 9437184 | tf_op jit(solution)/shard_map/pallas_call | solution.py:179
  236.3 4.0 %all-to-all-done.3 = bf16[4,256,256]{2,1,0:T(8,128)(2,1)S(1)} async-done(((bf16[4,256,256]{2,1,0:T(8,128)(2,1)}), bf16[4,256,256]{2,1,0:T(8,128)(2,1)S(1)}, u32[]{:S(2)}, u32[]{:S(2)}) %all-to-all-start.3) | async-done | bytes 524320 | tf_op jit(solution)/shard_map/all_to_all | solution.py:263
  240.3 17.4 %all_to_all.30 = bf16[4,256,256]{2,1,0:T(8,128)(2,1)S(1)} all-to-all(bf16[4,256,256]{2,1,0:T(8,128)(2,1)} %shard_map.74), channel_id=1, replica_groups=mesh['y'=4,'x'=4,'z'=2,'core'=2,'head'=4] {'head'}, dimensions={0} | all-to-all | bytes 1048576 | tf_op jit(solution)/shard_map/all_to_all | solution.py:263
  257.7 0.1 pad_maximum_fusion
  257.8 0.1 slice.34
  257.8 1.2 concatenate.11
  (12 shorter events, 0.1 us)
Async XLA Ops:
  6.5 1.0 copy-start
  6.5 90.8 %all-gather.3.cloned.1.call-start = ((), (), s32[]{:S(2)}) async-start(), calls=%async_computation.5 | async-start | bytes 4456448 | tf_op jit(solution)/shard_map/all_gather | solution.py:235
  9.2 11.4 %collective-permute-start.6 = (bf16[32,1024]{1,0:T(8,128)(2,1)S(1)}, bf16[32,1024]{1,0:T(8,128)(2,1)S(1)}, u32[]{:S(2)}, u32[]{:S(2)}) collective-permute-start(bf16[32,1024]{1,0:T(8,128)(2,1)S(1)} %get-tuple-element.14), channel_id=1, source_target_pairs={{0,1},{1,2},{2,3},{3,0},{4,5},{5,6},{6,7},{7,4},{8,9},{9,10},{10,1... | collective-permute-start | bytes 196616 | tf_op jit(solution)/shard_map/ppermute | solution.py:225
  12.6 9.5 %collective-permute-start.7 = (bf16[32,1024]{1,0:T(8,128)(2,1)S(1)}, bf16[32,1024]{1,0:T(8,128)(2,1)S(1)}, u32[]{:S(2)}, u32[]{:S(2)}) collective-permute-start(bf16[32,1024]{1,0:T(8,128)(2,1)S(1)} %get-tuple-element.14), channel_id=1, source_target_pairs={{0,2},{1,3},{2,0},{3,1},{4,6},{5,7},{6,4},{7,5},{8,10},{9,11},{10,... | collective-permute-start | bytes 196616 | tf_op jit(solution)/shard_map/ppermute | solution.py:225
  18.0 6.9 %collective-permute-start.8 = (bf16[32,1024]{1,0:T(8,128)(2,1)S(1)}, bf16[32,1024]{1,0:T(8,128)(2,1)S(1)}, u32[]{:S(2)}, u32[]{:S(2)}) collective-permute-start(bf16[32,1024]{1,0:T(8,128)(2,1)S(1)} %get-tuple-element.14), channel_id=1, source_target_pairs={{0,3},{1,0},{2,1},{3,2},{4,7},{5,4},{6,5},{7,6},{8,11},{9,8},{10,9... | collective-permute-start | bytes 196616 | tf_op jit(solution)/shard_map/ppermute | solution.py:225
  47.3 38.2 %all-to-all-start.2 = ((bf16[64,16,1024]{2,1,0:T(8,128)(2,1)}), bf16[64,16,1024]{2,1,0:T(8,128)(2,1)S(1)}, u32[]{:S(2)}, u32[]{:S(2)}) async-start(bf16[64,16,1024]{2,1,0:T(8,128)(2,1)} %gather_fusion.5), calls=%async_computation.2 | async-start | bytes 4194304 | tf_op jit(solution)/shard_map/all_to_all | solution.py:241
  85.5 46.5 %all-to-all-start.1 = ((bf16[64,16,1024]{2,1,0:T(8,128)(2,1)}), bf16[64,16,1024]{2,1,0:T(8,128)(2,1)}, u32[]{:S(2)}, u32[]{:S(2)}) async-start(bf16[64,16,1024]{2,1,0:T(8,128)(2,1)} %gather_fusion), calls=%async_computation.1 | async-start | bytes 4194304 | tf_op jit(solution)/shard_map/all_to_all | solution.py:241
  97.4 99.7 %collective-permute-start.9 = (bf16[16,4,32,1024]{3,2,1,0:T(8,128)(2,1)}, bf16[16,4,32,1024]{3,2,1,0:T(8,128)(2,1)}, u32[]{:S(2)}, u32[]{:S(2)}) collective-permute-start(bf16[16,4,32,1024]{3,2,1,0:T(8,128)(2,1)} %bitcast.83), channel_id=1, source_target_pairs={{0,4},{4,0},{1,5},{5,1},{2,6},{6,2},{3,7},{7,3},{8,12},{12,8},{9,1... | collective-permute-start | bytes 12582920 | tf_op jit(solution)/shard_map/ppermute | solution.py:256
  98.9 47.6 %collective-permute-start.3 = (bf16[16,16,1024]{2,1,0:T(8,128)(2,1)}, bf16[16,16,1024]{2,1,0:T(8,128)(2,1)}, u32[]{:S(2)}, u32[]{:S(2)}) collective-permute-start(bf16[16,16,1024]{2,1,0:T(8,128)(2,1)} %gather_fusion.7), channel_id=1, source_target_pairs={{0,1},{1,2},{2,3},{3,0},{4,5},{5,6},{6,7},{7,4},{8,9},{9,10},{10,1... | collective-permute-start | bytes 1572872 | tf_op jit(solution)/shard_map/ppermute | solution.py:251
  102.3 55.6 %collective-permute-start.4 = (bf16[16,16,1024]{2,1,0:T(8,128)(2,1)}, bf16[16,16,1024]{2,1,0:T(8,128)(2,1)}, u32[]{:S(2)}, u32[]{:S(2)}) collective-permute-start(bf16[16,16,1024]{2,1,0:T(8,128)(2,1)} %gather_fusion.8), channel_id=1, source_target_pairs={{0,2},{1,3},{2,0},{3,1},{4,6},{5,7},{6,4},{7,5},{8,10},{9,11},{10,... | collective-permute-start | bytes 1572872 | tf_op jit(solution)/shard_map/ppermute | solution.py:251
  107.5 89.6 %collective-permute-start.5 = (bf16[16,16,1024]{2,1,0:T(8,128)(2,1)}, bf16[16,16,1024]{2,1,0:T(8,128)(2,1)}, u32[]{:S(2)}, u32[]{:S(2)}) collective-permute-start(bf16[16,16,1024]{2,1,0:T(8,128)(2,1)} %gather_fusion.9), channel_id=1, source_target_pairs={{0,3},{1,0},{2,1},{3,2},{4,7},{5,4},{6,5},{7,6},{8,11},{9,8},{10,9... | collective-permute-start | bytes 1572872 | tf_op jit(solution)/shard_map/ppermute | solution.py:251
  134.2 78.3 %collective-permute-start.1 = (bf16[16,16,1024]{2,1,0:T(8,128)(2,1)S(1)}, bf16[16,16,1024]{2,1,0:T(8,128)(2,1)}, u32[]{:S(2)}, u32[]{:S(2)}) collective-permute-start(bf16[16,16,1024]{2,1,0:T(8,128)(2,1)S(1)} %gather_fusion.3), channel_id=1, source_target_pairs={{0,2},{1,3},{2,0},{3,1},{4,6},{5,7},{6,4},{7,5},{8,10},{9,11},{10,... | collective-permute-start | bytes 1572872 | tf_op jit(solution)/shard_map/ppermute | solution.py:251
  146.5 66.0 %collective-permute-start.2 = (bf16[16,16,1024]{2,1,0:T(8,128)(2,1)}, bf16[16,16,1024]{2,1,0:T(8,128)(2,1)}, u32[]{:S(2)}, u32[]{:S(2)}) collective-permute-start(bf16[16,16,1024]{2,1,0:T(8,128)(2,1)} %gather_fusion.4), channel_id=1, source_target_pairs={{0,3},{1,0},{2,1},{3,2},{4,7},{5,4},{6,5},{7,6},{8,11},{9,8},{10,9... | collective-permute-start | bytes 1572872 | tf_op jit(solution)/shard_map/ppermute | solution.py:251
  157.9 54.6 %collective-permute-start = (bf16[16,16,1024]{2,1,0:T(8,128)(2,1)}, bf16[16,16,1024]{2,1,0:T(8,128)(2,1)}, u32[]{:S(2)}, u32[]{:S(2)}) collective-permute-start(bf16[16,16,1024]{2,1,0:T(8,128)(2,1)} %gather_fusion.2), channel_id=1, source_target_pairs={{0,1},{1,2},{2,3},{3,0},{4,5},{5,6},{6,7},{7,4},{8,9},{9,10},{10,1... | collective-permute-start | bytes 1572872 | tf_op jit(solution)/shard_map/ppermute | solution.py:251
  222.7 17.6 %all-to-all-start.3 = ((bf16[4,256,256]{2,1,0:T(8,128)(2,1)}), bf16[4,256,256]{2,1,0:T(8,128)(2,1)S(1)}, u32[]{:S(2)}, u32[]{:S(2)}) async-start(bf16[4,256,256]{2,1,0:T(8,128)(2,1)} %shard_map.73), calls=%async_computation.3 | async-start | bytes 1048576 | tf_op jit(solution)/shard_map/all_to_all | solution.py:263
Sparse Core Ops, SparseCore 0:
  26.4 70.9 all-gather.2

commit v9 on v8

--- a/solution.py
+++ b/solution.py
@@ -236,15 +236,37 @@
     piece = encodings.shape[1] // CHUNKS
     pieces = encodings.reshape(-1, piece, width)
     sources = shard_ids.reshape(groups, -1)
+    flat = ("y", "x", "core")
+    z = lax.axis_index("z")
+    depth_y, depth_x, depth_z, cores = (lax.axis_size(axis) for axis in SPAN)
+    by_plane = wanted.reshape(depth_y, depth_x, depth_z, cores).transpose(2, 0, 1, 3)
+    by_plane = by_plane.reshape(depth_z, -1)
+    staying, leaving = by_plane[z], by_plane[1 - z]
+    sources = (
+        sources // 4 * 2
+        + sources % 2
+        + jnp.where(sources // 2 % 2 == z, 0, by_plane.shape[1])
+    )
+    crossings = (
+        [(p * groups + h, (1 - p) * groups + h) for p in (0, 1) for h in range(groups)],
+        [
+            (p * groups + h, (1 - p) * groups + (h + (1 if p else -1)) % groups)
+            for p in (0, 1)
+            for h in range(groups)
+        ],
+    )
+
+    def exchange(block):
+        return lax.all_to_all(block, flat, split_axis=0, concat_axis=0, tiled=True)
+
     owned = []
     for c in range(CHUNKS):
-        arrived = lax.all_to_all(
-            pieces[CHUNKS * wanted + c],
-            SPAN,
-            split_axis=0,
-            concat_axis=0,
-            tiled=True,
+        crossed = lax.ppermute(
+            pieces[CHUNKS * leaving + c], ("z", "head"), crossings[c % 2]
         )
+        same = exchange(pieces[CHUNKS * staying + c])
+        other = exchange(crossed)
+        arrived = jnp.concatenate([same, other], axis=0)
         for step in range(groups):
             block = arrived[sources[(head + step) % groups]]
             if step:

time: 267 us -> 306 us (1.15)
  the two profiles are of different devices: /device:TPU:6 before, /device:TPU:2 now
where the time goes in v9:
time: 306 us; the launch traced here: 305 us
  waiting for transfers between devices  114 us (37%)
  starting transfers between devices  83.6 us (27%)
  local copies, waits for them, and re-layouts  38.7 us (13%)
  Pallas kernels  35.7 us (12%)
  blocking collectives  17.1 us (6%)
  between operations  13.7 us (4%)
    ppermute x6, waiting for transfers between devices, layer(): lax.ppermute(block, 'head', [(i, (i + step) % groups) for i in range(grou...  40.6 us
    ppermute x6, starting transfers between devices, layer(): lax.ppermute(block, 'head', [(i, (i + step) % groups) for i in range(grou...  32.9 us
    all_gather x1, waiting for transfers between devices, layer(): weights = lax.all_gather(stacked, ('y', 'x'), axis=0, tiled=True)  32.5 us
    all_to_all x4, starting transfers between devices, exchange(): return lax.all_to_all(block, flat, split_axis=0, concat_axis=0, tiled=True)  22.1 us
    pallas_call x2, Pallas kernels, attend(): pl.pallas_call(attend_kernel, out_shape=jax.ShapeDtypeStruct((groups, row...  20.3 us
    all_to_all x1, blocking collectives, layer(): lax.all_to_all(result, 'head', split_axis=0, concat_axis=0, tiled=True)  17.1 us
    all_to_all x4, waiting for transfers between devices, exchange(): return lax.all_to_all(block, flat, split_axis=0, concat_axis=0, tiled=True)  16 us
    pallas_call x1, Pallas kernels, prepare(): pl.pallas_call(prepare_kernel, out_shape=(jax.ShapeDtypeStruct((spans * S...  15.4 us
  transfers between devices with their start and end apart: 19, of which 12 were waited for; matrix products, arithmetic and copies ran while one was open for 12% of the time, Pallas kernels for 8%

profile of v9, /device:TPU:2, one launch (start us, length us, event | category | flops | bytes accessed | tf_op | source)
XLA Modules:
  0.0 304.8 jit_solution(18357033313150261338)
XLA Ops:
  6.5 1.0 copy-done
  7.6 0.1 constant_dynamic-slice_fusion
  7.7 0.7 constant_dynamic-slice_fusion.3
  8.5 0.7 constant_dynamic-slice_fusion.1
  9.2 3.3 %collective-permute-start.8 = (bf16[32,1024]{1,0:T(8,128)(2,1)S(1)}, bf16[32,1024]{1,0:T(8,128)(2,1)S(1)}, u32[]{:S(2)}, u32[]{:S(2)}) collective-permute-start(bf16[32,1024]{1,0:T(8,128)(2,1)S(1)} %get-tuple-element.14), channel_id=1, source_target_pairs={{0,1},{1,2},{2,3},{3,0},{4,5},{5,6},{6,7},{7,4},{8,9},{9,10},{10,1... | collective-permute-start | bytes 196616 | tf_op jit(solution)/shard_map/ppermute | solution.py:225
  12.6 5.4 %collective-permute-start.9 = (bf16[32,1024]{1,0:T(8,128)(2,1)S(1)}, bf16[32,1024]{1,0:T(8,128)(2,1)S(1)}, u32[]{:S(2)}, u32[]{:S(2)}) collective-permute-start(bf16[32,1024]{1,0:T(8,128)(2,1)S(1)} %get-tuple-element.14), channel_id=1, source_target_pairs={{0,2},{1,3},{2,0},{3,1},{4,6},{5,7},{6,4},{7,5},{8,10},{9,11},{10,... | collective-permute-start | bytes 196616 | tf_op jit(solution)/shard_map/ppermute | solution.py:225
  18.0 2.7 collective-permute-start.10
  20.7 1.4 collective-permute-done.9
  22.1 2.8 collective-permute-done.10
  24.9 1.3 gather_fusion.12
  26.2 0.8 fusion.26
  27.1 0.1 eq.35
  27.3 0.1 broadcast_in_dim.20
  27.4 0.1 select_reduce_fusion
  27.5 0.7 copy.32
  28.2 8.0 %all-to-all-start = ((s32[64,1,1]{2,1,0:T(1,128)}), s32[64,1,1]{2,1,0:T(1,128)S(1)}, u32[]{:S(2)}, u32[]{:S(2)}) async-start(s32[64,1,1]{2,1,0:T(1,128)} %copy.32), calls=%async_computation | async-start | bytes 65536 | tf_op jit(solution)/shard_map/all_to_all | solution.py:234
  36.3 7.1 %all-to-all-done = s32[64,1,1]{2,1,0:T(1,128)S(1)} async-done(((s32[64,1,1]{2,1,0:T(1,128)}), s32[64,1,1]{2,1,0:T(1,128)S(1)}, u32[]{:S(2)}, u32[]{:S(2)}) %all-to-all-start) | async-done | bytes 288 | tf_op jit(solution)/shard_map/all_to_all | solution.py:234
  43.3 1.2 reduce
  44.6 0.1 reshape.280
  44.8 3.8 %gather_fusion.6 = bf16[32,16,1024]{2,1,0:T(8,128)(2,1)} fusion(bf16[128,16,1024]{2,1,0:T(8,128)(2,1)} %bitcast.81, s32[1024]{0:T(1024)S(1)} %pad_clamp_fusion.2), kind=kCustom, calls=%fused_computation.6 | custom fusion | bytes 2097280 | tf_op jit(solution)/shard_map/gather | solution.py:267
  48.6 5.0 %all-to-all-start.3 = ((bf16[32,16,1024]{2,1,0:T(8,128)(2,1)}), bf16[32,16,1024]{2,1,0:T(8,128)(2,1)S(1)}, u32[]{:S(2)}, u32[]{:S(2)}) async-start(bf16[32,16,1024]{2,1,0:T(8,128)(2,1)} %gather_fusion.6), calls=%async_computation.3 | async-start | bytes 2097152 | tf_op jit(solution)/shard_map/all_to_all | solution.py:260
  53.7 32.5 %all-gather.3.cloned.1.call-done = bf16[64,32,1024]{2,1,0:T(8,128)(2,1)} async-done(((bf16[4,32,1024]{2,1,0:T(8,128)(2,1)}), bf16[64,32,1024]{2,1,0:T(8,128)(2,1)}) %all-gather.3.cloned.1.call-update) | async-done | bytes 4194320 | tf_op jit(solution)/shard_map/all_gather | solution.py:235
  86.1 3.8 %gather_fusion.7 = bf16[32,16,1024]{2,1,0:T(8,128)(2,1)} fusion(bf16[128,16,1024]{2,1,0:T(8,128)(2,1)} %bitcast.82, s32[1024]{0:T(1024)S(1)} %pad_clamp_fusion.1), kind=kCustom, calls=%fused_computation.7 | custom fusion | bytes 2097280 | tf_op jit(solution)/shard_map/gather | solution.py:265
  89.9 0.6 collective-permute-start.4
  90.5 3.8 %gather_fusion = bf16[32,16,1024]{2,1,0:T(8,128)(2,1)} fusion(bf16[128,16,1024]{2,1,0:T(8,128)(2,1)} %bitcast.83, s32[1024]{0:T(1024)S(1)} %pad_clamp_fusion.8), kind=kCustom, calls=%fused_computation | custom fusion | bytes 2097280 | tf_op jit(solution)/shard_map/gather | solution.py:267
  94.3 5.9 %all-to-all-start.1 = ((bf16[32,16,1024]{2,1,0:T(8,128)(2,1)}), bf16[32,16,1024]{2,1,0:T(8,128)(2,1)S(1)}, u32[]{:S(2)}, u32[]{:S(2)}) async-start(bf16[32,16,1024]{2,1,0:T(8,128)(2,1)} %gather_fusion), calls=%async_computation.1 | async-start | bytes 2097152 | tf_op jit(solution)/shard_map/all_to_all | solution.py:260
  100.2 3.8 %gather_fusion.1 = bf16[32,16,1024]{2,1,0:T(8,128)(2,1)} fusion(bf16[128,16,1024]{2,1,0:T(8,128)(2,1)} %bitcast.84, s32[1024]{0:T(1024)S(1)} %pad_clamp_fusion.7), kind=kCustom, calls=%fused_computation.1 | custom fusion | bytes 2097280 | tf_op jit(solution)/shard_map/gather | solution.py:265
  104.0 3.4 %collective-permute-start = (bf16[32,16,1024]{2,1,0:T(8,128)(2,1)}, bf16[32,16,1024]{2,1,0:T(8,128)(2,1)}, u32[]{:S(2)}, u32[]{:S(2)}) collective-permute-start(bf16[32,16,1024]{2,1,0:T(8,128)(2,1)} %gather_fusion.1), channel_id=1, source_target_pairs={{0,11},{1,8},{2,9},{3,10},{8,1},{9,2},{10,3},{11,0},{4,15},{5,12},... | collective-permute-start | bytes 3145736 | tf_op jit(solution)/shard_map/ppermute | solution.py:264
  107.4 8.8 %all-to-all-done.1 = bf16[32,16,1024]{2,1,0:T(8,128)(2,1)S(1)} async-done(((bf16[32,16,1024]{2,1,0:T(8,128)(2,1)}), bf16[32,16,1024]{2,1,0:T(8,128)(2,1)S(1)}, u32[]{:S(2)}, u32[]{:S(2)}) %all-to-all-start.1) | async-done | bytes 1048608 | tf_op jit(solution)/shard_map/all_to_all | solution.py:260
  116.2 5.5 %all-to-all-start.4 = ((bf16[32,16,1024]{2,1,0:T(8,128)(2,1)}), bf16[32,16,1024]{2,1,0:T(8,128)(2,1)S(1)}, u32[]{:S(2)}, u32[]{:S(2)}) async-start(bf16[32,16,1024]{2,1,0:T(8,128)(2,1)} %collective-permute-done.4), calls=%async_computation.4 | async-start | bytes 2097152 | tf_op jit(solution)/shard_map/all_to_all | solution.py:260
  121.7 9.4 %collective-permute-done = bf16[32,16,1024]{2,1,0:T(8,128)(2,1)} collective-permute-done((bf16[32,16,1024]{2,1,0:T(8,128)(2,1)}, bf16[32,16,1024]{2,1,0:T(8,128)(2,1)}, u32[]{:S(2)}, u32[]{:S(2)}) %collective-permute-start) | collective-permute-done | bytes 1048608 | tf_op jit(solution)/shard_map/ppermute | solution.py:264
  131.1 6.5 %all-to-all-done.4 = bf16[32,16,1024]{2,1,0:T(8,128)(2,1)S(1)} async-done(((bf16[32,16,1024]{2,1,0:T(8,128)(2,1)}), bf16[32,16,1024]{2,1,0:T(8,128)(2,1)S(1)}, u32[]{:S(2)}, u32[]{:S(2)}) %all-to-all-start.4) | async-done | bytes 1048608 | tf_op jit(solution)/shard_map/all_to_all | solution.py:260
  137.7 5.7 %all-to-all-start.2 = ((bf16[32,16,1024]{2,1,0:T(8,128)(2,1)}), bf16[32,16,1024]{2,1,0:T(8,128)(2,1)}, u32[]{:S(2)}, u32[]{:S(2)}) async-start(bf16[32,16,1024]{2,1,0:T(8,128)(2,1)} %collective-permute-done), calls=%async_computation.2 | async-start | bytes 2097152 | tf_op jit(solution)/shard_map/all_to_all | solution.py:260
  143.5 1.4 constant_dynamic-update-slice_fusion.3
  144.9 0.1 copy-done.5
  145.1 0.1 constant_dynamic-update-slice_fusion.2
  145.2 1.5 gather_fusion.9
  146.6 2.0 collective-permute-start.5
  148.6 1.4 gather_fusion.10
  150.0 3.8 %collective-permute-start.6 = (bf16[16,16,1024]{2,1,0:T(8,128)(2,1)}, bf16[16,16,1024]{2,1,0:T(8,128)(2,1)}, u32[]{:S(2)}, u32[]{:S(2)}) collective-permute-start(bf16[16,16,1024]{2,1,0:T(8,128)(2,1)} %gather_fusion.10), channel_id=1, source_target_pairs={{0,2},{1,3},{2,0},{3,1},{4,6},{5,7},{6,4},{7,5},{8,10},{9,11},{10,... | collective-permute-start | bytes 1572872 | tf_op jit(solution)/shard_map/ppermute | solution.py:273
  153.8 1.4 gather_fusion.11
  155.2 2.3 collective-permute-start.7
  157.5 1.3 constant_dynamic-update-slice_fusion.1
  158.8 0.7 all-to-all-done.2
  159.5 1.3 constant_dynamic-update-slice_fusion
  160.8 1.4 gather_fusion.4
  162.2 1.4 gather_fusion.5
  163.6 0.6 gather_fusion.3
  164.2 4.0 %collective-permute-start.2 = (bf16[16,16,1024]{2,1,0:T(8,128)(2,1)}, bf16[16,16,1024]{2,1,0:T(8,128)(2,1)}, u32[]{:S(2)}, u32[]{:S(2)}) collective-permute-start(bf16[16,16,1024]{2,1,0:T(8,128)(2,1)} %gather_fusion.4), channel_id=1, source_target_pairs={{0,2},{1,3},{2,0},{3,1},{4,6},{5,7},{6,4},{7,5},{8,10},{9,11},{10,... | collective-permute-start | bytes 1572872 | tf_op jit(solution)/shard_map/ppermute | solution.py:273
  168.2 0.4 collective-permute-done.5
  168.6 1.3 collective-permute-start.3
  169.9 21.3 %collective-permute-done.6 = bf16[16,16,1024]{2,1,0:T(8,128)(2,1)} collective-permute-done((bf16[16,16,1024]{2,1,0:T(8,128)(2,1)}, bf16[16,16,1024]{2,1,0:T(8,128)(2,1)}, u32[]{:S(2)}, u32[]{:S(2)}) %collective-permute-start.6) | collective-permute-done | bytes 524320 | tf_op jit(solution)/shard_map/ppermute | solution.py:273
  191.2 19.4 %collective-permute-start.1 = (bf16[16,16,1024]{2,1,0:T(8,128)(2,1)S(1)}, bf16[16,16,1024]{2,1,0:T(8,128)(2,1)}, u32[]{:S(2)}, u32[]{:S(2)}) collective-permute-start(bf16[16,16,1024]{2,1,0:T(8,128)(2,1)S(1)} %gather_fusion.3), channel_id=1, source_target_pairs={{0,1},{1,2},{2,3},{3,0},{4,5},{5,6},{6,7},{7,4},{8,9},{9,10},{10,1... | collective-permute-start | bytes 1572872 | tf_op jit(solution)/shard_map/ppermute | solution.py:273
  210.7 0.6 pad_add_fusion.where_ref
  211.3 3.0 gather_fusion.8
  214.2 1.4 gather_fusion.2
  215.6 18.9 %collective-permute-done.7 = bf16[16,16,1024]{2,1,0:T(8,128)(2,1)} collective-permute-done((bf16[16,16,1024]{2,1,0:T(8,128)(2,1)}, bf16[16,16,1024]{2,1,0:T(8,128)(2,1)}, u32[]{:S(2)}, u32[]{:S(2)}) %collective-permute-start.7) | collective-permute-done | bytes 524320 | tf_op jit(solution)/shard_map/ppermute | solution.py:273
  234.6 15.4 %prepare.1 = (bf16[512,1024]{1,0:T(8,128)(2,1)}, bf16[1024,1024]{1,0:T(8,128)(2,1)}, bf16[1024,1024]{1,0:T(8,128)(2,1)}, bf16[2,16,4,32,1024]{4,3,2,1,0:T(8,128)(2,1)}) custom-call(s32[2]{0:T(128)} %pad_add_fusion.where_ref, bf16[256,1024]{1,0:T(8,128)(2,1)} %bitcast.88, bf16[256,1024]{1,0:T(8,128)(2,1)} %bitcast.24.refs_1_, ...), custom_call_target="tpu_custom_call" | custom-call | flops 5368709120 | bytes 18874368 | tf_op jit(solution)/shard_map/prepare/pallas_call | solution.py:131
  250.0 10.2 %shard_map.73 = bf16[4,256,256]{2,1,0:T(8,128)(2,1)} custom-call(bf16[256,1024]{1,0:T(8,128)(2,1)} %bitcast.86, bf16[256,1024]{1,0:T(8,128)(2,1)} %bitcast.12.refs_1_, bf16[256,1024]{1,0:T(8,128)(2,1)} %bitcast.15.refs_2_, bf16[256,1024]{1,0:T(8,128)(2,1)} %bitcast.18.refs_3_, bf16[512,1024]{1,0:T(8,128)(2,1)} %get-tuple-element.9.refs_4_, ...), custom_call_target="tpu_custom_call" | custom-call | flops 5368709120 | bytes 9437184 | tf_op jit(solution)/shard_map/pallas_call | solution.py:179
  260.2 5.2 %all-to-all-start.5 = ((bf16[4,256,256]{2,1,0:T(8,128)(2,1)}), bf16[4,256,256]{2,1,0:T(8,128)(2,1)S(1)}, u32[]{:S(2)}, u32[]{:S(2)}) async-start(bf16[4,256,256]{2,1,0:T(8,128)(2,1)} %shard_map.73), calls=%async_computation.5 | async-start | bytes 1048576 | tf_op jit(solution)/shard_map/all_to_all | solution.py:285
  265.4 10.2 %shard_map.74 = bf16[4,256,256]{2,1,0:T(8,128)(2,1)} custom-call(bf16[256,1024]{1,0:T(8,128)(2,1)} %bitcast.87, bf16[256,1024]{1,0:T(8,128)(2,1)} %bitcast.12.refs_1_, bf16[256,1024]{1,0:T(8,128)(2,1)} %bitcast.15.refs_2_, bf16[256,1024]{1,0:T(8,128)(2,1)} %bitcast.18.refs_3_, bf16[512,1024]{1,0:T(8,128)(2,1)} %get-tuple-element.9.refs_4_, ...), custom_call_target="tpu_custom_call" | custom-call | flops 5368709120 | bytes 9437184 | tf_op jit(solution)/shard_map/pallas_call | solution.py:179
  275.6 3.9 %all-to-all-done.5 = bf16[4,256,256]{2,1,0:T(8,128)(2,1)S(1)} async-done(((bf16[4,256,256]{2,1,0:T(8,128)(2,1)}), bf16[4,256,256]{2,1,0:T(8,128)(2,1)S(1)}, u32[]{:S(2)}, u32[]{:S(2)}) %all-to-all-start.5) | async-done | bytes 524320 | tf_op jit(solution)/shard_map/all_to_all | solution.py:285
  279.5 17.1 %all_to_all.39 = bf16[4,256,256]{2,1,0:T(8,128)(2,1)S(1)} all-to-all(bf16[4,256,256]{2,1,0:T(8,128)(2,1)} %shard_map.74), channel_id=1, replica_groups=mesh['y'=4,'x'=4,'z'=2,'core'=2,'head'=4] {'head'}, dimensions={0} | all-to-all | bytes 1048576 | tf_op jit(solution)/shard_map/all_to_all | solution.py:285
  296.8 1.2 concatenate.19
  (43 shorter events, 0.8 us)
Async XLA Ops:
  6.5 1.0 copy-start
  6.5 79.6 %all-gather.3.cloned.1.call-start = ((), (), s32[]{:S(2)}) async-start(), calls=%async_computation.7 | async-start | bytes 4456448 | tf_op jit(solution)/shard_map/all_gather | solution.py:235
  9.2 11.4 %collective-permute-start.8 = (bf16[32,1024]{1,0:T(8,128)(2,1)S(1)}, bf16[32,1024]{1,0:T(8,128)(2,1)S(1)}, u32[]{:S(2)}, u32[]{:S(2)}) collective-permute-start(bf16[32,1024]{1,0:T(8,128)(2,1)S(1)} %get-tuple-element.14), channel_id=1, source_target_pairs={{0,1},{1,2},{2,3},{3,0},{4,5},{5,6},{6,7},{7,4},{8,9},{9,10},{10,1... | collective-permute-start | bytes 196616 | tf_op jit(solution)/shard_map/ppermute | solution.py:225
  12.6 9.5 %collective-permute-start.9 = (bf16[32,1024]{1,0:T(8,128)(2,1)S(1)}, bf16[32,1024]{1,0:T(8,128)(2,1)S(1)}, u32[]{:S(2)}, u32[]{:S(2)}) collective-permute-start(bf16[32,1024]{1,0:T(8,128)(2,1)S(1)} %get-tuple-element.14), channel_id=1, source_target_pairs={{0,2},{1,3},{2,0},{3,1},{4,6},{5,7},{6,4},{7,5},{8,10},{9,11},{10,... | collective-permute-start | bytes 196616 | tf_op jit(solution)/shard_map/ppermute | solution.py:225
  18.0 6.9 %collective-permute-start.10 = (bf16[32,1024]{1,0:T(8,128)(2,1)S(1)}, bf16[32,1024]{1,0:T(8,128)(2,1)S(1)}, u32[]{:S(2)}, u32[]{:S(2)}) collective-permute-start(bf16[32,1024]{1,0:T(8,128)(2,1)S(1)} %get-tuple-element.14), channel_id=1, source_target_pairs={{0,3},{1,0},{2,1},{3,2},{4,7},{5,4},{6,5},{7,6},{8,11},{9,8},{10,9... | collective-permute-start | bytes 196616 | tf_op jit(solution)/shard_map/ppermute | solution.py:225
  28.2 15.1 %all-to-all-start = ((s32[64,1,1]{2,1,0:T(1,128)}), s32[64,1,1]{2,1,0:T(1,128)S(1)}, u32[]{:S(2)}, u32[]{:S(2)}) async-start(s32[64,1,1]{2,1,0:T(1,128)} %copy.32), calls=%async_computation | async-start | bytes 65536 | tf_op jit(solution)/shard_map/all_to_all | solution.py:234
  48.6 45.7 %all-to-all-start.3 = ((bf16[32,16,1024]{2,1,0:T(8,128)(2,1)}), bf16[32,16,1024]{2,1,0:T(8,128)(2,1)S(1)}, u32[]{:S(2)}, u32[]{:S(2)}) async-start(bf16[32,16,1024]{2,1,0:T(8,128)(2,1)} %gather_fusion.6), calls=%async_computation.3 | async-start | bytes 2097152 | tf_op jit(solution)/shard_map/all_to_all | solution.py:260
  86.1 148.4 %collective-permute-start.11 = (bf16[16,4,32,1024]{3,2,1,0:T(8,128)(2,1)}, bf16[16,4,32,1024]{3,2,1,0:T(8,128)(2,1)}, u32[]{:S(2)}, u32[]{:S(2)}) collective-permute-start(bf16[16,4,32,1024]{3,2,1,0:T(8,128)(2,1)} %bitcast.95), channel_id=1, source_target_pairs={{0,4},{4,0},{1,5},{5,1},{2,6},{6,2},{3,7},{7,3},{8,12},{12,8},{9,1... | collective-permute-start | bytes 12582920 | tf_op jit(solution)/shard_map/ppermute | solution.py:278
  89.9 26.2 %collective-permute-start.4 = (bf16[32,16,1024]{2,1,0:T(8,128)(2,1)}, bf16[32,16,1024]{2,1,0:T(8,128)(2,1)}, u32[]{:S(2)}, u32[]{:S(2)}) collective-permute-start(bf16[32,16,1024]{2,1,0:T(8,128)(2,1)} %gather_fusion.7), channel_id=1, source_target_pairs={{0,8},{1,9},{2,10},{3,11},{8,0},{9,1},{10,2},{11,3},{4,12},{5,13},... | collective-permute-start | bytes 3145736 | tf_op jit(solution)/shard_map/ppermute | solution.py:264
  94.3 9.7 %copy-start.2 = (bf16[32,16,1024]{2,1,0:T(8,128)(2,1)}, bf16[32,16,1024]{2,1,0:T(8,128)(2,1)S(1)}, u32[]{:S(2)}) copy-start(bf16[32,16,1024]{2,1,0:T(8,128)(2,1)S(1)} %all-to-all-done.3) | copy-start | bytes 3145732
  94.3 21.9 %all-to-all-start.1 = ((bf16[32,16,1024]{2,1,0:T(8,128)(2,1)}), bf16[32,16,1024]{2,1,0:T(8,128)(2,1)S(1)}, u32[]{:S(2)}, u32[]{:S(2)}) async-start(bf16[32,16,1024]{2,1,0:T(8,128)(2,1)} %gather_fusion), calls=%async_computation.1 | async-start | bytes 2097152 | tf_op jit(solution)/shard_map/all_to_all | solution.py:260
  104.0 27.1 %collective-permute-start = (bf16[32,16,1024]{2,1,0:T(8,128)(2,1)}, bf16[32,16,1024]{2,1,0:T(8,128)(2,1)}, u32[]{:S(2)}, u32[]{:S(2)}) collective-permute-start(bf16[32,16,1024]{2,1,0:T(8,128)(2,1)} %gather_fusion.1), channel_id=1, source_target_pairs={{0,11},{1,8},{2,9},{3,10},{8,1},{9,2},{10,3},{11,0},{4,15},{5,12},... | collective-permute-start | bytes 3145736 | tf_op jit(solution)/shard_map/ppermute | solution.py:264
  116.2 21.5 %copy-start.3 = (bf16[32,16,1024]{2,1,0:T(8,128)(2,1)}, bf16[32,16,1024]{2,1,0:T(8,128)(2,1)S(1)}, u32[]{:S(2)}) copy-start(bf16[32,16,1024]{2,1,0:T(8,128)(2,1)S(1)} %all-to-all-done.1) | copy-start | bytes 3145732
  116.2 21.5 %all-to-all-start.4 = ((bf16[32,16,1024]{2,1,0:T(8,128)(2,1)}), bf16[32,16,1024]{2,1,0:T(8,128)(2,1)S(1)}, u32[]{:S(2)}, u32[]{:S(2)}) async-start(bf16[32,16,1024]{2,1,0:T(8,128)(2,1)} %collective-permute-done.4), calls=%async_computation.4 | async-start | bytes 2097152 | tf_op jit(solution)/shard_map/all_to_all | solution.py:260
  137.7 5.8 %copy-start.4 = (bf16[32,16,1024]{2,1,0:T(8,128)(2,1)}, bf16[32,16,1024]{2,1,0:T(8,128)(2,1)S(1)}, u32[]{:S(2)}) copy-start(bf16[32,16,1024]{2,1,0:T(8,128)(2,1)S(1)} %all-to-all-done.4) | copy-start | bytes 3145732
  137.7 21.9 %all-to-all-start.2 = ((bf16[32,16,1024]{2,1,0:T(8,128)(2,1)}), bf16[32,16,1024]{2,1,0:T(8,128)(2,1)}, u32[]{:S(2)}, u32[]{:S(2)}) async-start(bf16[32,16,1024]{2,1,0:T(8,128)(2,1)} %collective-permute-done), calls=%async_computation.2 | async-start | bytes 2097152 | tf_op jit(solution)/shard_map/all_to_all | solution.py:260
  143.5 1.5 copy-start.5
  145.2 12.3 %copy-start.1 = (bf16[64,16,1024]{2,1,0:T(8,128)(2,1)}, bf16[64,16,1024]{2,1,0:T(8,128)(2,1)S(1)}, u32[]{:S(2)}) copy-start(bf16[64,16,1024]{2,1,0:T(8,128)(2,1)S(1)} %constant_dynamic-update-slice_fusion.2) | copy-start | bytes 6291460
  146.6 22.0 %collective-permute-start.5 = (bf16[16,16,1024]{2,1,0:T(8,128)(2,1)}, bf16[16,16,1024]{2,1,0:T(8,128)(2,1)}, u32[]{:S(2)}, u32[]{:S(2)}) collective-permute-start(bf16[16,16,1024]{2,1,0:T(8,128)(2,1)} %gather_fusion.9), channel_id=1, source_target_pairs={{0,1},{1,2},{2,3},{3,0},{4,5},{5,6},{6,7},{7,4},{8,9},{9,10},{10,1... | collective-permute-start | bytes 1572872 | tf_op jit(solution)/shard_map/ppermute | solution.py:273
  150.0 41.2 %collective-permute-start.6 = (bf16[16,16,1024]{2,1,0:T(8,128)(2,1)}, bf16[16,16,1024]{2,1,0:T(8,128)(2,1)}, u32[]{:S(2)}, u32[]{:S(2)}) collective-permute-start(bf16[16,16,1024]{2,1,0:T(8,128)(2,1)} %gather_fusion.10), channel_id=1, source_target_pairs={{0,2},{1,3},{2,0},{3,1},{4,6},{5,7},{6,4},{7,5},{8,10},{9,11},{10,... | collective-permute-start | bytes 1572872 | tf_op jit(solution)/shard_map/ppermute | solution.py:273
  155.2 79.4 %collective-permute-start.7 = (bf16[16,16,1024]{2,1,0:T(8,128)(2,1)}, bf16[16,16,1024]{2,1,0:T(8,128)(2,1)}, u32[]{:S(2)}, u32[]{:S(2)}) collective-permute-start(bf16[16,16,1024]{2,1,0:T(8,128)(2,1)} %gather_fusion.11), channel_id=1, source_target_pairs={{0,3},{1,0},{2,1},{3,2},{4,7},{5,4},{6,5},{7,6},{8,11},{9,8},{10,9... | collective-permute-start | bytes 1572872 | tf_op jit(solution)/shard_map/ppermute | solution.py:273
  164.2 85.8 %collective-permute-start.2 = (bf16[16,16,1024]{2,1,0:T(8,128)(2,1)}, bf16[16,16,1024]{2,1,0:T(8,128)(2,1)}, u32[]{:S(2)}, u32[]{:S(2)}) collective-permute-start(bf16[16,16,1024]{2,1,0:T(8,128)(2,1)} %gather_fusion.4), channel_id=1, source_target_pairs={{0,2},{1,3},{2,0},{3,1},{4,6},{5,7},{6,4},{7,5},{8,10},{9,11},{10,... | collective-permute-start | bytes 1572872 | tf_op jit(solution)/shard_map/ppermute | solution.py:273
  168.6 81.4 %collective-permute-start.3 = (bf16[16,16,1024]{2,1,0:T(8,128)(2,1)}, bf16[16,16,1024]{2,1,0:T(8,128)(2,1)}, u32[]{:S(2)}, u32[]{:S(2)}) collective-permute-start(bf16[16,16,1024]{2,1,0:T(8,128)(2,1)} %gather_fusion.5), channel_id=1, source_target_pairs={{0,3},{1,0},{2,1},{3,2},{4,7},{5,4},{6,5},{7,6},{8,11},{9,8},{10,9... | collective-permute-start | bytes 1572872 | tf_op jit(solution)/shard_map/ppermute | solution.py:273
  191.2 58.8 %collective-permute-start.1 = (bf16[16,16,1024]{2,1,0:T(8,128)(2,1)S(1)}, bf16[16,16,1024]{2,1,0:T(8,128)(2,1)}, u32[]{:S(2)}, u32[]{:S(2)}) collective-permute-start(bf16[16,16,1024]{2,1,0:T(8,128)(2,1)S(1)} %gather_fusion.3), channel_id=1, source_target_pairs={{0,1},{1,2},{2,3},{3,0},{4,5},{5,6},{6,7},{7,4},{8,9},{9,10},{10,1... | collective-permute-start | bytes 1572872 | tf_op jit(solution)/shard_map/ppermute | solution.py:273
  260.2 19.3 %all-to-all-start.5 = ((bf16[4,256,256]{2,1,0:T(8,128)(2,1)}), bf16[4,256,256]{2,1,0:T(8,128)(2,1)S(1)}, u32[]{:S(2)}, u32[]{:S(2)}) async-start(bf16[4,256,256]{2,1,0:T(8,128)(2,1)} %shard_map.73), calls=%async_computation.5 | async-start | bytes 1048576 | tf_op jit(solution)/shard_map/all_to_all | solution.py:285
Sparse Core Ops, SparseCore 0:
  26.4 59.7 all-gather.2

commit v10 on v9

--- a/solution.py
+++ b/solution.py
@@ -166,7 +166,7 @@
 def attend(part, chunks, queries, keys, values, weights):
     held, width = chunks[0].shape
     here = queries.shape[0] // SPAN_LEN // PARTS
-    some = held // PARTS
+    some = held
     rows = here * SPAN_LEN
     early = keys.shape[0] // PARTS
     late = some * len(chunks)
@@ -180,7 +180,7 @@
         attend_kernel,
         out_shape=jax.ShapeDtypeStruct((groups, rows, cols), jnp.bfloat16),
         grid=(groups,),
-        in_specs=[pl.BlockSpec((some, width), lambda g: (part, 0)) for _ in chunks]
+        in_specs=[pl.BlockSpec((some, width), lambda g: (0, 0)) for _ in chunks]
         + [
             columns(rows),
             columns(early),
@@ -267,20 +267,27 @@
         same = exchange(pieces[CHUNKS * staying + c])
         other = exchange(crossed)
         arrived = jnp.concatenate([same, other], axis=0)
-        for step in range(groups):
-            block = arrived[sources[(head + step) % groups]]
-            if step:
-                block = lax.ppermute(
-                    block, "head", [(i, (i + step) % groups) for i in range(groups)]
-                )
-            owned.append(block.reshape(-1, width))
+        whole = c < CHUNKS - 1
+        for p in range(1 if whole else PARTS):
+            taken = sources if whole else jnp.split(sources, PARTS, axis=1)[p]
+            blocks = []
+            for step in range(groups):
+                block = arrived[taken[(head + step) % groups]]
+                if step:
+                    block = lax.ppermute(
+                        block, "head", [(i, (i + step) % groups) for i in range(groups)]
+                    )
+                blocks.append(block.reshape(-1, width))
+            owned.append(blocks)
     weights = weights.reshape(-1, groups, depth, width)
     other = lax.ppermute(weights, "core", [(0, 1), (1, 0)])
     where = jnp.stack([head, lax.axis_index("core")])
-    queries, keys, values, weights = prepare(where, owned[:groups], decoder_states, weights, other)
+    queries, keys, values, weights = prepare(
+        where, owned[0], decoder_states, weights, other
+    )
     returned = []
     for p in range(PARTS):
-        result = attend(p, owned[groups:], queries, keys, values, weights)
+        result = attend(p, owned[1 + p], queries, keys, values, weights)
         returned.append(
             lax.all_to_all(result, "head", split_axis=0, concat_axis=0, tiled=True)
         )

time: 306 us -> 315 us (1.029)
  the two profiles are of different devices: /device:TPU:2 before, /device:TPU:34 now
where the time goes in v10:
time: 315 us; the launch traced here: 313 us
  waiting for transfers between devices  122 us (39%)
  starting transfers between devices  70.8 us (22%)
  local copies, waits for them, and re-layouts  48.5 us (15%)
  Pallas kernels  35.7 us (11%)
  blocking collectives  20.3 us (6%)
  between operations  13.8 us (4%)
    ppermute x9, waiting for transfers between devices, layer(): lax.ppermute(block, 'head', [(i, (i + step) % groups) for i in range(grou...  53.5 us
    all_gather x1, waiting for transfers between devices, layer(): weights = lax.all_gather(stacked, ('y', 'x'), axis=0, tiled=True)  32.5 us
    ppermute x9, starting transfers between devices, layer(): lax.ppermute(block, 'head', [(i, (i + step) % groups) for i in range(grou...  22 us
    all_to_all x4, starting transfers between devices, exchange(): return lax.all_to_all(block, flat, split_axis=0, concat_axis=0, tiled=True)  21.6 us
    pallas_call x2, Pallas kernels, attend(): pl.pallas_call(attend_kernel, out_shape=jax.ShapeDtypeStruct((groups, row...  20.3 us
    all_to_all x1, blocking collectives, layer(): lax.all_to_all(result, 'head', split_axis=0, concat_axis=0, tiled=True)  20.3 us
    gather x12, local copies, waits for them, and re-layouts, layer(): block = arrived[taken[(head + step) % groups]]  20.2 us
    all_to_all x4, waiting for transfers between devices, exchange(): return lax.all_to_all(block, flat, split_axis=0, concat_axis=0, tiled=True)  18.8 us
  transfers between devices with their start and end apart: 22, of which 14 were waited for; matrix products, arithmetic and copies ran while one was open for 14% of the time, Pallas kernels for 8%

profile of v10, /device:TPU:34, one launch (start us, length us, event | category | flops | bytes accessed | tf_op | source)
XLA Modules:
  0.0 313.5 jit_solution(2141616086286239610)
XLA Ops:
  6.5 1.0 copy-done
  7.7 0.7 constant_dynamic-slice_fusion.7
  8.5 0.7 constant_dynamic-slice_fusion.5
  9.2 3.3 %collective-permute-start.8 = (bf16[32,1024]{1,0:T(8,128)(2,1)S(1)}, bf16[32,1024]{1,0:T(8,128)(2,1)S(1)}, u32[]{:S(2)}, u32[]{:S(2)}) collective-permute-start(bf16[32,1024]{1,0:T(8,128)(2,1)S(1)} %get-tuple-element.14), channel_id=1, source_target_pairs={{0,1},{1,2},{2,3},{3,0},{4,5},{5,6},{6,7},{7,4},{8,9},{9,10},{10,1... | collective-permute-start | bytes 196616 | tf_op jit(solution)/shard_map/ppermute | solution.py:225
  12.6 4.5 %collective-permute-start.9 = (bf16[32,1024]{1,0:T(8,128)(2,1)S(1)}, bf16[32,1024]{1,0:T(8,128)(2,1)S(1)}, u32[]{:S(2)}, u32[]{:S(2)}) collective-permute-start(bf16[32,1024]{1,0:T(8,128)(2,1)S(1)} %get-tuple-element.14), channel_id=1, source_target_pairs={{0,2},{1,3},{2,0},{3,1},{4,6},{5,7},{6,4},{7,5},{8,10},{9,11},{10,... | collective-permute-start | bytes 196616 | tf_op jit(solution)/shard_map/ppermute | solution.py:225
  17.1 2.7 collective-permute-start.10
  19.8 1.2 collective-permute-done.9
  21.0 1.9 collective-permute-done.10
  22.9 1.3 gather_fusion.12
  24.1 0.8 fusion.43
  25.4 0.7 copy.32
  26.1 9.7 %all-to-all-start = ((s32[64,1,1]{2,1,0:T(1,128)}), s32[64,1,1]{2,1,0:T(1,128)S(1)}, u32[]{:S(2)}, u32[]{:S(2)}) async-start(s32[64,1,1]{2,1,0:T(1,128)} %copy.32), calls=%async_computation | async-start | bytes 65536 | tf_op jit(solution)/shard_map/all_to_all | solution.py:234
  35.8 6.2 %all-to-all-done = s32[64,1,1]{2,1,0:T(1,128)S(1)} async-done(((s32[64,1,1]{2,1,0:T(1,128)}), s32[64,1,1]{2,1,0:T(1,128)S(1)}, u32[]{:S(2)}, u32[]{:S(2)}) %all-to-all-start) | async-done | bytes 288 | tf_op jit(solution)/shard_map/all_to_all | solution.py:234
  42.0 1.2 reduce
  43.5 3.8 %gather_fusion.6 = bf16[32,16,1024]{2,1,0:T(8,128)(2,1)} fusion(bf16[128,16,1024]{2,1,0:T(8,128)(2,1)} %bitcast.125, s32[1024]{0:T(1024)S(1)} %pad_clamp_fusion.10), kind=kCustom, calls=%fused_computation.6 | custom fusion | bytes 2097280 | tf_op jit(solution)/shard_map/gather | solution.py:267
  47.3 5.0 %all-to-all-start.3 = ((bf16[32,16,1024]{2,1,0:T(8,128)(2,1)}), bf16[32,16,1024]{2,1,0:T(8,128)(2,1)S(1)}, u32[]{:S(2)}, u32[]{:S(2)}) async-start(bf16[32,16,1024]{2,1,0:T(8,128)(2,1)} %gather_fusion.6), calls=%async_computation.3 | async-start | bytes 2097152 | tf_op jit(solution)/shard_map/all_to_all | solution.py:260
  52.3 32.5 %all-gather.3.cloned.1.call-done = bf16[64,32,1024]{2,1,0:T(8,128)(2,1)} async-done(((bf16[4,32,1024]{2,1,0:T(8,128)(2,1)}), bf16[64,32,1024]{2,1,0:T(8,128)(2,1)}) %all-gather.3.cloned.1.call-update) | async-done | bytes 4194320 | tf_op jit(solution)/shard_map/all_gather | solution.py:235
  84.8 3.8 %gather_fusion.7 = bf16[32,16,1024]{2,1,0:T(8,128)(2,1)} fusion(bf16[128,16,1024]{2,1,0:T(8,128)(2,1)} %bitcast.126, s32[1024]{0:T(1024)S(1)} %pad_clamp_fusion.9), kind=kCustom, calls=%fused_computation.7 | custom fusion | bytes 2097280 | tf_op jit(solution)/shard_map/gather | solution.py:265
  88.6 1.5 collective-permute-start.4
  90.1 3.8 %gather_fusion = bf16[32,16,1024]{2,1,0:T(8,128)(2,1)} fusion(bf16[128,16,1024]{2,1,0:T(8,128)(2,1)} %bitcast.127, s32[1024]{0:T(1024)S(1)} %pad_clamp_fusion.16), kind=kCustom, calls=%fused_computation | custom fusion | bytes 2097280 | tf_op jit(solution)/shard_map/gather | solution.py:267
  93.8 5.9 %all-to-all-start.1 = ((bf16[32,16,1024]{2,1,0:T(8,128)(2,1)}), bf16[32,16,1024]{2,1,0:T(8,128)(2,1)S(1)}, u32[]{:S(2)}, u32[]{:S(2)}) async-start(bf16[32,16,1024]{2,1,0:T(8,128)(2,1)} %gather_fusion), calls=%async_computation.1 | async-start | bytes 2097152 | tf_op jit(solution)/shard_map/all_to_all | solution.py:260
  99.8 3.8 %gather_fusion.1 = bf16[32,16,1024]{2,1,0:T(8,128)(2,1)} fusion(bf16[128,16,1024]{2,1,0:T(8,128)(2,1)} %bitcast.128, s32[1024]{0:T(1024)S(1)} %pad_clamp_fusion.15), kind=kCustom, calls=%fused_computation.1 | custom fusion | bytes 2097280 | tf_op jit(solution)/shard_map/gather | solution.py:265
  103.6 1.1 collective-permute-start
  104.7 11.0 %all-to-all-done.1 = bf16[32,16,1024]{2,1,0:T(8,128)(2,1)S(1)} async-done(((bf16[32,16,1024]{2,1,0:T(8,128)(2,1)}), bf16[32,16,1024]{2,1,0:T(8,128)(2,1)S(1)}, u32[]{:S(2)}, u32[]{:S(2)}) %all-to-all-start.1) | async-done | bytes 1048608 | tf_op jit(solution)/shard_map/all_to_all | solution.py:260
  115.7 5.0 %all-to-all-start.4 = ((bf16[32,16,1024]{2,1,0:T(8,128)(2,1)}), bf16[32,16,1024]{2,1,0:T(8,128)(2,1)S(1)}, u32[]{:S(2)}, u32[]{:S(2)}) async-start(bf16[32,16,1024]{2,1,0:T(8,128)(2,1)} %collective-permute-done.4), calls=%async_computation.4 | async-start | bytes 2097152 | tf_op jit(solution)/shard_map/all_to_all | solution.py:260
  121.0 8.1 %collective-permute-done = bf16[32,16,1024]{2,1,0:T(8,128)(2,1)} collective-permute-done((bf16[32,16,1024]{2,1,0:T(8,128)(2,1)}, bf16[32,16,1024]{2,1,0:T(8,128)(2,1)}, u32[]{:S(2)}, u32[]{:S(2)}) %collective-permute-start) | collective-permute-done | bytes 1048608 | tf_op jit(solution)/shard_map/ppermute | solution.py:264
  129.1 7.8 %all-to-all-done.4 = bf16[32,16,1024]{2,1,0:T(8,128)(2,1)S(1)} async-done(((bf16[32,16,1024]{2,1,0:T(8,128)(2,1)}), bf16[32,16,1024]{2,1,0:T(8,128)(2,1)S(1)}, u32[]{:S(2)}, u32[]{:S(2)}) %all-to-all-start.4) | async-done | bytes 1048608 | tf_op jit(solution)/shard_map/all_to_all | solution.py:260
  136.9 5.7 %all-to-all-start.2 = ((bf16[32,16,1024]{2,1,0:T(8,128)(2,1)}), bf16[32,16,1024]{2,1,0:T(8,128)(2,1)}, u32[]{:S(2)}, u32[]{:S(2)}) async-start(bf16[32,16,1024]{2,1,0:T(8,128)(2,1)} %collective-permute-done), calls=%async_computation.2 | async-start | bytes 2097152 | tf_op jit(solution)/shard_map/all_to_all | solution.py:260
  142.6 1.4 constant_dynamic-update-slice_fusion.3
  144.3 1.5 gather_fusion.9
  145.8 2.0 collective-permute-start.5
  147.7 1.4 gather_fusion.10
  149.2 3.8 %collective-permute-start.6 = (bf16[16,16,1024]{2,1,0:T(8,128)(2,1)}, bf16[16,16,1024]{2,1,0:T(8,128)(2,1)}, u32[]{:S(2)}, u32[]{:S(2)}) collective-permute-start(bf16[16,16,1024]{2,1,0:T(8,128)(2,1)} %gather_fusion.10), channel_id=1, source_target_pairs={{0,2},{1,3},{2,0},{3,1},{4,6},{5,7},{6,4},{7,5},{8,10},{9,11},{10,... | collective-permute-start | bytes 1572872 | tf_op jit(solution)/shard_map/ppermute | solution.py:277
  153.5 2.4 collective-permute-start.7
  155.9 0.7 pad_add_fusion.where_ref
  156.6 1.3 constant_dynamic-update-slice_fusion.1
  157.9 3.0 gather_fusion.8
  160.9 1.3 constant_dynamic-update-slice_fusion
  162.8 0.8 collective-permute-start.1
  163.6 1.3 gather_fusion.4
  164.9 1.3 gather_fusion.5
  166.2 1.3 gather_fusion.2
  167.5 28.8 %collective-permute-done.5 = bf16[16,16,1024]{2,1,0:T(8,128)(2,1)} collective-permute-done((bf16[16,16,1024]{2,1,0:T(8,128)(2,1)}, bf16[16,16,1024]{2,1,0:T(8,128)(2,1)}, u32[]{:S(2)}, u32[]{:S(2)}) %collective-permute-start.5) | collective-permute-done | bytes 524320 | tf_op jit(solution)/shard_map/ppermute | solution.py:277
  196.3 3.9 %collective-permute-start.2 = (bf16[8,16,1024]{2,1,0:T(8,128)(2,1)}, bf16[8,16,1024]{2,1,0:T(8,128)(2,1)S(1)}, u32[]{:S(2)}, u32[]{:S(2)}) collective-permute-start(bf16[8,16,1024]{2,1,0:T(8,128)(2,1)} %gather_fusion.4), channel_id=1, source_target_pairs={{0,2},{1,3},{2,0},{3,1},{4,6},{5,7},{6,4},{7,5},{8,10},{9,11},{10,... | collective-permute-start | bytes 786440 | tf_op jit(solution)/shard_map/ppermute | solution.py:277
  200.2 15.4 %prepare.1 = (bf16[512,1024]{1,0:T(8,128)(2,1)}, bf16[1024,1024]{1,0:T(8,128)(2,1)}, bf16[1024,1024]{1,0:T(8,128)(2,1)}, bf16[2,16,4,32,1024]{4,3,2,1,0:T(8,128)(2,1)}) custom-call(s32[2]{0:T(128)} %pad_add_fusion.where_ref, bf16[256,1024]{1,0:T(8,128)(2,1)} %bitcast.130, bf16[256,1024]{1,0:T(8,128)(2,1)} %bitcast.28.refs_1_, ...), custom_call_target="tpu_custom_call" | custom-call | flops 5368709120 | bytes 18874368 | tf_op jit(solution)/shard_map/prepare/pallas_call | solution.py:131
  215.8 3.9 %collective-permute-done.2 = bf16[8,16,1024]{2,1,0:T(8,128)(2,1)S(1)} collective-permute-done((bf16[8,16,1024]{2,1,0:T(8,128)(2,1)}, bf16[8,16,1024]{2,1,0:T(8,128)(2,1)S(1)}, u32[]{:S(2)}, u32[]{:S(2)}) %collective-permute-start.2) | collective-permute-done | bytes 262176 | tf_op jit(solution)/shard_map/ppermute | solution.py:277
  219.8 3.4 %collective-permute-done.3 = bf16[8,16,1024]{2,1,0:T(8,128)(2,1)S(1)} collective-permute-done((bf16[8,16,1024]{2,1,0:T(8,128)(2,1)}, bf16[8,16,1024]{2,1,0:T(8,128)(2,1)S(1)}, u32[]{:S(2)}, u32[]{:S(2)}) %collective-permute-start.3) | collective-permute-done | bytes 262176 | tf_op jit(solution)/shard_map/ppermute | solution.py:277
  223.2 0.7 copy-done.8
  223.9 10.2 %shard_map.73 = bf16[4,256,256]{2,1,0:T(8,128)(2,1)} custom-call(bf16[128,1024]{1,0:T(8,128)(2,1)} %bitcast.131, bf16[128,1024]{1,0:T(8,128)(2,1)} %bitcast.12.refs_1_, bf16[128,1024]{1,0:T(8,128)(2,1)} %bitcast.141, bf16[128,1024]{1,0:T(8,128)(2,1)} %bitcast.142, bf16[512,1024]{1,0:T(8,128)(2,1)} %get-tuple-element.9.refs_4_, ...), custom_call_target="tpu_custom_call" | custom-call | flops 5368709120 | bytes 9437184 | tf_op jit(solution)/shard_map/pallas_call | solution.py:179
  234.0 4.5 %all-to-all-start.5 = ((bf16[4,256,256]{2,1,0:T(8,128)(2,1)}), bf16[4,256,256]{2,1,0:T(8,128)(2,1)S(1)}, u32[]{:S(2)}, u32[]{:S(2)}) async-start(bf16[4,256,256]{2,1,0:T(8,128)(2,1)} %shard_map.73), calls=%async_computation.5 | async-start | bytes 1048576 | tf_op jit(solution)/shard_map/all_to_all | solution.py:292
  238.5 2.2 gather_fusion.16
  240.7 4.2 %collective-permute-start.14 = (bf16[8,16,1024]{2,1,0:T(8,128)(2,1)S(1)}, bf16[8,16,1024]{2,1,0:T(8,128)(2,1)S(1)}, u32[]{:S(2)}, u32[]{:S(2)}) collective-permute-start(bf16[8,16,1024]{2,1,0:T(8,128)(2,1)S(1)} %gather_fusion.16), channel_id=1, source_target_pairs={{0,3},{1,0},{2,1},{3,2},{4,7},{5,4},{6,5},{7,6},{8,11},{9,8},{10,9... | collective-permute-start | bytes 786440 | tf_op jit(solution)/shard_map/ppermute | solution.py:277
  244.9 2.2 gather_fusion.15
  247.1 2.4 collective-permute-start.13
  249.5 2.2 gather_fusion.14
  251.7 2.4 collective-permute-start.12
  254.1 2.9 gather_fusion.13
  257.0 5.6 %collective-permute-done.14 = bf16[8,16,1024]{2,1,0:T(8,128)(2,1)S(1)} collective-permute-done((bf16[8,16,1024]{2,1,0:T(8,128)(2,1)S(1)}, bf16[8,16,1024]{2,1,0:T(8,128)(2,1)S(1)}, u32[]{:S(2)}, u32[]{:S(2)}) %collective-permute-start.14) | collective-permute-done | bytes 262176 | tf_op jit(solution)/shard_map/ppermute | solution.py:277
  262.6 9.2 %collective-permute-done.13 = bf16[8,16,1024]{2,1,0:T(8,128)(2,1)S(1)} collective-permute-done((bf16[8,16,1024]{2,1,0:T(8,128)(2,1)S(1)}, bf16[8,16,1024]{2,1,0:T(8,128)(2,1)S(1)}, u32[]{:S(2)}, u32[]{:S(2)}) %collective-permute-start.13) | collective-permute-done | bytes 262176 | tf_op jit(solution)/shard_map/ppermute | solution.py:277
  271.8 2.3 collective-permute-done.12
  274.1 0.7 copy-done.11
  274.8 10.1 %shard_map.74 = bf16[4,256,256]{2,1,0:T(8,128)(2,1)} custom-call(bf16[128,1024]{1,0:T(8,128)(2,1)} %bitcast.132, bf16[128,1024]{1,0:T(8,128)(2,1)} %bitcast.145, bf16[128,1024]{1,0:T(8,128)(2,1)} %bitcast.144, bf16[128,1024]{1,0:T(8,128)(2,1)} %bitcast.143, bf16[512,1024]{1,0:T(8,128)(2,1)} %get-tuple-element.9.refs_4_, ...), custom_call_target="tpu_custom_call" | custom-call | flops 5368709120 | bytes 9437184 | tf_op jit(solution)/shard_map/pallas_call | solution.py:179
  285.0 20.3 %all_to_all.39 = bf16[4,256,256]{2,1,0:T(8,128)(2,1)S(1)} all-to-all(bf16[4,256,256]{2,1,0:T(8,128)(2,1)} %shard_map.74), channel_id=1, replica_groups=mesh['y'=4,'x'=4,'z'=2,'core'=2,'head'=4] {'head'}, dimensions={0} | all-to-all | bytes 1048576 | tf_op jit(solution)/shard_map/all_to_all | solution.py:292
  305.4 1.2 concatenate.19
  (75 shorter events, 3.0 us)
Async XLA Ops:
  6.5 1.0 copy-start
  6.5 78.3 %all-gather.3.cloned.1.call-start = ((), (), s32[]{:S(2)}) async-start(), calls=%async_computation.7 | async-start | bytes 4456448 | tf_op jit(solution)/shard_map/all_gather | solution.py:235
  9.2 10.5 %collective-permute-start.8 = (bf16[32,1024]{1,0:T(8,128)(2,1)S(1)}, bf16[32,1024]{1,0:T(8,128)(2,1)S(1)}, u32[]{:S(2)}, u32[]{:S(2)}) collective-permute-start(bf16[32,1024]{1,0:T(8,128)(2,1)S(1)} %get-tuple-element.14), channel_id=1, source_target_pairs={{0,1},{1,2},{2,3},{3,0},{4,5},{5,6},{6,7},{7,4},{8,9},{9,10},{10,1... | collective-permute-start | bytes 196616 | tf_op jit(solution)/shard_map/ppermute | solution.py:225
  12.6 8.4 %collective-permute-start.9 = (bf16[32,1024]{1,0:T(8,128)(2,1)S(1)}, bf16[32,1024]{1,0:T(8,128)(2,1)S(1)}, u32[]{:S(2)}, u32[]{:S(2)}) collective-permute-start(bf16[32,1024]{1,0:T(8,128)(2,1)S(1)} %get-tuple-element.14), channel_id=1, source_target_pairs={{0,2},{1,3},{2,0},{3,1},{4,6},{5,7},{6,4},{7,5},{8,10},{9,11},{10,... | collective-permute-start | bytes 196616 | tf_op jit(solution)/shard_map/ppermute | solution.py:225
  17.1 5.7 %collective-permute-start.10 = (bf16[32,1024]{1,0:T(8,128)(2,1)S(1)}, bf16[32,1024]{1,0:T(8,128)(2,1)S(1)}, u32[]{:S(2)}, u32[]{:S(2)}) collective-permute-start(bf16[32,1024]{1,0:T(8,128)(2,1)S(1)} %get-tuple-element.14), channel_id=1, source_target_pairs={{0,3},{1,0},{2,1},{3,2},{4,7},{5,4},{6,5},{7,6},{8,11},{9,8},{10,9... | collective-permute-start | bytes 196616 | tf_op jit(solution)/shard_map/ppermute | solution.py:225
  26.1 15.8 %all-to-all-start = ((s32[64,1,1]{2,1,0:T(1,128)}), s32[64,1,1]{2,1,0:T(1,128)S(1)}, u32[]{:S(2)}, u32[]{:S(2)}) async-start(s32[64,1,1]{2,1,0:T(1,128)} %copy.32), calls=%async_computation | async-start | bytes 65536 | tf_op jit(solution)/shard_map/all_to_all | solution.py:234
  47.3 46.5 %all-to-all-start.3 = ((bf16[32,16,1024]{2,1,0:T(8,128)(2,1)}), bf16[32,16,1024]{2,1,0:T(8,128)(2,1)S(1)}, u32[]{:S(2)}, u32[]{:S(2)}) async-start(bf16[32,16,1024]{2,1,0:T(8,128)(2,1)} %gather_fusion.6), calls=%async_computation.3 | async-start | bytes 2097152 | tf_op jit(solution)/shard_map/all_to_all | solution.py:260
  84.8 115.4 %collective-permute-start.11 = (bf16[16,4,32,1024]{3,2,1,0:T(8,128)(2,1)}, bf16[16,4,32,1024]{3,2,1,0:T(8,128)(2,1)}, u32[]{:S(2)}, u32[]{:S(2)}) collective-permute-start(bf16[16,4,32,1024]{3,2,1,0:T(8,128)(2,1)} %bitcast.139), channel_id=1, source_target_pairs={{0,4},{4,0},{1,5},{5,1},{2,6},{6,2},{3,7},{7,3},{8,12},{12,8},{9,1... | collective-permute-start | bytes 12582920 | tf_op jit(solution)/shard_map/ppermute | solution.py:283
  88.6 27.1 %collective-permute-start.4 = (bf16[32,16,1024]{2,1,0:T(8,128)(2,1)}, bf16[32,16,1024]{2,1,0:T(8,128)(2,1)}, u32[]{:S(2)}, u32[]{:S(2)}) collective-permute-start(bf16[32,16,1024]{2,1,0:T(8,128)(2,1)} %gather_fusion.7), channel_id=1, source_target_pairs={{0,8},{1,9},{2,10},{3,11},{8,0},{9,1},{10,2},{11,3},{4,12},{5,13},... | collective-permute-start | bytes 3145736 | tf_op jit(solution)/shard_map/ppermute | solution.py:264
  93.8 9.8 %copy-start.3 = (bf16[32,16,1024]{2,1,0:T(8,128)(2,1)}, bf16[32,16,1024]{2,1,0:T(8,128)(2,1)S(1)}, u32[]{:S(2)}) copy-start(bf16[32,16,1024]{2,1,0:T(8,128)(2,1)S(1)} %all-to-all-done.3) | copy-start | bytes 3145732
  93.8 21.9 %all-to-all-start.1 = ((bf16[32,16,1024]{2,1,0:T(8,128)(2,1)}), bf16[32,16,1024]{2,1,0:T(8,128)(2,1)S(1)}, u32[]{:S(2)}, u32[]{:S(2)}) async-start(bf16[32,16,1024]{2,1,0:T(8,128)(2,1)} %gather_fusion), calls=%async_computation.1 | async-start | bytes 2097152 | tf_op jit(solution)/shard_map/all_to_all | solution.py:260
  103.6 25.5 %collective-permute-start = (bf16[32,16,1024]{2,1,0:T(8,128)(2,1)}, bf16[32,16,1024]{2,1,0:T(8,128)(2,1)}, u32[]{:S(2)}, u32[]{:S(2)}) collective-permute-start(bf16[32,16,1024]{2,1,0:T(8,128)(2,1)} %gather_fusion.1), channel_id=1, source_target_pairs={{0,11},{1,8},{2,9},{3,10},{8,1},{9,2},{10,3},{11,0},{4,15},{5,12},... | collective-permute-start | bytes 3145736 | tf_op jit(solution)/shard_map/ppermute | solution.py:264
  115.7 21.2 %copy-start.4 = (bf16[32,16,1024]{2,1,0:T(8,128)(2,1)}, bf16[32,16,1024]{2,1,0:T(8,128)(2,1)S(1)}, u32[]{:S(2)}) copy-start(bf16[32,16,1024]{2,1,0:T(8,128)(2,1)S(1)} %all-to-all-done.1) | copy-start | bytes 3145732
  115.7 21.1 %all-to-all-start.4 = ((bf16[32,16,1024]{2,1,0:T(8,128)(2,1)}), bf16[32,16,1024]{2,1,0:T(8,128)(2,1)S(1)}, u32[]{:S(2)}, u32[]{:S(2)}) async-start(bf16[32,16,1024]{2,1,0:T(8,128)(2,1)} %collective-permute-done.4), calls=%async_computation.4 | async-start | bytes 2097152 | tf_op jit(solution)/shard_map/all_to_all | solution.py:260
  136.9 5.7 %copy-start.5 = (bf16[32,16,1024]{2,1,0:T(8,128)(2,1)}, bf16[32,16,1024]{2,1,0:T(8,128)(2,1)S(1)}, u32[]{:S(2)}) copy-start(bf16[32,16,1024]{2,1,0:T(8,128)(2,1)S(1)} %all-to-all-done.4) | copy-start | bytes 3145732
  136.9 24.1 %all-to-all-start.2 = ((bf16[32,16,1024]{2,1,0:T(8,128)(2,1)}), bf16[32,16,1024]{2,1,0:T(8,128)(2,1)}, u32[]{:S(2)}, u32[]{:S(2)}) async-start(bf16[32,16,1024]{2,1,0:T(8,128)(2,1)} %collective-permute-done), calls=%async_computation.2 | async-start | bytes 2097152 | tf_op jit(solution)/shard_map/all_to_all | solution.py:260
  142.6 1.5 copy-start.6
  144.3 12.3 %copy-start.2 = (bf16[64,16,1024]{2,1,0:T(8,128)(2,1)}, bf16[64,16,1024]{2,1,0:T(8,128)(2,1)S(1)}, u32[]{:S(2)}) copy-start(bf16[64,16,1024]{2,1,0:T(8,128)(2,1)S(1)} %constant_dynamic-update-slice_fusion.2) | copy-start | bytes 6291460
  145.8 50.5 %collective-permute-start.5 = (bf16[16,16,1024]{2,1,0:T(8,128)(2,1)}, bf16[16,16,1024]{2,1,0:T(8,128)(2,1)}, u32[]{:S(2)}, u32[]{:S(2)}) collective-permute-start(bf16[16,16,1024]{2,1,0:T(8,128)(2,1)} %gather_fusion.9), channel_id=1, source_target_pairs={{0,1},{1,2},{2,3},{3,0},{4,5},{5,6},{6,7},{7,4},{8,9},{9,10},{10,1... | collective-permute-start | bytes 1572872 | tf_op jit(solution)/shard_map/ppermute | solution.py:277
  149.2 51.0 %collective-permute-start.6 = (bf16[16,16,1024]{2,1,0:T(8,128)(2,1)}, bf16[16,16,1024]{2,1,0:T(8,128)(2,1)}, u32[]{:S(2)}, u32[]{:S(2)}) collective-permute-start(bf16[16,16,1024]{2,1,0:T(8,128)(2,1)} %gather_fusion.10), channel_id=1, source_target_pairs={{0,2},{1,3},{2,0},{3,1},{4,6},{5,7},{6,4},{7,5},{8,10},{9,11},{10,... | collective-permute-start | bytes 1572872 | tf_op jit(solution)/shard_map/ppermute | solution.py:277
  153.5 46.7 %collective-permute-start.7 = (bf16[16,16,1024]{2,1,0:T(8,128)(2,1)S(1)}, bf16[16,16,1024]{2,1,0:T(8,128)(2,1)}, u32[]{:S(2)}, u32[]{:S(2)}) collective-permute-start(bf16[16,16,1024]{2,1,0:T(8,128)(2,1)S(1)} %gather_fusion.11), channel_id=1, source_target_pairs={{0,3},{1,0},{2,1},{3,2},{4,7},{5,4},{6,5},{7,6},{8,11},{9,8},{10,9... | collective-permute-start | bytes 1572872 | tf_op jit(solution)/shard_map/ppermute | solution.py:277
  162.2 4.0 %copy-start.1 = (bf16[64,16,1024]{2,1,0:T(8,128)(2,1)}, bf16[64,16,1024]{2,1,0:T(8,128)(2,1)S(1)}, u32[]{:S(2)}) copy-start(bf16[64,16,1024]{2,1,0:T(8,128)(2,1)S(1)} %constant_dynamic-update-slice_fusion) | copy-start | bytes 6291460
  162.8 53.0 %collective-permute-start.1 = (bf16[8,16,1024]{2,1,0:T(8,128)(2,1)S(1)}, bf16[8,16,1024]{2,1,0:T(8,128)(2,1)}, u32[]{:S(2)}, u32[]{:S(2)}) collective-permute-start(bf16[8,16,1024]{2,1,0:T(8,128)(2,1)S(1)} %gather_fusion.3), channel_id=1, source_target_pairs={{0,1},{1,2},{2,3},{3,0},{4,5},{5,6},{6,7},{7,4},{8,9},{9,10},{10,1... | collective-permute-start | bytes 786440 | tf_op jit(solution)/shard_map/ppermute | solution.py:277
  196.3 23.5 %collective-permute-start.2 = (bf16[8,16,1024]{2,1,0:T(8,128)(2,1)}, bf16[8,16,1024]{2,1,0:T(8,128)(2,1)S(1)}, u32[]{:S(2)}, u32[]{:S(2)}) collective-permute-start(bf16[8,16,1024]{2,1,0:T(8,128)(2,1)} %gather_fusion.4), channel_id=1, source_target_pairs={{0,2},{1,3},{2,0},{3,1},{4,6},{5,7},{6,4},{7,5},{8,10},{9,11},{10,... | collective-permute-start | bytes 786440 | tf_op jit(solution)/shard_map/ppermute | solution.py:277
  200.2 23.0 %collective-permute-start.3 = (bf16[8,16,1024]{2,1,0:T(8,128)(2,1)}, bf16[8,16,1024]{2,1,0:T(8,128)(2,1)S(1)}, u32[]{:S(2)}, u32[]{:S(2)}) collective-permute-start(bf16[8,16,1024]{2,1,0:T(8,128)(2,1)} %gather_fusion.5), channel_id=1, source_target_pairs={{0,3},{1,0},{2,1},{3,2},{4,7},{5,4},{6,5},{7,6},{8,11},{9,8},{10,9... | collective-permute-start | bytes 786440 | tf_op jit(solution)/shard_map/ppermute | solution.py:277
  219.8 3.4 %copy-start.7 = (bf16[8,16,1024]{2,1,0:T(8,128)(2,1)}, bf16[8,16,1024]{2,1,0:T(8,128)(2,1)S(1)}, u32[]{:S(2)}) copy-start(bf16[8,16,1024]{2,1,0:T(8,128)(2,1)S(1)} %collective-permute-done.2) | copy-start | bytes 786436
  223.2 0.7 copy-start.8
  234.0 50.9 %all-to-all-start.5 = ((bf16[4,256,256]{2,1,0:T(8,128)(2,1)}), bf16[4,256,256]{2,1,0:T(8,128)(2,1)S(1)}, u32[]{:S(2)}, u32[]{:S(2)}) async-start(bf16[4,256,256]{2,1,0:T(8,128)(2,1)} %shard_map.73), calls=%async_computation.5 | async-start | bytes 1048576 | tf_op jit(solution)/shard_map/all_to_all | solution.py:292
  240.7 21.9 %collective-permute-start.14 = (bf16[8,16,1024]{2,1,0:T(8,128)(2,1)S(1)}, bf16[8,16,1024]{2,1,0:T(8,128)(2,1)S(1)}, u32[]{:S(2)}, u32[]{:S(2)}) collective-permute-start(bf16[8,16,1024]{2,1,0:T(8,128)(2,1)S(1)} %gather_fusion.16), channel_id=1, source_target_pairs={{0,3},{1,0},{2,1},{3,2},{4,7},{5,4},{6,5},{7,6},{8,11},{9,8},{10,9... | collective-permute-start | bytes 786440 | tf_op jit(solution)/shard_map/ppermute | solution.py:277
  247.1 24.8 %collective-permute-start.13 = (bf16[8,16,1024]{2,1,0:T(8,128)(2,1)S(1)}, bf16[8,16,1024]{2,1,0:T(8,128)(2,1)S(1)}, u32[]{:S(2)}, u32[]{:S(2)}) collective-permute-start(bf16[8,16,1024]{2,1,0:T(8,128)(2,1)S(1)} %gather_fusion.15), channel_id=1, source_target_pairs={{0,2},{1,3},{2,0},{3,1},{4,6},{5,7},{6,4},{7,5},{8,10},{9,11},{10,... | collective-permute-start | bytes 786440 | tf_op jit(solution)/shard_map/ppermute | solution.py:277
  251.7 22.4 %collective-permute-start.12 = (bf16[8,16,1024]{2,1,0:T(8,128)(2,1)S(1)}, bf16[8,16,1024]{2,1,0:T(8,128)(2,1)S(1)}, u32[]{:S(2)}, u32[]{:S(2)}) collective-permute-start(bf16[8,16,1024]{2,1,0:T(8,128)(2,1)S(1)} %gather_fusion.14), channel_id=1, source_target_pairs={{0,1},{1,2},{2,3},{3,0},{4,5},{5,6},{6,7},{7,4},{8,9},{9,10},{10,1... | collective-permute-start | bytes 786440 | tf_op jit(solution)/shard_map/ppermute | solution.py:277
  262.6 11.5 %copy-start.9 = (bf16[8,16,1024]{2,1,0:T(8,128)(2,1)}, bf16[8,16,1024]{2,1,0:T(8,128)(2,1)S(1)}, u32[]{:S(2)}) copy-start(bf16[8,16,1024]{2,1,0:T(8,128)(2,1)S(1)} %collective-permute-done.14) | copy-start | bytes 786436
  271.8 2.3 copy-start.10
  274.1 0.7 copy-start.11
Sparse Core Ops, SparseCore 0:
  24.3 60.4 all-gather.2
